TPU v7x, 512 devices: a 8x2x16 block of a 8x8x16 slice. The times are simulated.
512 devices in a mesh: job: 2 (over y), row: 16 (over z), col: 8 (over x), samp: 2 (over core).
Axes of the slice: x: 8, y: 2, z: 16, core: 2. Of those that a mesh axis runs over, the one named last changes fastest.
The devices are a block of a 8x8x16 slice.
Arguments:
- pair_repr: bfloat16 [1024, 512, 128], P(('job', 'row'), ('col', 'samp')), parts along dimension 0, may hold values from -100 to 100
- asym_id: int32 [1024], P('job'), parts along dimension 0, may hold values from 0 to 7, never falling along the last dimension, each value on 1 to 128 neighbouring positions
- valid_len: int32 [2], P('job'), parts along dimension 0, may hold values from 256 to 512
- rel_embed: bfloat16 [128, 128], replicated, may hold values from -12 to 12
- pair_gain: float32 [128], replicated, may hold values from 0.25 to 1.75
- bias_weight: bfloat16 [128, 16], replicated, may hold values from -64 to 64
- tokens: bfloat16 [128, 512, 768], P(('job', 'col', 'samp'), 'row'), parts along dimension 0, may hold values from -6 to 6
- token_gain: float32 [1, 768], replicated, may hold values from 0.25 to 1.75
- qkv_weight: bfloat16 [1, 3, 768, 768], P(None, None, None, 'row'), may hold values from -0.21875 to 0.21875
- out_weight: bfloat16 [1, 768, 768], P(None, 'row'), may hold values from -0.21875 to 0.21875
Outputs:
- refined: bfloat16 [128, 512, 768], P(('job', 'col', 'samp'), 'row'), parts along dimension 0
There are 2 independent parts, one for each index of `job`. A program takes and returns all parts, laid end to end along the dimension named above; an argument that names none is the same for every part. Nothing has to cross between parts.
Inputs may be any that keep to these rules, and one draw needn't show every extreme that they name: `asym_id`: chain indices never fall along the tokens.
All inputs are finite; a program needn't handle non-finite values.
Results may differ from a plain program's by a relative error of at most 0.002.
The roundings to bfloat16 on the way count: a program that leaves them out, or rounds other values in their place, can miss the bound.
Values may be sent and summed in bfloat16 or wider, within the bound.
No kernel may reach another device: no remote copies, remote signals or barrier semaphores. Data moves between devices by JAX's collectives and lax.ppermute only.
A program may use at most 64 MiB of HBM per device.

v0:
```python
import math

import jax
import jax.numpy as jnp
from jax import lax
from jax.sharding import PartitionSpec as P

HEAD_DIM = 48


epsilon = 1e-05


def joined_along(tiles, dim):
    dims = list(tiles.shape[1:])
    dims[dim] *= tiles.shape[0]
    return jnp.moveaxis(tiles, 0, dim).reshape(dims)


def from_everyone(shard, axis):
    copies = jnp.broadcast_to(shard, (lax.axis_size(axis), *shard.shape))
    return lax.all_to_all(copies, axis, split_axis=0, concat_axis=0, tiled=True)


def gathered_copies(shard, axis, dim):
    return joined_along(from_everyone(shard, axis), dim)


def normalize(values, gain_vector):
    average = jnp.mean(values, axis=-1, keepdims=True)
    centered = values - average
    variance = jnp.mean(centered * centered, axis=-1, keepdims=True)
    return centered * lax.rsqrt(variance + epsilon) * gain_vector


def bias_tile_of(pair_repr, asym_id, rel_embed, pair_gain, bias_weight):
    tile_rows, tile_cols, channels = pair_repr.shape
    bin_count = rel_embed.shape[0]
    reach_max = bin_count // 2 - 1
    first_row = lax.axis_index("row") * tile_rows
    first_col = lax.axis_index(("col", "samp")) * tile_cols
    row_ids = first_row + jnp.arange(tile_rows, dtype=jnp.int32)
    col_ids = first_col + jnp.arange(tile_cols, dtype=jnp.int32)
    row_chain = lax.dynamic_slice_in_dim(asym_id, first_row, tile_rows, 0)
    col_chain = lax.dynamic_slice_in_dim(asym_id, first_col, tile_cols, 0)
    offset = jnp.clip(row_ids[:, None] - col_ids[None, :], -reach_max, reach_max) + reach_max
    bin_ids = jnp.where(row_chain[:, None] == col_chain[None, :], offset, bin_count - 1)
    onehot = (
        bin_ids.reshape(-1)[:, None] == jnp.arange(bin_count, dtype=jnp.int32)[None, :]
    ).astype(jnp.bfloat16)
    summed = pair_repr.reshape(-1, channels).astype(jnp.float32) + jnp.dot(
        onehot, rel_embed, preferred_element_type=jnp.float32
    )
    normed = normalize(summed, pair_gain).astype(jnp.bfloat16)
    projected = lax.dot_general(
        bias_weight, normed, (((0,), (1,)), ((), ())), preferred_element_type=jnp.float32
    )
    return projected.reshape(bias_weight.shape[1], tile_rows, tile_cols)


def attend(queries, key_rows, value_rows, pair_bias, keymask, score_scale):
    head_count, query_count, key_count = pair_bias.shape
    model_width = queries.shape[-1]
    head_width = model_width // head_count
    query_h = queries.reshape(query_count, head_count, head_width)
    key_h = key_rows.reshape(key_count, head_count, head_width)
    value_h = value_rows.reshape(key_count, head_count, head_width)
    scores = (
        jnp.einsum("ihd,jhd->hij", query_h, key_h, preferred_element_type=jnp.float32) * score_scale
        + pair_bias
    )
    scores = jnp.where(keymask[None, None, :], scores, -1e30)
    row_max = jnp.max(scores, axis=-1, keepdims=True)
    weights = jnp.where(keymask[None, None, :], jnp.exp(scores - row_max), 0.0)
    row_total = jnp.sum(weights, axis=-1, keepdims=True)
    probs = (weights / row_total).astype(jnp.bfloat16)
    attended = jnp.einsum("hij,jhd->ihd", probs, value_h, preferred_element_type=jnp.float32)
    return attended.reshape(query_count, model_width).astype(jnp.bfloat16)


def per_device(
    pair_repr,
    asym_id,
    valid_len,
    rel_embed,
    pair_gain,
    bias_weight,
    tokens,
    token_gain,
    qkv_weight,
    out_weight,
):
    sample_count, token_rows, model_width = tokens.shape
    total_tokens = asym_id.shape[0]
    keymask = jnp.arange(total_tokens, dtype=jnp.int32) < valid_len[0]
    score_scale = 1.0 / math.sqrt(HEAD_DIM)
    bias_tile = bias_tile_of(pair_repr, asym_id, rel_embed, pair_gain, bias_weight)
    head_tile = lax.all_to_all(bias_tile, "row", split_axis=0, concat_axis=1, tiled=True)
    pair_bias = gathered_copies(head_tile, ("col", "samp"), 2)

    def one_sample(sample_item):
        return attend(
            sample_item[0], sample_item[1], sample_item[2], pair_bias, keymask, score_scale
        )

    current = tokens
    normed = normalize(current.astype(jnp.float32), token_gain[0]).astype(jnp.bfloat16)
    layer_weight = qkv_weight[0]
    projected = jnp.einsum(
        "snc,pcw->psnw",
        lax.all_gather(normed, "row", axis=1, tiled=True),
        layer_weight,
        preferred_element_type=jnp.float32,
    ).astype(jnp.bfloat16)
    head_out = lax.map(one_sample, (projected[0], projected[1], projected[2]))
    attended = lax.all_to_all(head_out, "row", split_axis=1, concat_axis=2, tiled=True)
    flattened = attended.reshape(sample_count * token_rows, model_width)
    update = jnp.dot(
        flattened, gathered_copies(out_weight[0], "row", 0), preferred_element_type=jnp.float32
    )
    current = (
        current.astype(jnp.float32) + update.reshape(sample_count, token_rows, model_width)
    ).astype(jnp.bfloat16)
    return current


def solution(mesh):
    return jax.shard_map(
        per_device,
        mesh=mesh,
        in_specs=(
            P(("job", "row"), ("col", "samp"), None),
            P("job"),
            P("job"),
            P(),
            P(),
            P(),
            P(("job", "col", "samp"), "row", None),
            P(),
            P(None, None, None, "row"),
            P(None, "row", None),
        ),
        out_specs=P(("job", "col", "samp"), "row", None),
        check_vma=False,
    )
```

profile of v0, /device:TPU:80, one launch (start us, length us, event | category | flops | bytes accessed | tf_op | source)
XLA Modules:
  0.0 211.4 jit_solution(4686499185839951413)
XLA Ops:
  6.6 1.1 convert_reduce_fusion
  7.7 1.1 fusion.31
  8.8 0.7 reduce.4
  9.5 1.8 fusion.33
  11.4 0.8 fusion.40
  12.7 1.0 fusion.41
  14.2 56.2 %all_to_all.37 = f32[16,1,1024]{2,1,0:T(1,128)S(1)} all-to-all(f32[16,1,1024]{2,1,0:T(1,128)S(1)} %reshape.165), channel_id=1, replica_groups=mesh['job'=2,'row'=16,'col'=8,'samp'=2] {'row'}, dimensions={0} | all-to-all | bytes 131072 | tf_op jit(solution)/shard_map/all_to_all | solution.py:98
  70.9 0.7 reduce.5
  71.8 1.1 broadcast_in_dim.49
  72.9 7.6 %all-to-all-start.1 = ((f32[16,1,512,32]{2,3,1,0:T(8,128)}), f32[16,1,512,32]{2,3,1,0:T(8,128)S(1)}, u32[]{:S(2)}, u32[]{:S(2)}) async-start(f32[16,1,512,32]{2,3,1,0:T(8,128)} %broadcast_in_dim.49), calls=%async_computation.1 | async-start | bytes 2097152 | tf_op jit(solution)/shard_map/all_to_all | solution.py:22
  80.6 41.6 %all-gather.2.cloned.1.call-done = bf16[4,512,768]{2,1,0:T(8,128)(2,1)} async-done(((bf16[4,32,768]{2,1,0:T(8,128)(2,1)}), bf16[4,512,768]{2,1,0:T(8,128)(2,1)}) %all-gather.2.cloned.1.call-update) | async-done | bytes 3145744 | tf_op jit(solution)/shard_map/all_gather | solution.py:111
  122.1 3.0 %fusion.21 = bf16[3,4,512,48]{2,3,0,1:T(8,128)(2,1)S(1)} fusion(bf16[4,512,768]{2,1,0:T(8,128)(2,1)} %all-gather.2.cloned.1.call-done, bf16[1,3,768,48]{2,3,1,0:T(8,128)(2,1)S(1)} %copy-done), kind=kOutput, calls=%fused_computation.23 | convolution fusion | flops 453279744 | bytes 3956736 | tf_op jit(solution)/shard_map/snc,pcw->psnw/dot_general | solution.py:109
  125.2 6.6 %while.11 = (s32[]{:T(128)}, bf16[4,512,48]{1,2,0:T(8,128)(2,1)S(1)}, bf16[4,512,48]{1,2,0:T(8,128)(2,1)S(1)}, bf16[4,512,48]{1,2,0:T(8,128)(2,1)S(1)}, bf16[4,5...) while((s32[]{:T(128)}, bf16[4,512,48]{1,2,0:T(8,128)(2,1)S(1)}, ...), condition=%wide.region_7.8_spmd.clone, body=%wide.region_4.7_spmd.clone.sunk | while | flops 53239296 | bytes 4405345 | solution.py:115
  125.3 0.7 iota_compare_fusion.4
  126.9 0.7 iota_compare_fusion.4
  128.5 0.7 iota_compare_fusion.4
  130.2 0.7 iota_compare_fusion.4
  132.2 0.8 reshape.167
  133.0 20.2 %all_to_all.38 = bf16[16,2,3072]{2,1,0:T(2,128)(2,1)S(1)} all-to-all(bf16[16,2,3072]{2,1,0:T(2,128)(2,1)S(1)} %reshape.167), channel_id=1, replica_groups=mesh['job'=2,'row'=16,'col'=8,'samp'=2] {'row'}, dimensions={0} | all-to-all | bytes 393216 | tf_op jit(solution)/shard_map/all_to_all | solution.py:116
  153.1 1.1 broadcast_in_dim.50
  154.2 5.1 %all-to-all-start.3 = ((bf16[16,48,768]{2,1,0:T(8,128)(2,1)}), bf16[16,48,768]{2,1,0:T(8,128)(2,1)S(1)}, u32[]{:S(2)}, u32[]{:S(2)}) async-start(bf16[16,48,768]{2,1,0:T(8,128)(2,1)} %broadcast_in_dim.50), calls=%async_computation.3 | async-start | bytes 2359296 | tf_op jit(solution)/shard_map/all_to_all | solution.py:22
  159.3 0.5 reshape.168
  159.9 43.5 %all-to-all-done.3 = bf16[16,48,768]{2,1,0:T(8,128)(2,1)S(1)} async-done(((bf16[16,48,768]{2,1,0:T(8,128)(2,1)}), bf16[16,48,768]{2,1,0:T(8,128)(2,1)S(1)}, u32[]{:S(2)}, u32[]{:S(2)}) %all-to-all-start.3) | async-done | bytes 1179680 | tf_op jit(solution)/shard_map/all_to_all | solution.py:22
  203.4 1.1 fusion.26
  (49 shorter events, 6.1 us)
Async XLA Ops:
  6.5 115.6 %copy-start = (bf16[1,3,768,48]{2,3,1,0:T(8,128)(2,1)S(1)}, bf16[1,3,768,48]{2,3,1,0:T(8,128)(2,1)}, u32[]{:S(2)}) copy-start(bf16[1,3,768,48]{2,3,1,0:T(8,128)(2,1)} %param.20) | copy-start | bytes 663556
  6.6 5.8 %copy-start.2 = (bf16[32,32,128]{2,1,0:T(8,128)(2,1)S(1)}, bf16[32,32,128]{2,1,0:T(8,128)(2,1)}, u32[]{:S(2)}) copy-start(bf16[32,32,128]{2,1,0:T(8,128)(2,1)} %param.12) | copy-start | bytes 786436
  6.6 115.6 %all-gather.2.cloned.1.call-start = ((), (), s32[]{:S(2)}) async-start(), calls=%async_computation.4 | async-start | bytes 3342336 | tf_op jit(solution)/shard_map/all_gather | solution.py:111
  9.5 3.1 %copy-start.4 = (bf16[128,128]{1,0:T(8,128)(2,1)S(1)}, bf16[128,128]{1,0:T(8,128)(2,1)}, u32[]{:S(2)}) copy-start(bf16[128,128]{1,0:T(8,128)(2,1)} %param.15) | copy-start | bytes 98308
  12.4 1.3 copy-start.5
  12.4 1.3 copy-start.6
  72.9 52.3 %all-to-all-start.1 = ((f32[16,1,512,32]{2,3,1,0:T(8,128)}), f32[16,1,512,32]{2,3,1,0:T(8,128)S(1)}, u32[]{:S(2)}, u32[]{:S(2)}) async-start(f32[16,1,512,32]{2,3,1,0:T(8,128)} %broadcast_in_dim.49), calls=%async_computation.1 | async-start | bytes 2097152 | tf_op jit(solution)/shard_map/all_to_all | solution.py:22
  131.8 21.3 %copy-start.3 = (bf16[1,48,768]{2,1,0:T(8,128)(2,1)S(1)}, bf16[1,48,768]{2,1,0:T(8,128)(2,1)}, u32[]{:S(2)}) copy-start(bf16[1,48,768]{2,1,0:T(8,128)(2,1)} %param.21) | copy-start | bytes 221188
  154.2 49.2 %all-to-all-start.3 = ((bf16[16,48,768]{2,1,0:T(8,128)(2,1)}), bf16[16,48,768]{2,1,0:T(8,128)(2,1)S(1)}, u32[]{:S(2)}, u32[]{:S(2)}) async-start(bf16[16,48,768]{2,1,0:T(8,128)(2,1)} %broadcast_in_dim.50), calls=%async_computation.3 | async-start | bytes 2359296 | tf_op jit(solution)/shard_map/all_to_all | solution.py:22
  159.3 44.1 %copy-start.1 = (bf16[4,32,768]{2,1,0:T(8,128)(2,1)S(1)}, bf16[4,32,768]{2,1,0:T(8,128)(2,1)}, u32[]{:S(2)}) copy-start(bf16[4,32,768]{2,1,0:T(8,128)(2,1)} %param.18) | copy-start | bytes 589828
Sparse Core Ops, SparseCore 0:
  11.5 110.6 all-gather.1
where the time goes:
time: 213 us; the launch traced here: 211 us
  waiting for transfers between devices  85.1 us (40%)
  blocking collectives  76.3 us (36%)
  between operations  13.7 us (6%)
  starting transfers between devices  12.7 us (6%)
  other arithmetic  9.07 us (4%)
  matrix products  8.31 us (4%)
  local copies, waits for them, and re-layouts  6.06 us (3%)
    all_to_all x1, blocking collectives, per_device(): lax.all_to_all(bias_tile, 'row', split_axis=0, concat_axis=1, tiled=True)  56.2 us
    all_to_all x2, waiting for transfers between devices, from_everyone(): return lax.all_to_all(copies, axis, split_axis=0, concat_axis=0, tiled=True)  43.5 us
    all_gather x1, waiting for transfers between devices, per_device(): lax.all_gather(normed, 'row', axis=1, tiled=True)  41.6 us
    all_to_all x1, blocking collectives, per_device(): lax.all_to_all(head_out, 'row', split_axis=1, concat_axis=2, tiled=True)  20.2 us
    all_to_all x2, starting transfers between devices, from_everyone(): return lax.all_to_all(copies, axis, split_axis=0, concat_axis=0, tiled=True)  12.7 us
  transfers between devices with their start and end apart: 3, of which 2 were waited for; matrix products, arithmetic and copies ran while one was open for 4% of the time, Pallas kernels for 0%

commit v1 on v0

v1 whole, which is shorter than its diff:
```python
import math

import jax
import jax.numpy as jnp
from jax import lax
from jax.sharding import PartitionSpec as P

HEAD_DIM = 48
QUAD = 4

epsilon = 1e-05


def normalize(values, gain_vector):
    average = jnp.mean(values, axis=-1, keepdims=True)
    centered = values - average
    variance = jnp.mean(centered * centered, axis=-1, keepdims=True)
    return centered * lax.rsqrt(variance + epsilon) * gain_vector


def exchange(blocks, axis, groups=None):
    return lax.all_to_all(
        blocks, axis, split_axis=0, concat_axis=0, axis_index_groups=groups, tiled=True
    )


def bias_tile_of(pair_repr, asym_id, rel_embed, pair_gain, bias_weight):
    tile_rows, tile_cols, channels = pair_repr.shape
    bin_count = rel_embed.shape[0]
    reach_max = bin_count // 2 - 1
    first_row = lax.axis_index("row") * tile_rows
    first_col = lax.axis_index(("col", "samp")) * tile_cols
    row_ids = first_row + jnp.arange(tile_rows, dtype=jnp.int32)
    col_ids = first_col + jnp.arange(tile_cols, dtype=jnp.int32)
    row_chain = lax.dynamic_slice_in_dim(asym_id, first_row, tile_rows, 0)
    col_chain = lax.dynamic_slice_in_dim(asym_id, first_col, tile_cols, 0)
    offset = jnp.clip(row_ids[:, None] - col_ids[None, :], -reach_max, reach_max) + reach_max
    bin_ids = jnp.where(row_chain[:, None] == col_chain[None, :], offset, bin_count - 1)
    onehot = (
        bin_ids.reshape(-1)[:, None] == jnp.arange(bin_count, dtype=jnp.int32)[None, :]
    ).astype(jnp.bfloat16)
    summed = pair_repr.reshape(-1, channels).astype(jnp.float32) + jnp.dot(
        onehot, rel_embed, preferred_element_type=jnp.float32
    )
    normed = normalize(summed, pair_gain).astype(jnp.bfloat16)
    projected = lax.dot_general(
        bias_weight, normed, (((0,), (1,)), ((), ())), preferred_element_type=jnp.float32
    )
    return projected


def per_device(
    pair_repr,
    asym_id,
    valid_len,
    rel_embed,
    pair_gain,
    bias_weight,
    tokens,
    token_gain,
    qkv_weight,
    out_weight,
):
    sample_count, token_rows, width = tokens.shape
    total = asym_id.shape[0]
    rows = lax.axis_size("row")
    cols = lax.axis_size("col")
    tile_rows, tile_cols, _ = pair_repr.shape
    heads = bias_weight.shape[1]
    quads = rows // QUAD
    strided = [[a + QUAD * b for b in range(quads)] for a in range(QUAD)]
    adjacent = [[QUAD * a + b for b in range(QUAD)] for a in range(quads)]
    z = lax.axis_index("row")
    side = (z // QUAD) % 2
    core = lax.axis_index("samp")
    swap = [(0, 1), (1, 0)]
    keymask = jnp.arange(total, dtype=jnp.int32) < valid_len[0]
    score_scale = 1.0 / math.sqrt(HEAD_DIM)

    own_w = qkv_weight[0]
    half = width // 2
    part = lax.dynamic_slice_in_dim(own_w, core * half, half, 1)
    far = lax.ppermute(part, "row", [(i, i ^ QUAD) for i in range(rows)])
    near = lax.ppermute(far, "samp", swap)
    other_w = jnp.where(
        core == 0, jnp.concatenate([far, near], 1), jnp.concatenate([near, far], 1)
    )
    own_first = side == core
    w_a = jnp.where(own_first, own_w, other_w)
    w_b = jnp.where(own_first, other_w, own_w)
    w_pair = jnp.stack([w_a, w_b])

    paired = bias_weight.reshape(-1, heads // 8, 2, QUAD).transpose(0, 1, 3, 2).reshape(-1, heads)
    tile = bias_tile_of(pair_repr, asym_id, rel_embed, pair_gain, paired)
    tile = tile.reshape(heads // 8, 1, QUAD, 2, tile_rows * tile_cols)
    tile = jnp.broadcast_to(tile, (heads // 8, 2, QUAD, 2, tile_rows * tile_cols))
    by_row = exchange(tile.reshape(rows, 2, tile_rows * tile_cols), "row")
    by_key = by_row.reshape(rows, 2, tile_rows, tile_cols).transpose(1, 3, 0, 2)
    by_key = by_key.reshape(1, 2, tile_cols, total)
    fanned = jnp.broadcast_to(by_key, (cols, 2, tile_cols, total)).reshape(
        2 * cols, tile_cols, total
    )
    bias_a = exchange(fanned, ("col", "samp")).reshape(total, total)
    bias_b = lax.ppermute(bias_a, "samp", swap)
    biases = jnp.stack([bias_a, bias_b])

    normed = normalize(tokens.astype(jnp.float32), token_gain[0]).astype(jnp.bfloat16)
    halves = normed.reshape(2, sample_count // 2 * token_rows, width)
    gathered = exchange(jnp.concatenate([halves] * (quads // 2)), "row", strided)
    gathered = jnp.broadcast_to(gathered[None], (QUAD, *gathered.shape))
    gathered = exchange(gathered, "row", adjacent)
    gathered = gathered.reshape(QUAD, quads, sample_count // 2, token_rows, width)
    gathered = gathered.transpose(2, 1, 0, 3, 4).reshape(sample_count // 2, total, width)

    depth = out_weight.shape[1]
    slice_rows = depth // cols
    piece = lax.dynamic_slice_in_dim(
        out_weight[0], lax.axis_index("col") * slice_rows, slice_rows, 0
    )
    pieces = exchange(jnp.broadcast_to(piece[None], (rows, *piece.shape)), "row")
    pieces = exchange(
        jnp.broadcast_to(pieces.reshape(1, rows * slice_rows, width), (cols, rows * slice_rows, width)),
        "col",
    )
    w_out = pieces.reshape(cols, rows // 8, 2, QUAD, slice_rows, width)
    w_out = w_out.transpose(1, 3, 2, 0, 4, 5).reshape(width, width)

    projected = jnp.einsum(
        "snc,hpcw->pshnw", gathered, w_pair, preferred_element_type=jnp.float32
    ).astype(jnp.bfloat16)
    query, key, value = projected[0], projected[1], projected[2]
    scores = (
        jnp.einsum("shjd,shid->shji", key, query, preferred_element_type=jnp.float32) * score_scale
        + biases[None]
    )
    mask = keymask[None, None, :, None]
    scores = jnp.where(mask, scores, -1e30)
    row_max = jnp.max(scores, axis=2, keepdims=True)
    weights = jnp.where(mask, jnp.exp(scores - row_max), 0.0)
    row_total = jnp.sum(weights, axis=2, keepdims=True)
    probs = (weights / row_total).astype(jnp.bfloat16)
    attended = jnp.einsum(
        "shji,shjd->sihd", probs, value, preferred_element_type=jnp.float32
    ).astype(jnp.bfloat16)
    attended = jnp.where(core == 0, attended, attended[:, :, ::-1])

    back = attended.reshape(sample_count // 2, rows, token_rows, 2 * HEAD_DIM)
    back = exchange(back.transpose(1, 0, 2, 3), "row")
    back = back.reshape(rows // 8, 2, QUAD, sample_count // 2, token_rows, 2 * HEAD_DIM)
    back = back.transpose(1, 3, 4, 0, 2, 5).reshape(sample_count * token_rows, width)
    update = jnp.dot(back, w_out, preferred_element_type=jnp.float32)
    return (
        tokens.astype(jnp.float32) + update.reshape(sample_count, token_rows, width)
    ).astype(jnp.bfloat16)


def solution(mesh):
    return jax.shard_map(
        per_device,
        mesh=mesh,
        in_specs=(
            P(("job", "row"), ("col", "samp"), None),
            P("job"),
            P("job"),
            P(),
            P(),
            P(),
            P(("job", "col", "samp"), "row", None),
            P(),
            P(None, None, None, "row"),
            P(None, "row", None),
        ),
        out_specs=P(("job", "col", "samp"), "row", None),
        check_vma=False,
    )
```

time: 213 us -> 261 us (1.23)
  starting transfers between devices: 12.7 us -> 84 us
  blocking collectives: 76.3 us -> 34.5 us
  waiting for transfers between devices: 85.1 us -> 114 us
  between operations: 13.7 us -> 1.07 us
  other arithmetic: 9.07 us -> 5.59 us
  local copies, waits for them, and re-layouts: 6.06 us -> 8.98 us
  matrix products: 8.31 us -> 11.2 us
    all_to_all x2 -> x6, starting transfers between devices: 12.7 us -> 71.9 us  [exchange(): lax.all_to_all(blocks, axis, split_axis=0, concat_axis=0, axis_index_grou...]
    all_to_all x2 -> x6, waiting for transfers between devices: 43.5 us -> 96.3 us  [exchange(): lax.all_to_all(blocks, axis, split_axis=0, concat_axis=0, axis_index_grou...]
    all_to_all x2 -> x1, blocking collectives: 76.3 us -> 34.5 us  [exchange(): lax.all_to_all(blocks, axis, split_axis=0, concat_axis=0, axis_index_grou...]
    all_gather x1 -> x0, waiting for transfers between devices: 41.6 us -> none  [per_device(): lax.all_gather(normed, 'row', axis=1, tiled=True)]
    ppermute x0 -> x3, waiting for transfers between devices: none -> 18.2 us  [the longest x1 18.1 us: per_device(): far = lax.ppermute(part, 'row', [(i, i ^ QUAD) for i in range(rows)])]
    ppermute x0 -> x3, starting transfers between devices: none -> 12.1 us  [the longest x1 6.07 us: per_device(): far = lax.ppermute(part, 'row', [(i, i ^ QUAD) for i in range(rows)])]
    sub x0 -> x1, matrix products: none -> 5.49 us  [per_device(): weights = jnp.where(mask, jnp.exp(scores - row_max), 0.0)]
    another operation x0 -> x1, other arithmetic: none -> 3.03 us  [per_device(): biases = jnp.stack([bias_a, bias_b])]
  transfers between devices with their start and end apart: 3 -> 9, of which waited for: 2 -> 7; matrix products, arithmetic and copies ran while one was open for 4% -> 7% of each run, Pallas kernels for 0% -> 0%
where the time goes in v1:
time: 261 us; the launch traced here: 260 us
  waiting for transfers between devices  114 us (44%)
  starting transfers between devices  84 us (32%)
  blocking collectives  34.5 us (13%)
  matrix products  11.2 us (4%)
  local copies, waits for them, and re-layouts  8.98 us (3%)
  other arithmetic  5.59 us (2%)
    all_to_all x6, waiting for transfers between devices, exchange(): lax.all_to_all(blocks, axis, split_axis=0, concat_axis=0, axis_index_grou...  96.3 us
    all_to_all x6, starting transfers between devices, exchange(): lax.all_to_all(blocks, axis, split_axis=0, concat_axis=0, axis_index_grou...  71.9 us
    all_to_all x1, blocking collectives, exchange(): lax.all_to_all(blocks, axis, split_axis=0, concat_axis=0, axis_index_grou...  34.5 us
    ppermute x1, waiting for transfers between devices, per_device(): far = lax.ppermute(part, 'row', [(i, i ^ QUAD) for i in range(rows)])  18.1 us
    ppermute x1, starting transfers between devices, per_device(): far = lax.ppermute(part, 'row', [(i, i ^ QUAD) for i in range(rows)])  6.07 us
    sub x1, matrix products, per_device(): weights = jnp.where(mask, jnp.exp(scores - row_max), 0.0)  5.49 us
  transfers between devices with their start and end apart: 9, of which 7 were waited for; matrix products, arithmetic and copies ran while one was open for 7% of the time, Pallas kernels for 0%

profile of v1, /device:TPU:80, one launch (start us, length us, event | category | flops | bytes accessed | tf_op | source)
XLA Modules:
  0.0 259.8 jit_solution(10739914088505033008)
XLA Ops:
  2.2 1.2 fusion.40
  4.5 43.7 %all-to-all-start.2 = ((f32[16,2,1024]{2,1,0:T(2,128)}), f32[16,2,1024]{2,1,0:T(2,128)S(1)}, u32[]{:S(2)}, u32[]{:S(2)}) async-start(f32[16,2,1024]{2,1,0:T(2,128)} %bitcast.21), calls=%async_computation.2 | async-start | bytes 262144 | tf_op jit(solution)/shard_map/all_to_all | solution.py:22
  48.6 14.2 %all-to-all-done.2 = f32[16,2,1024]{2,1,0:T(2,128)S(1)} async-done(((f32[16,2,1024]{2,1,0:T(2,128)}), f32[16,2,1024]{2,1,0:T(2,128)S(1)}, u32[]{:S(2)}, u32[]{:S(2)}) %all-to-all-start.2) | async-done | bytes 131104 | tf_op jit(solution)/shard_map/all_to_all | solution.py:22
  63.5 4.0 %all-to-all-start.5 = ((bf16[16,6,768]{2,1,0:T(8,128)(2,1)}), bf16[16,6,768]{2,1,0:T(8,128)(2,1)S(1)}, u32[]{:S(2)}, u32[]{:S(2)}) async-start(bf16[16,6,768]{2,1,0:T(8,128)(2,1)} %broadcast_in_dim.81), calls=%async_computation.5 | async-start | bytes 393216 | tf_op jit(solution)/shard_map/all_to_all | solution.py:22
  68.5 14.7 %all-to-all-done.5 = bf16[16,6,768]{2,1,0:T(8,128)(2,1)S(1)} async-done(((bf16[16,6,768]{2,1,0:T(8,128)(2,1)}), bf16[16,6,768]{2,1,0:T(8,128)(2,1)S(1)}, u32[]{:S(2)}, u32[]{:S(2)}) %all-to-all-start.5) | async-done | bytes 147488 | tf_op jit(solution)/shard_map/all_to_all | solution.py:22
  83.2 4.8 %all-to-all-start = ((bf16[4,64,768]{2,1,0:T(8,128)(2,1)}), bf16[4,64,768]{2,1,0:T(8,128)(2,1)S(1)}, u32[]{:S(2)}, u32[]{:S(2)}) async-start(bf16[4,64,768]{2,1,0:T(8,128)(2,1)} %pad_maximum_fusion.1), calls=%async_computation | async-start | bytes 786432 | tf_op jit(solution)/shard_map/all_to_all | solution.py:22
  88.4 20.6 %all-to-all-done = bf16[4,64,768]{2,1,0:T(8,128)(2,1)S(1)} async-done(((bf16[4,64,768]{2,1,0:T(8,128)(2,1)}), bf16[4,64,768]{2,1,0:T(8,128)(2,1)S(1)}, u32[]{:S(2)}, u32[]{:S(2)}) %all-to-all-start) | async-done | bytes 393248 | tf_op jit(solution)/shard_map/all_to_all | solution.py:22
  109.2 34.5 %all_to_all.35 = f32[16,32,512]{2,1,0:T(8,128)} all-to-all(f32[16,32,512]{2,1,0:T(8,128)S(1)} %bitcast.66), channel_id=1, replica_groups=mesh['job'=2,'row'=16,'col'=8,'samp'=2] {'col','samp'}, dimensions={0} | all-to-all | bytes 2097152 | tf_op jit(solution)/shard_map/all_to_all | solution.py:22
  143.7 1.3 broadcast_in_dim.40
  145.0 6.6 %all-to-all-start.1 = ((bf16[4,4,64,768]{3,2,1,0:T(8,128)(2,1)}), bf16[4,4,64,768]{3,2,1,0:T(8,128)(2,1)S(1)}, u32[]{:S(2)}, u32[]{:S(2)}) async-start(bf16[4,4,64,768]{3,2,1,0:T(8,128)(2,1)} %broadcast_in_dim.40), calls=%async_computation.1 | async-start | bytes 3145728 | tf_op jit(solution)/shard_map/all_to_all | solution.py:22
  151.6 3.3 %collective-permute-start.2 = (f32[512,512]{1,0:T(8,128)}, f32[512,512]{1,0:T(8,128)}, u32[]{:S(2)}, u32[]{:S(2)}) collective-permute-start(f32[512,512]{1,0:T(8,128)} %bitcast.26), channel_id=1, source_target_pairs={{0,1},{1,0},{2,3},{3,2},{4,5},{5,4},{6,7},{7,6},{8,9},{9,8},{10,11... | collective-permute-start | bytes 3145736 | tf_op jit(solution)/shard_map/ppermute | solution.py:104
  154.9 6.1 %collective-permute-start = (bf16[3,384,48]{1,2,0:T(8,128)(2,1)S(1)}, bf16[3,384,48]{1,2,0:T(8,128)(2,1)S(1)}, u32[]{:S(2)}, u32[]{:S(2)}) collective-permute-start(bf16[3,384,48]{1,2,0:T(8,128)(2,1)S(1)} %dynamic-slice_bitcast_fusion), channel_id=1, source_target_pairs={{0,64},{16,80},{32,96},{48,112},{64,0},{80,16},{96,32},{112,48},{1... | collective-permute-start | bytes 331784 | tf_op jit(solution)/shard_map/ppermute | solution.py:83
  161.7 18.1 %collective-permute-done = bf16[3,384,48]{1,2,0:T(8,128)(2,1)S(1)} collective-permute-done((bf16[3,384,48]{1,2,0:T(8,128)(2,1)S(1)}, bf16[3,384,48]{1,2,0:T(8,128)(2,1)S(1)}, u32[]{:S(2)}, u32[]{:S(2)}) %collective-permute-start) | collective-permute-done | bytes 110624 | tf_op jit(solution)/shard_map/ppermute | solution.py:83
  179.8 2.8 %collective-permute-start.1 = (bf16[3,384,48]{1,2,0:T(8,128)(2,1)S(1)}, bf16[3,384,48]{1,2,0:T(8,128)(2,1)S(1)}, u32[]{:S(2)}, u32[]{:S(2)}) collective-permute-start(bf16[3,384,48]{1,2,0:T(8,128)(2,1)S(1)} %collective-permute-done), channel_id=1, source_target_pairs={{0,1},{1,0},{2,3},{3,2},{4,5},{5,4},{6,7},{7,6},{8,9},{9,8},{10,11... | collective-permute-start | bytes 331784 | tf_op jit(solution)/shard_map/ppermute | solution.py:84
  182.7 11.6 %all-to-all-done.1 = bf16[4,4,64,768]{3,2,1,0:T(8,128)(2,1)S(1)} async-done(((bf16[4,4,64,768]{3,2,1,0:T(8,128)(2,1)}), bf16[4,4,64,768]{3,2,1,0:T(8,128)(2,1)S(1)}, u32[]{:S(2)}, u32[]{:S(2)}) %all-to-all-start.1) | async-done | bytes 1572896 | tf_op jit(solution)/shard_map/all_to_all | solution.py:22
  194.2 1.1 broadcast_in_dim.83
  195.4 3.8 %all-to-all-start.6 = ((bf16[8,96,768]{2,1,0:T(8,128)(2,1)}), bf16[8,96,768]{2,1,0:T(8,128)(2,1)S(1)}, u32[]{:S(2)}, u32[]{:S(2)}) async-start(bf16[8,96,768]{2,1,0:T(8,128)(2,1)} %broadcast_in_dim.83), calls=%async_computation.6 | async-start | bytes 2359296 | tf_op jit(solution)/shard_map/all_to_all | solution.py:22
  199.3 3.0 %pad_maximum_fusion = f32[2,512,512]{2,1,0:T(8,128)} fusion(f32[1,512,512]{2,1,0:T(8,128)} %bitcast.27, f32[1,512,512]{2,1,0:T(8,128)} %bitcast.25), kind=kLoop, calls=%fused_computation.5 | loop fusion | flops 524288 | bytes 4194304 | tf_op jit(solution)/shard_map/stack | solution.py:105
  203.2 5.5 %fusion.41 = (f32[2,2,512]{2,1,0:T(2,128)S(1)}, f32[2,2,512,512]{3,2,1,0:T(8,128)}) fusion(f32[2,512,512]{2,1,0:T(8,128)} %pad_maximum_fusion, pred[512]{0:T(512)(128)(4,1)S(1)} %iota_compare_fusion.2, bf16[2,2,512,48]{2,3,0,1:T(8,128)(2,1)S(1)} %get-tuple-element.6, bf16[2,2,512,48]{2,3,0,1:T(8,128)(2,1)S(1)} %get-tuple-element.7), kind=kOutput, calls=%fused_computation.68 | convolution fusion | flops 106955264 | bytes 6693376 | tf_op jit(solution)/shard_map/sub | solution.py:139
  208.7 2.7 %fusion.10 = bf16[2,512,2,48]{1,3,2,0:T(8,128)(2,1)S(1)} fusion(f32[2,2,512,512]{3,2,1,0:T(8,128)} %get-tuple-element.15, f32[2,2,512]{2,1,0:T(2,128)S(1)} %get-tuple-element.14, bf16[2,2,512,48]{2,3,0,1:T(8,128)(2,1)S(1)} %get-tuple-element.5), kind=kOutput, calls=%fused_computation.17 | convolution fusion | flops 102858752 | bytes 4595712 | tf_op jit(solution)/shard_map/shji,shjd->sihd/dot_general | solution.py:142
  212.8 18.4 %all-to-all-done.6 = bf16[8,96,768]{2,1,0:T(8,128)(2,1)S(1)} async-done(((bf16[8,96,768]{2,1,0:T(8,128)(2,1)}), bf16[8,96,768]{2,1,0:T(8,128)(2,1)S(1)}, u32[]{:S(2)}, u32[]{:S(2)}) %all-to-all-start.6) | async-done | bytes 1179680 | tf_op jit(solution)/shard_map/all_to_all | solution.py:22
  231.2 9.0 %all-to-all-start.4 = ((bf16[16,2,32,96]{3,2,1,0:T(8,128)(2,1)}), bf16[16,2,32,96]{3,2,1,0:T(8,128)(2,1)S(1)}, u32[]{:S(2)}, u32[]{:S(2)}) async-start(bf16[16,2,32,96]{3,2,1,0:T(8,128)(2,1)} %copy.36), calls=%async_computation.4 | async-start | bytes 524288 | tf_op jit(solution)/shard_map/all_to_all | solution.py:22
  241.6 16.8 %all-to-all-done.4 = bf16[16,2,32,96]{3,2,1,0:T(8,128)(2,1)S(1)} async-done(((bf16[16,2,32,96]{3,2,1,0:T(8,128)(2,1)}), bf16[16,2,32,96]{3,2,1,0:T(8,128)(2,1)S(1)}, u32[]{:S(2)}, u32[]{:S(2)}) %all-to-all-start.4) | async-done | bytes 196640 | tf_op jit(solution)/shard_map/all_to_all | solution.py:22
  258.8 1.0 fusion.8
  (56 shorter events, 10.0 us)
Async XLA Ops:
  0.0 48.2 %copy-start = (bf16[1,48,768]{2,1,0:T(8,128)(2,1)S(1)}, bf16[1,48,768]{2,1,0:T(8,128)(2,1)}, u32[]{:S(2)}) copy-start(bf16[1,48,768]{2,1,0:T(8,128)(2,1)} %param.19) | copy-start | bytes 221188
  0.0 3.5 %copy-start.3 = (bf16[128,16]{0,1:T(8,128)(2,1)S(1)}, bf16[128,16]{0,1:T(8,128)(2,1)}, u32[]{:S(2)}) copy-start(bf16[128,16]{0,1:T(8,128)(2,1)} %param.15) | copy-start | bytes 12292
  0.0 3.5 %copy-start.5 = (f32[128]{0:T(128)S(1)}, f32[128]{0:T(128)}, u32[]{:S(2)}) copy-start(f32[128]{0:T(128)} %param.14) | copy-start | bytes 1540
  2.0 46.2 %copy-start.4 = (f32[1,768]{1,0:T(1,128)S(1)}, f32[1,768]{1,0:T(1,128)}, u32[]{:S(2)}) copy-start(f32[1,768]{1,0:T(1,128)} %param.17) | copy-start | bytes 9220
  2.0 46.3 %copy-start.1 = (bf16[4,32,768]{2,1,0:T(8,128)(2,1)S(1)}, bf16[4,32,768]{2,1,0:T(8,128)(2,1)}, u32[]{:S(2)}) copy-start(bf16[4,32,768]{2,1,0:T(8,128)(2,1)} %param.16) | copy-start | bytes 589828
  4.5 58.3 %all-to-all-start.2 = ((f32[16,2,1024]{2,1,0:T(2,128)}), f32[16,2,1024]{2,1,0:T(2,128)S(1)}, u32[]{:S(2)}, u32[]{:S(2)}) async-start(f32[16,2,1024]{2,1,0:T(2,128)} %bitcast.21), calls=%async_computation.2 | async-start | bytes 262144 | tf_op jit(solution)/shard_map/all_to_all | solution.py:22
  63.5 19.7 %all-to-all-start.5 = ((bf16[16,6,768]{2,1,0:T(8,128)(2,1)}), bf16[16,6,768]{2,1,0:T(8,128)(2,1)S(1)}, u32[]{:S(2)}, u32[]{:S(2)}) async-start(bf16[16,6,768]{2,1,0:T(8,128)(2,1)} %broadcast_in_dim.81), calls=%async_computation.5 | async-start | bytes 393216 | tf_op jit(solution)/shard_map/all_to_all | solution.py:22
  83.2 25.8 %all-to-all-start = ((bf16[4,64,768]{2,1,0:T(8,128)(2,1)}), bf16[4,64,768]{2,1,0:T(8,128)(2,1)S(1)}, u32[]{:S(2)}, u32[]{:S(2)}) async-start(bf16[4,64,768]{2,1,0:T(8,128)(2,1)} %pad_maximum_fusion.1), calls=%async_computation | async-start | bytes 786432 | tf_op jit(solution)/shard_map/all_to_all | solution.py:22
  143.7 11.2 %copy-start.2 = (bf16[1,3,768,48]{2,3,1,0:T(8,128)(2,1)S(1)}, bf16[1,3,768,48]{2,3,1,0:T(8,128)(2,1)}, u32[]{:S(2)}) copy-start(bf16[1,3,768,48]{2,3,1,0:T(8,128)(2,1)} %param.18) | copy-start | bytes 663556
  145.0 49.3 %all-to-all-start.1 = ((bf16[4,4,64,768]{3,2,1,0:T(8,128)(2,1)}), bf16[4,4,64,768]{3,2,1,0:T(8,128)(2,1)S(1)}, u32[]{:S(2)}, u32[]{:S(2)}) async-start(bf16[4,4,64,768]{3,2,1,0:T(8,128)(2,1)} %broadcast_in_dim.40), calls=%async_computation.1 | async-start | bytes 3145728 | tf_op jit(solution)/shard_map/all_to_all | solution.py:22
  151.6 47.7 %collective-permute-start.2 = (f32[512,512]{1,0:T(8,128)}, f32[512,512]{1,0:T(8,128)}, u32[]{:S(2)}, u32[]{:S(2)}) collective-permute-start(f32[512,512]{1,0:T(8,128)} %bitcast.26), channel_id=1, source_target_pairs={{0,1},{1,0},{2,3},{3,2},{4,5},{5,4},{6,7},{7,6},{8,9},{9,8},{10,11... | collective-permute-start | bytes 3145736 | tf_op jit(solution)/shard_map/ppermute | solution.py:104
  154.9 24.9 %collective-permute-start = (bf16[3,384,48]{1,2,0:T(8,128)(2,1)S(1)}, bf16[3,384,48]{1,2,0:T(8,128)(2,1)S(1)}, u32[]{:S(2)}, u32[]{:S(2)}) collective-permute-start(bf16[3,384,48]{1,2,0:T(8,128)(2,1)S(1)} %dynamic-slice_bitcast_fusion), channel_id=1, source_target_pairs={{0,64},{16,80},{32,96},{48,112},{64,0},{80,16},{96,32},{112,48},{1... | collective-permute-start | bytes 331784 | tf_op jit(solution)/shard_map/ppermute | solution.py:83
  179.8 19.3 %collective-permute-start.1 = (bf16[3,384,48]{1,2,0:T(8,128)(2,1)S(1)}, bf16[3,384,48]{1,2,0:T(8,128)(2,1)S(1)}, u32[]{:S(2)}, u32[]{:S(2)}) collective-permute-start(bf16[3,384,48]{1,2,0:T(8,128)(2,1)S(1)} %collective-permute-done), channel_id=1, source_target_pairs={{0,1},{1,0},{2,3},{3,2},{4,5},{5,4},{6,7},{7,6},{8,9},{9,8},{10,11... | collective-permute-start | bytes 331784 | tf_op jit(solution)/shard_map/ppermute | solution.py:84
  195.4 35.8 %all-to-all-start.6 = ((bf16[8,96,768]{2,1,0:T(8,128)(2,1)}), bf16[8,96,768]{2,1,0:T(8,128)(2,1)S(1)}, u32[]{:S(2)}, u32[]{:S(2)}) async-start(bf16[8,96,768]{2,1,0:T(8,128)(2,1)} %broadcast_in_dim.83), calls=%async_computation.6 | async-start | bytes 2359296 | tf_op jit(solution)/shard_map/all_to_all | solution.py:22
  231.2 27.2 %all-to-all-start.4 = ((bf16[16,2,32,96]{3,2,1,0:T(8,128)(2,1)}), bf16[16,2,32,96]{3,2,1,0:T(8,128)(2,1)S(1)}, u32[]{:S(2)}, u32[]{:S(2)}) async-start(bf16[16,2,32,96]{3,2,1,0:T(8,128)(2,1)} %copy.36), calls=%async_computation.4 | async-start | bytes 524288 | tf_op jit(solution)/shard_map/all_to_all | solution.py:22

commit v2 on v1

--- a/solution.py
+++ b/solution.py
@@ -68,7 +68,6 @@
     tile_rows, tile_cols, _ = pair_repr.shape
     heads = bias_weight.shape[1]
     quads = rows // QUAD
-    strided = [[a + QUAD * b for b in range(quads)] for a in range(QUAD)]
     adjacent = [[QUAD * a + b for b in range(QUAD)] for a in range(quads)]
     z = lax.axis_index("row")
     side = (z // QUAD) % 2
@@ -77,6 +76,10 @@
     keymask = jnp.arange(total, dtype=jnp.int32) < valid_len[0]
     score_scale = 1.0 / math.sqrt(HEAD_DIM)
 
+    def shifted(value, axis, by):
+        size = lax.axis_size(axis)
+        return lax.ppermute(value, axis, [(i, (i + by) % size) for i in range(size)])
+
     own_w = qkv_weight[0]
     half = width // 2
     part = lax.dynamic_slice_in_dim(own_w, core * half, half, 1)
@@ -96,34 +99,60 @@
     tile = jnp.broadcast_to(tile, (heads // 8, 2, QUAD, 2, tile_rows * tile_cols))
     by_row = exchange(tile.reshape(rows, 2, tile_rows * tile_cols), "row")
     by_key = by_row.reshape(rows, 2, tile_rows, tile_cols).transpose(1, 3, 0, 2)
-    by_key = by_key.reshape(1, 2, tile_cols, total)
-    fanned = jnp.broadcast_to(by_key, (cols, 2, tile_cols, total)).reshape(
-        2 * cols, tile_cols, total
-    )
-    bias_a = exchange(fanned, ("col", "samp")).reshape(total, total)
+    by_key = by_key.reshape(2, tile_cols, total)
+    keep = jnp.where(core == 0, by_key[0], by_key[1])
+    got = lax.ppermute(jnp.where(core == 0, by_key[1], by_key[0]), "samp", swap)
+    chip_keys = jnp.where(
+        core == 0, jnp.concatenate([keep, got]), jnp.concatenate([got, keep])
+    )
+    col = lax.axis_index("col")
+
+    def all_cols(block):
+        size = block.shape[0]
+        whole = jnp.zeros((cols * size, *block.shape[1:]), block.dtype)
+        start = (0,) * (block.ndim - 1)
+        whole = lax.dynamic_update_slice(whole, block, (col * size, *start))
+        up = down = block
+        for step in range(1, cols // 2 + 1):
+            up = shifted(up, "col", 1)
+            whole = lax.dynamic_update_slice(whole, up, ((col - step) % cols * size, *start))
+            if step < cols // 2:
+                down = shifted(down, "col", -1)
+                whole = lax.dynamic_update_slice(whole, down, ((col + step) % cols * size, *start))
+        return whole
+
+    bias_a = all_cols(chip_keys)
     bias_b = lax.ppermute(bias_a, "samp", swap)
     biases = jnp.stack([bias_a, bias_b])
 
     normed = normalize(tokens.astype(jnp.float32), token_gain[0]).astype(jnp.bfloat16)
-    halves = normed.reshape(2, sample_count // 2 * token_rows, width)
-    gathered = exchange(jnp.concatenate([halves] * (quads // 2)), "row", strided)
-    gathered = jnp.broadcast_to(gathered[None], (QUAD, *gathered.shape))
-    gathered = exchange(gathered, "row", adjacent)
-    gathered = gathered.reshape(QUAD, quads, sample_count // 2, token_rows, width)
-    gathered = gathered.transpose(2, 1, 0, 3, 4).reshape(sample_count // 2, total, width)
-
+    half_rows = sample_count // 2 * token_rows
+    halves = normed.reshape(2, half_rows, width)
     depth = out_weight.shape[1]
     slice_rows = depth // cols
-    piece = lax.dynamic_slice_in_dim(
-        out_weight[0], lax.axis_index("col") * slice_rows, slice_rows, 0
-    )
-    pieces = exchange(jnp.broadcast_to(piece[None], (rows, *piece.shape)), "row")
-    pieces = exchange(
-        jnp.broadcast_to(pieces.reshape(1, rows * slice_rows, width), (cols, rows * slice_rows, width)),
-        "col",
-    )
-    w_out = pieces.reshape(cols, rows // 8, 2, QUAD, slice_rows, width)
+    piece = lax.dynamic_slice_in_dim(out_weight[0], col * slice_rows, slice_rows, 0)
+    same = jnp.concatenate([jnp.where(side == 0, halves[0], halves[1]), piece])
+    cross = jnp.concatenate([jnp.where(side == 0, halves[1], halves[0]), piece])
+    around = jnp.stack(
+        [
+            same,
+            shifted(cross, "row", -QUAD),
+            shifted(same, "row", 2 * QUAD),
+            shifted(cross, "row", QUAD),
+        ]
+    )
+    around = lax.dynamic_slice_in_dim(
+        jnp.concatenate([around, around]), (quads - z // QUAD) % quads, quads, 0
+    )
+    gathered = jnp.broadcast_to(around[None], (QUAD, *around.shape))
+    gathered = exchange(gathered, "row", adjacent)
+    pieces = gathered[:, :, half_rows:].transpose(1, 0, 2, 3).reshape(-1, width)
+    w_out = all_cols(pieces).reshape(cols, rows // 8, 2, QUAD, slice_rows, width)
     w_out = w_out.transpose(1, 3, 2, 0, 4, 5).reshape(width, width)
+    gathered = gathered[:, :, :half_rows].reshape(
+        QUAD, quads, sample_count // 2, token_rows, width
+    )
+    gathered = gathered.transpose(2, 1, 0, 3, 4).reshape(sample_count // 2, total, width)
 
     projected = jnp.einsum(
         "snc,hpcw->pshnw", gathered, w_pair, preferred_element_type=jnp.float32

time: 261 us -> 210 us (0.80)
  waiting for transfers between devices: 114 us -> 52.5 us
  starting transfers between devices: 84 us -> 126 us
  blocking collectives: 34.5 us -> 0 us
  other arithmetic: 5.59 us -> 8.24 us
    ppermute x0 -> x18, starting transfers between devices: none -> 94 us  [the longest x17 92 us: shifted(): lax.ppermute(value, axis, [(i, (i + by) % size) for i in range(size)])]
    all_to_all x6 -> x3, waiting for transfers between devices: 96.3 us -> 13.3 us  [exchange(): lax.all_to_all(blocks, axis, split_axis=0, concat_axis=0, axis_index_grou...]
    all_to_all x6 -> x3, starting transfers between devices: 71.9 us -> 24.9 us  [exchange(): lax.all_to_all(blocks, axis, split_axis=0, concat_axis=0, axis_index_grou...]
    all_to_all x1 -> x0, blocking collectives: 34.5 us -> none  [exchange(): lax.all_to_all(blocks, axis, split_axis=0, concat_axis=0, axis_index_grou...]
    ppermute x0 -> x18, waiting for transfers between devices: none -> 23.3 us  [the longest x17 22.2 us: shifted(): lax.ppermute(value, axis, [(i, (i + by) % size) for i in range(size)])]
    ppermute x1, waiting for transfers between devices: 18.1 us -> 14.3 us  [per_device(): far = lax.ppermute(part, 'row', [(i, i ^ QUAD) for i in range(rows)])]
    ppermute x1, starting transfers between devices: 6.07 us -> 3.45 us  [per_device(): far = lax.ppermute(part, 'row', [(i, i ^ QUAD) for i in range(rows)])]
  transfers between devices with their start and end apart: 9 -> 24, of which waited for: 7 -> 10; matrix products, arithmetic and copies ran while one was open for 7% -> 10% of each run, Pallas kernels for 0% -> 0%
where the time goes in v2:
time: 210 us; the launch traced here: 209 us
  starting transfers between devices  126 us (60%)
  waiting for transfers between devices  52.5 us (25%)
  local copies, waits for them, and re-layouts  10.6 us (5%)
  matrix products  9.53 us (5%)
  other arithmetic  8.24 us (4%)
    ppermute x17, starting transfers between devices, shifted(): lax.ppermute(value, axis, [(i, (i + by) % size) for i in range(size)])  92 us
    all_to_all x3, starting transfers between devices, exchange(): lax.all_to_all(blocks, axis, split_axis=0, concat_axis=0, axis_index_grou...  24.9 us
    ppermute x17, waiting for transfers between devices, shifted(): lax.ppermute(value, axis, [(i, (i + by) % size) for i in range(size)])  22.2 us
    ppermute x1, waiting for transfers between devices, per_device(): far = lax.ppermute(part, 'row', [(i, i ^ QUAD) for i in range(rows)])  14.3 us
    all_to_all x3, waiting for transfers between devices, exchange(): lax.all_to_all(blocks, axis, split_axis=0, concat_axis=0, axis_index_grou...  13.3 us
  transfers between devices with their start and end apart: 24, of which 10 were waited for; matrix products, arithmetic and copies ran while one was open for 10% of the time, Pallas kernels for 0%

profile of v2, /device:TPU:80, one launch (start us, length us, event | category | flops | bytes accessed | tf_op | source)
XLA Modules:
  0.0 208.8 jit_solution(401553135039791701)
XLA Ops:
  4.2 17.8 %collective-permute-start.4 = (bf16[70,768]{1,0:T(8,128)(2,1)S(1)}, bf16[70,768]{1,0:T(8,128)(2,1)S(1)}, u32[]{:S(2)}, u32[]{:S(2)}) collective-permute-start(bf16[70,768]{1,0:T(8,128)(2,1)S(1)} %get-tuple-element.17), channel_id=1, source_target_pairs={{0,64},{16,80},{32,96},{48,112},{64,128},{80,144},{96,160},{112,17... | collective-permute-start | bytes 322568 | tf_op jit(solution)/shard_map/ppermute | solution.py:81
  22.1 23.0 %collective-permute-start.2 = (bf16[70,768]{1,0:T(8,128)(2,1)S(1)}, bf16[70,768]{1,0:T(8,128)(2,1)S(1)}, u32[]{:S(2)}, u32[]{:S(2)}) collective-permute-start(bf16[70,768]{1,0:T(8,128)(2,1)S(1)} %get-tuple-element.17), channel_id=1, source_target_pairs={{0,192},{16,208},{32,224},{48,240},{64,0},{80,16},{96,32},{112,48}... | collective-permute-start | bytes 322568 | tf_op jit(solution)/shard_map/ppermute | solution.py:81
  45.0 7.3 %collective-permute-start.3 = (bf16[70,768]{1,0:T(8,128)(2,1)S(1)}, bf16[70,768]{1,0:T(8,128)(2,1)S(1)}, u32[]{:S(2)}, u32[]{:S(2)}) collective-permute-start(bf16[70,768]{1,0:T(8,128)(2,1)S(1)} %get-tuple-element.16), channel_id=1, source_target_pairs={{0,128},{16,144},{32,160},{48,176},{64,192},{80,208},{96,224},{112... | collective-permute-start | bytes 322568 | tf_op jit(solution)/shard_map/ppermute | solution.py:81
  54.9 15.4 %all-to-all-start.1 = ((f32[16,2,1024]{2,1,0:T(2,128)}), f32[16,2,1024]{2,1,0:T(2,128)S(1)}, u32[]{:S(2)}, u32[]{:S(2)}) async-start(f32[16,2,1024]{2,1,0:T(2,128)} %bitcast.27), calls=%async_computation.1 | async-start | bytes 262144 | tf_op jit(solution)/shard_map/all_to_all | solution.py:22
  70.8 13.3 %all-to-all-done.1 = f32[16,2,1024]{2,1,0:T(2,128)S(1)} async-done(((f32[16,2,1024]{2,1,0:T(2,128)}), f32[16,2,1024]{2,1,0:T(2,128)S(1)}, u32[]{:S(2)}, u32[]{:S(2)}) %all-to-all-start.1) | async-done | bytes 131104 | tf_op jit(solution)/shard_map/all_to_all | solution.py:22
  85.8 3.7 %all-to-all-start = ((bf16[4,4,70,768]{3,1,2,0:T(4,128)(2,1)}), bf16[4,4,70,768]{3,1,2,0:T(4,128)(2,1)S(1)}, u32[]{:S(2)}, u32[]{:S(2)}) async-start(bf16[4,4,70,768]{3,1,2,0:T(4,128)(2,1)} %broadcast_in_dim.32), calls=%async_computation | async-start | bytes 3440640 | tf_op jit(solution)/shard_map/all_to_all | solution.py:22
  93.2 3.6 %collective-permute-start.6 = (f32[64,512]{1,0:T(8,128)S(1)}, f32[64,512]{1,0:T(8,128)S(1)}, u32[]{:S(2)}, u32[]{:S(2)}) collective-permute-start(f32[64,512]{1,0:T(8,128)S(1)} %get-tuple-element.6), channel_id=1, source_target_pairs={{0,2},{2,4},{4,6},{6,8},{8,10},{10,12},{12,14},{14,0},{1,3},{3,5},... | collective-permute-start | bytes 393224 | tf_op jit(solution)/shard_map/ppermute | solution.py:81
  96.7 4.1 %collective-permute-start.7 = (f32[64,512]{1,0:T(8,128)S(1)}, f32[64,512]{1,0:T(8,128)S(1)}, u32[]{:S(2)}, u32[]{:S(2)}) collective-permute-start(f32[64,512]{1,0:T(8,128)S(1)} %get-tuple-element.6), channel_id=1, source_target_pairs={{0,14},{2,0},{4,2},{6,4},{8,6},{10,8},{12,10},{14,12},{1,15},{3,1}... | collective-permute-start | bytes 393224 | tf_op jit(solution)/shard_map/ppermute | solution.py:81
  104.7 5.2 %collective-permute-start.9 = (f32[64,512]{1,0:T(8,128)S(1)}, f32[64,512]{1,0:T(8,128)S(1)}, u32[]{:S(2)}, u32[]{:S(2)}) collective-permute-start(f32[64,512]{1,0:T(8,128)S(1)} %collective-permute-done.7), channel_id=1, source_target_pairs={{0,14},{2,0},{4,2},{6,4},{8,6},{10,8},{12,10},{14,12},{1,15},{3,1}... | collective-permute-start | bytes 393224 | tf_op jit(solution)/shard_map/ppermute | solution.py:81
  112.8 5.2 %collective-permute-start.11 = (f32[64,512]{1,0:T(8,128)S(1)}, f32[64,512]{1,0:T(8,128)S(1)}, u32[]{:S(2)}, u32[]{:S(2)}) collective-permute-start(f32[64,512]{1,0:T(8,128)S(1)} %collective-permute-done.9), channel_id=1, source_target_pairs={{0,14},{2,0},{4,2},{6,4},{8,6},{10,8},{12,10},{14,12},{1,15},{3,1}... | collective-permute-start | bytes 393224 | tf_op jit(solution)/shard_map/ppermute | solution.py:81
  120.9 6.1 %collective-permute-done.12 = f32[64,512]{1,0:T(8,128)S(1)} collective-permute-done((f32[64,512]{1,0:T(8,128)S(1)}, f32[64,512]{1,0:T(8,128)S(1)}, u32[]{:S(2)}, u32[]{:S(2)}) %collective-permute-start.12) | collective-permute-done | bytes 131104 | tf_op jit(solution)/shard_map/ppermute | solution.py:81
  127.0 2.0 collective-permute-start.13
  129.0 3.5 %collective-permute-start = (bf16[3,384,48]{1,2,0:T(8,128)(2,1)S(1)}, bf16[3,384,48]{1,2,0:T(8,128)(2,1)}, u32[]{:S(2)}, u32[]{:S(2)}) collective-permute-start(bf16[3,384,48]{1,2,0:T(8,128)(2,1)S(1)} %dynamic-slice_bitcast_fusion), channel_id=1, source_target_pairs={{0,64},{16,80},{32,96},{48,112},{64,0},{80,16},{96,32},{112,48},{1... | collective-permute-start | bytes 331784 | tf_op jit(solution)/shard_map/ppermute | solution.py:86
  133.2 14.3 %collective-permute-done = bf16[3,384,48]{1,2,0:T(8,128)(2,1)} collective-permute-done((bf16[3,384,48]{1,2,0:T(8,128)(2,1)S(1)}, bf16[3,384,48]{1,2,0:T(8,128)(2,1)}, u32[]{:S(2)}, u32[]{:S(2)}) %collective-permute-start) | collective-permute-done | bytes 110624 | tf_op jit(solution)/shard_map/ppermute | solution.py:86
  152.1 2.7 %pad_maximum_fusion = f32[2,512,512]{2,1,0:T(8,128)} fusion(f32[1,512,512]{2,1,0:T(8,128)} %bitcast.32, f32[1,512,512]{2,1,0:T(8,128)S(1)} %bitcast.77), kind=kLoop, calls=%fused_computation.5 | loop fusion | flops 524288 | bytes 4194304 | tf_op jit(solution)/shard_map/stack | solution.py:126
  156.9 4.0 %collective-permute-start.14 = (bf16[96,768]{1,0:T(8,128)(2,1)S(1)}, bf16[96,768]{1,0:T(8,128)(2,1)}, u32[]{:S(2)}, u32[]{:S(2)}) collective-permute-start(bf16[96,768]{1,0:T(8,128)(2,1)S(1)} %reshape.211), channel_id=1, source_target_pairs={{0,2},{2,4},{4,6},{6,8},{8,10},{10,12},{12,14},{14,0},{1,3},{3,5},... | collective-permute-start | bytes 442376 | tf_op jit(solution)/shard_map/ppermute | solution.py:81
  163.4 4.0 %fusion.41 = (f32[2,2,512]{2,1,0:T(2,128)S(1)}, f32[2,2,512,512]{3,2,1,0:T(8,128)}) fusion(f32[2,512,512]{2,1,0:T(8,128)S(1)} %copy-done.2, pred[512]{0:T(512)(128)(4,1)S(1)} %iota_compare_fusion.2, bf16[2,2,512,48]{2,3,0,1:T(8,128)(2,1)S(1)} %get-tuple-element.8, bf16[2,2,512,48]{2,3,0,1:T(8,128)(2,1)S(1)} %get-tuple-element.9), kind=kOutput, calls=%fused_computation.100 | convolution fusion | flops 106955264 | bytes 6693376 | tf_op jit(solution)/shard_map/sub | solution.py:168
  167.4 2.7 %fusion.10 = bf16[2,512,2,48]{1,3,2,0:T(8,128)(2,1)S(1)} fusion(f32[2,2,512,512]{3,2,1,0:T(8,128)} %get-tuple-element.23, f32[2,2,512]{2,1,0:T(2,128)S(1)} %get-tuple-element.22, bf16[2,2,512,48]{2,3,0,1:T(8,128)(2,1)S(1)} %get-tuple-element.7), kind=kOutput, calls=%fused_computation.17 | convolution fusion | flops 102858752 | bytes 4595712 | tf_op jit(solution)/shard_map/shji,shjd->sihd/dot_general | solution.py:171
  171.5 5.8 %all-to-all-start.2 = ((bf16[16,2,32,96]{3,2,1,0:T(8,128)(2,1)}), bf16[16,2,32,96]{3,2,1,0:T(8,128)(2,1)S(1)}, u32[]{:S(2)}, u32[]{:S(2)}) async-start(bf16[16,2,32,96]{3,2,1,0:T(8,128)(2,1)} %copy.43), calls=%async_computation.2 | async-start | bytes 524288 | tf_op jit(solution)/shard_map/all_to_all | solution.py:22
  177.5 3.2 %collective-permute-start.17 = (bf16[96,768]{1,0:T(8,128)(2,1)}, bf16[96,768]{1,0:T(8,128)(2,1)S(1)}, u32[]{:S(2)}, u32[]{:S(2)}) collective-permute-start(bf16[96,768]{1,0:T(8,128)(2,1)} %collective-permute-done.15), channel_id=1, source_target_pairs={{0,14},{2,0},{4,2},{6,4},{8,6},{10,8},{12,10},{14,12},{1,15},{3,1}... | collective-permute-start | bytes 442376 | tf_op jit(solution)/shard_map/ppermute | solution.py:81
  180.7 2.7 %collective-permute-start.16 = (bf16[96,768]{1,0:T(8,128)(2,1)}, bf16[96,768]{1,0:T(8,128)(2,1)S(1)}, u32[]{:S(2)}, u32[]{:S(2)}) collective-permute-start(bf16[96,768]{1,0:T(8,128)(2,1)} %collective-permute-done.14), channel_id=1, source_target_pairs={{0,2},{2,4},{4,6},{6,8},{8,10},{10,12},{12,14},{14,0},{1,3},{3,5},... | collective-permute-start | bytes 442376 | tf_op jit(solution)/shard_map/ppermute | solution.py:81
  185.3 4.4 %collective-permute-start.19 = (bf16[96,768]{1,0:T(8,128)(2,1)S(1)}, bf16[96,768]{1,0:T(8,128)(2,1)S(1)}, u32[]{:S(2)}, u32[]{:S(2)}) collective-permute-start(bf16[96,768]{1,0:T(8,128)(2,1)S(1)} %collective-permute-done.17), channel_id=1, source_target_pairs={{0,14},{2,0},{4,2},{6,4},{8,6},{10,8},{12,10},{14,12},{1,15},{3,1}... | collective-permute-start | bytes 442376 | tf_op jit(solution)/shard_map/ppermute | solution.py:81
  191.7 6.3 %collective-permute-done.18 = bf16[96,768]{1,0:T(8,128)(2,1)S(1)} collective-permute-done((bf16[96,768]{1,0:T(8,128)(2,1)S(1)}, bf16[96,768]{1,0:T(8,128)(2,1)S(1)}, u32[]{:S(2)}, u32[]{:S(2)}) %collective-permute-start.18) | collective-permute-done | bytes 147488 | tf_op jit(solution)/shard_map/ppermute | solution.py:81
  200.0 6.3 %collective-permute-done.20 = bf16[96,768]{1,0:T(8,128)(2,1)S(1)} collective-permute-done((bf16[96,768]{1,0:T(8,128)(2,1)S(1)}, bf16[96,768]{1,0:T(8,128)(2,1)S(1)}, u32[]{:S(2)}, u32[]{:S(2)}) %collective-permute-start.20) | collective-permute-done | bytes 147488 | tf_op jit(solution)/shard_map/ppermute | solution.py:81
  (123 shorter events, 40.6 us)
Async XLA Ops:
  4.2 66.2 %collective-permute-start.4 = (bf16[70,768]{1,0:T(8,128)(2,1)S(1)}, bf16[70,768]{1,0:T(8,128)(2,1)S(1)}, u32[]{:S(2)}, u32[]{:S(2)}) collective-permute-start(bf16[70,768]{1,0:T(8,128)(2,1)S(1)} %get-tuple-element.17), channel_id=1, source_target_pairs={{0,64},{16,80},{32,96},{48,112},{64,128},{80,144},{96,160},{112,17... | collective-permute-start | bytes 322568 | tf_op jit(solution)/shard_map/ppermute | solution.py:81
  22.1 48.3 %collective-permute-start.2 = (bf16[70,768]{1,0:T(8,128)(2,1)S(1)}, bf16[70,768]{1,0:T(8,128)(2,1)S(1)}, u32[]{:S(2)}, u32[]{:S(2)}) collective-permute-start(bf16[70,768]{1,0:T(8,128)(2,1)S(1)} %get-tuple-element.17), channel_id=1, source_target_pairs={{0,192},{16,208},{32,224},{48,240},{64,0},{80,16},{96,32},{112,48}... | collective-permute-start | bytes 322568 | tf_op jit(solution)/shard_map/ppermute | solution.py:81
  45.0 25.4 %collective-permute-start.3 = (bf16[70,768]{1,0:T(8,128)(2,1)S(1)}, bf16[70,768]{1,0:T(8,128)(2,1)S(1)}, u32[]{:S(2)}, u32[]{:S(2)}) collective-permute-start(bf16[70,768]{1,0:T(8,128)(2,1)S(1)} %get-tuple-element.16), channel_id=1, source_target_pairs={{0,128},{16,144},{32,160},{48,176},{64,192},{80,208},{96,224},{112... | collective-permute-start | bytes 322568 | tf_op jit(solution)/shard_map/ppermute | solution.py:81
  54.9 29.2 %all-to-all-start.1 = ((f32[16,2,1024]{2,1,0:T(2,128)}), f32[16,2,1024]{2,1,0:T(2,128)S(1)}, u32[]{:S(2)}, u32[]{:S(2)}) async-start(f32[16,2,1024]{2,1,0:T(2,128)} %bitcast.27), calls=%async_computation.1 | async-start | bytes 262144 | tf_op jit(solution)/shard_map/all_to_all | solution.py:22
  85.8 69.1 %all-to-all-start = ((bf16[4,4,70,768]{3,1,2,0:T(4,128)(2,1)}), bf16[4,4,70,768]{3,1,2,0:T(4,128)(2,1)S(1)}, u32[]{:S(2)}, u32[]{:S(2)}) async-start(bf16[4,4,70,768]{3,1,2,0:T(4,128)(2,1)} %broadcast_in_dim.32), calls=%async_computation | async-start | bytes 3440640 | tf_op jit(solution)/shard_map/all_to_all | solution.py:22
  89.8 3.2 %collective-permute-start.5 = (f32[32,512]{1,0:T(8,128)S(1)}, f32[32,512]{1,0:T(8,128)S(1)}, u32[]{:S(2)}, u32[]{:S(2)}) collective-permute-start(f32[32,512]{1,0:T(8,128)S(1)} %copy.38), channel_id=1, source_target_pairs={{0,1},{1,0},{2,3},{3,2},{4,5},{5,4},{6,7},{7,6},{8,9},{9,8},{10,11... | collective-permute-start | bytes 196616 | tf_op jit(solution)/shard_map/ppermute | solution.py:104
  93.2 9.6 %collective-permute-start.6 = (f32[64,512]{1,0:T(8,128)S(1)}, f32[64,512]{1,0:T(8,128)S(1)}, u32[]{:S(2)}, u32[]{:S(2)}) collective-permute-start(f32[64,512]{1,0:T(8,128)S(1)} %get-tuple-element.6), channel_id=1, source_target_pairs={{0,2},{2,4},{4,6},{6,8},{8,10},{10,12},{12,14},{14,0},{1,3},{3,5},... | collective-permute-start | bytes 393224 | tf_op jit(solution)/shard_map/ppermute | solution.py:81
  96.7 7.9 %collective-permute-start.7 = (f32[64,512]{1,0:T(8,128)S(1)}, f32[64,512]{1,0:T(8,128)S(1)}, u32[]{:S(2)}, u32[]{:S(2)}) collective-permute-start(f32[64,512]{1,0:T(8,128)S(1)} %get-tuple-element.6), channel_id=1, source_target_pairs={{0,14},{2,0},{4,2},{6,4},{8,6},{10,8},{12,10},{14,12},{1,15},{3,1}... | collective-permute-start | bytes 393224 | tf_op jit(solution)/shard_map/ppermute | solution.py:81
  102.7 8.1 %collective-permute-start.8 = (f32[64,512]{1,0:T(8,128)S(1)}, f32[64,512]{1,0:T(8,128)S(1)}, u32[]{:S(2)}, u32[]{:S(2)}) collective-permute-start(f32[64,512]{1,0:T(8,128)S(1)} %collective-permute-done.6), channel_id=1, source_target_pairs={{0,2},{2,4},{4,6},{6,8},{8,10},{10,12},{12,14},{14,0},{1,3},{3,5},... | collective-permute-start | bytes 393224 | tf_op jit(solution)/shard_map/ppermute | solution.py:81
  104.7 8.1 %collective-permute-start.9 = (f32[64,512]{1,0:T(8,128)S(1)}, f32[64,512]{1,0:T(8,128)S(1)}, u32[]{:S(2)}, u32[]{:S(2)}) collective-permute-start(f32[64,512]{1,0:T(8,128)S(1)} %collective-permute-done.7), channel_id=1, source_target_pairs={{0,14},{2,0},{4,2},{6,4},{8,6},{10,8},{12,10},{14,12},{1,15},{3,1}... | collective-permute-start | bytes 393224 | tf_op jit(solution)/shard_map/ppermute | solution.py:81
  110.8 8.1 %collective-permute-start.10 = (f32[64,512]{1,0:T(8,128)S(1)}, f32[64,512]{1,0:T(8,128)S(1)}, u32[]{:S(2)}, u32[]{:S(2)}) collective-permute-start(f32[64,512]{1,0:T(8,128)S(1)} %collective-permute-done.8), channel_id=1, source_target_pairs={{0,2},{2,4},{4,6},{6,8},{8,10},{10,12},{12,14},{14,0},{1,3},{3,5},... | collective-permute-start | bytes 393224 | tf_op jit(solution)/shard_map/ppermute | solution.py:81
  112.8 8.1 %collective-permute-start.11 = (f32[64,512]{1,0:T(8,128)S(1)}, f32[64,512]{1,0:T(8,128)S(1)}, u32[]{:S(2)}, u32[]{:S(2)}) collective-permute-start(f32[64,512]{1,0:T(8,128)S(1)} %collective-permute-done.9), channel_id=1, source_target_pairs={{0,14},{2,0},{4,2},{6,4},{8,6},{10,8},{12,10},{14,12},{1,15},{3,1}... | collective-permute-start | bytes 393224 | tf_op jit(solution)/shard_map/ppermute | solution.py:81
  118.9 8.1 %collective-permute-start.12 = (f32[64,512]{1,0:T(8,128)S(1)}, f32[64,512]{1,0:T(8,128)S(1)}, u32[]{:S(2)}, u32[]{:S(2)}) collective-permute-start(f32[64,512]{1,0:T(8,128)S(1)} %collective-permute-done.10), channel_id=1, source_target_pairs={{0,2},{2,4},{4,6},{6,8},{8,10},{10,12},{12,14},{14,0},{1,3},{3,5},... | collective-permute-start | bytes 393224 | tf_op jit(solution)/shard_map/ppermute | solution.py:81
  127.0 25.0 %collective-permute-start.13 = (f32[512,512]{1,0:T(8,128)S(1)}, f32[512,512]{1,0:T(8,128)}, u32[]{:S(2)}, u32[]{:S(2)}) collective-permute-start(f32[512,512]{1,0:T(8,128)S(1)} %constant_dynamic-update-slice_fusion.8), channel_id=1, source_target_pairs={{0,1},{1,0},{2,3},{3,2},{4,5},{5,4},{6,7},{7,6},{8,9},{9,8},{10,11... | collective-permute-start | bytes 3145736 | tf_op jit(solution)/shard_map/ppermute | solution.py:125
  129.0 18.5 %collective-permute-start = (bf16[3,384,48]{1,2,0:T(8,128)(2,1)S(1)}, bf16[3,384,48]{1,2,0:T(8,128)(2,1)}, u32[]{:S(2)}, u32[]{:S(2)}) collective-permute-start(bf16[3,384,48]{1,2,0:T(8,128)(2,1)S(1)} %dynamic-slice_bitcast_fusion), channel_id=1, source_target_pairs={{0,64},{16,80},{32,96},{48,112},{64,0},{80,16},{96,32},{112,48},{1... | collective-permute-start | bytes 331784 | tf_op jit(solution)/shard_map/ppermute | solution.py:86
  147.5 3.4 %collective-permute-start.1 = (bf16[3,384,48]{1,2,0:T(8,128)(2,1)}, bf16[3,384,48]{1,2,0:T(8,128)(2,1)S(1)}, u32[]{:S(2)}, u32[]{:S(2)}) collective-permute-start(bf16[3,384,48]{1,2,0:T(8,128)(2,1)} %collective-permute-done), channel_id=1, source_target_pairs={{0,1},{1,0},{2,3},{3,2},{4,5},{5,4},{6,7},{7,6},{8,9},{9,8},{10,11... | collective-permute-start | bytes 331784 | tf_op jit(solution)/shard_map/ppermute | solution.py:87
  155.0 22.5 %collective-permute-start.15 = (bf16[96,768]{1,0:T(8,128)(2,1)S(1)}, bf16[96,768]{1,0:T(8,128)(2,1)}, u32[]{:S(2)}, u32[]{:S(2)}) collective-permute-start(bf16[96,768]{1,0:T(8,128)(2,1)S(1)} %reshape.211), channel_id=1, source_target_pairs={{0,14},{2,0},{4,2},{6,4},{8,6},{10,8},{12,10},{14,12},{1,15},{3,1}... | collective-permute-start | bytes 442376 | tf_op jit(solution)/shard_map/ppermute | solution.py:81
  156.9 23.7 %collective-permute-start.14 = (bf16[96,768]{1,0:T(8,128)(2,1)S(1)}, bf16[96,768]{1,0:T(8,128)(2,1)}, u32[]{:S(2)}, u32[]{:S(2)}) collective-permute-start(bf16[96,768]{1,0:T(8,128)(2,1)S(1)} %reshape.211), channel_id=1, source_target_pairs={{0,2},{2,4},{4,6},{6,8},{8,10},{10,12},{12,14},{14,0},{1,3},{3,5},... | collective-permute-start | bytes 442376 | tf_op jit(solution)/shard_map/ppermute | solution.py:81
  171.5 35.8 %all-to-all-start.2 = ((bf16[16,2,32,96]{3,2,1,0:T(8,128)(2,1)}), bf16[16,2,32,96]{3,2,1,0:T(8,128)(2,1)S(1)}, u32[]{:S(2)}, u32[]{:S(2)}) async-start(bf16[16,2,32,96]{3,2,1,0:T(8,128)(2,1)} %copy.43), calls=%async_computation.2 | async-start | bytes 524288 | tf_op jit(solution)/shard_map/all_to_all | solution.py:22
  177.5 7.8 %collective-permute-start.17 = (bf16[96,768]{1,0:T(8,128)(2,1)}, bf16[96,768]{1,0:T(8,128)(2,1)S(1)}, u32[]{:S(2)}, u32[]{:S(2)}) collective-permute-start(bf16[96,768]{1,0:T(8,128)(2,1)} %collective-permute-done.15), channel_id=1, source_target_pairs={{0,14},{2,0},{4,2},{6,4},{8,6},{10,8},{12,10},{14,12},{1,15},{3,1}... | collective-permute-start | bytes 442376 | tf_op jit(solution)/shard_map/ppermute | solution.py:81
  180.7 9.0 %collective-permute-start.16 = (bf16[96,768]{1,0:T(8,128)(2,1)}, bf16[96,768]{1,0:T(8,128)(2,1)S(1)}, u32[]{:S(2)}, u32[]{:S(2)}) collective-permute-start(bf16[96,768]{1,0:T(8,128)(2,1)} %collective-permute-done.14), channel_id=1, source_target_pairs={{0,2},{2,4},{4,6},{6,8},{8,10},{10,12},{12,14},{14,0},{1,3},{3,5},... | collective-permute-start | bytes 442376 | tf_op jit(solution)/shard_map/ppermute | solution.py:81
  185.3 14.6 %collective-permute-start.19 = (bf16[96,768]{1,0:T(8,128)(2,1)S(1)}, bf16[96,768]{1,0:T(8,128)(2,1)S(1)}, u32[]{:S(2)}, u32[]{:S(2)}) collective-permute-start(bf16[96,768]{1,0:T(8,128)(2,1)S(1)} %collective-permute-done.17), channel_id=1, source_target_pairs={{0,14},{2,0},{4,2},{6,4},{8,6},{10,8},{12,10},{14,12},{1,15},{3,1}... | collective-permute-start | bytes 442376 | tf_op jit(solution)/shard_map/ppermute | solution.py:81
  189.7 8.3 %collective-permute-start.18 = (bf16[96,768]{1,0:T(8,128)(2,1)S(1)}, bf16[96,768]{1,0:T(8,128)(2,1)S(1)}, u32[]{:S(2)}, u32[]{:S(2)}) collective-permute-start(bf16[96,768]{1,0:T(8,128)(2,1)S(1)} %collective-permute-done.16), channel_id=1, source_target_pairs={{0,2},{2,4},{4,6},{6,8},{8,10},{10,12},{12,14},{14,0},{1,3},{3,5},... | collective-permute-start | bytes 442376 | tf_op jit(solution)/shard_map/ppermute | solution.py:81
  198.0 8.3 %collective-permute-start.20 = (bf16[96,768]{1,0:T(8,128)(2,1)S(1)}, bf16[96,768]{1,0:T(8,128)(2,1)S(1)}, u32[]{:S(2)}, u32[]{:S(2)}) collective-permute-start(bf16[96,768]{1,0:T(8,128)(2,1)S(1)} %collective-permute-done.18), channel_id=1, source_target_pairs={{0,2},{2,4},{4,6},{6,8},{8,10},{10,12},{12,14},{14,0},{1,3},{3,5},... | collective-permute-start | bytes 442376 | tf_op jit(solution)/shard_map/ppermute | solution.py:81
  (9 other events, 251.2 us)

commit v3 on v2

--- a/solution.py
+++ b/solution.py
@@ -1,9 +1,13 @@
+import functools
 import math
 
 import jax
 import jax.numpy as jnp
 from jax import lax
+from jax.experimental import pallas as pl
+from jax.experimental.pallas import tpu as pltpu
 from jax.sharding import PartitionSpec as P
+
 
 HEAD_DIM = 48
 QUAD = 4
@@ -47,6 +51,63 @@
         bias_weight, normed, (((0,), (1,)), ((), ())), preferred_element_type=jnp.float32
     )
     return projected
+
+
+def attend_kernel(info_ref, blocks_ref, w_ref, bias_a_ref, bias_b_ref, out_ref, *, samples, scale):
+    neighbours, quads, block_rows, _ = blocks_ref.shape
+    token_rows = block_rows // samples
+    total = bias_a_ref.shape[0]
+    valid, quad, core = info_ref[0], info_ref[1], info_ref[2]
+    key_ok = lax.broadcasted_iota(jnp.int32, (total, 1), 0) < valid
+    dot = functools.partial(lax.dot_general, preferred_element_type=jnp.float32)
+    for u in range(samples):
+        x = jnp.concatenate(
+            [
+                blocks_ref[j, lax.rem(a - quad + quads, quads), pl.ds(u * token_rows, token_rows), :]
+                for a in range(quads)
+                for j in range(neighbours)
+            ]
+        )
+        projected = dot(w_ref[...], x, (((1,), (1,)), ((), ()))).astype(jnp.bfloat16)
+        outs = []
+        for h, bias_ref in enumerate((bias_a_ref, bias_b_ref)):
+            query, key, value = (
+                projected[(h * 3 + p) * HEAD_DIM : (h * 3 + p + 1) * HEAD_DIM] for p in range(3)
+            )
+            scores = dot(key, query, (((0,), (0,)), ((), ()))) * scale + bias_ref[...]
+            scores = jnp.where(key_ok, scores, -1e30)
+            row_max = jnp.max(scores, axis=0, keepdims=True)
+            weights = jnp.where(key_ok, jnp.exp(scores - row_max), 0.0)
+            inverse = 1.0 / jnp.sum(weights, axis=0, keepdims=True)
+            probs = (weights * inverse).astype(jnp.bfloat16)
+            outs.append(dot(value, probs, (((1,), (0,)), ((), ()))))
+        swapped = core == 1
+        low = jnp.where(swapped, outs[1], outs[0])
+        high = jnp.where(swapped, outs[0], outs[1])
+        both = jnp.concatenate([low, high]).T.astype(jnp.bfloat16)
+        for i in range(total // token_rows):
+            out_ref[i, u] = both[i * token_rows : (i + 1) * token_rows]
+
+
+def attend(info, blocks, w, bias_a, bias_b, samples):
+    _, _, block_rows, width = blocks.shape
+    total = bias_a.shape[0]
+    token_rows = block_rows // samples
+    vmem = pl.BlockSpec(memory_space=pltpu.VMEM)
+    flops = 2 * samples * total * (width * w.shape[0] + 4 * total * HEAD_DIM)
+    return pl.pallas_call(
+        functools.partial(attend_kernel, samples=samples, scale=1.0 / math.sqrt(HEAD_DIM)),
+        out_shape=jax.ShapeDtypeStruct(
+            (total // token_rows, samples, token_rows, 2 * HEAD_DIM), jnp.bfloat16
+        ),
+        in_specs=[pl.BlockSpec(memory_space=pltpu.SMEM), vmem, vmem, vmem, vmem],
+        out_specs=vmem,
+        compiler_params=pltpu.CompilerParams(vmem_limit_bytes=48 * 1024 * 1024),
+        cost_estimate=pl.CostEstimate(
+            flops=flops, bytes_accessed=6 * 1024 * 1024, transcendentals=samples * 2 * total * total
+        ),
+        name="attend",
+    )(info, blocks, w, bias_a, bias_b)
 
 
 def per_device(
@@ -73,8 +134,6 @@
     side = (z // QUAD) % 2
     core = lax.axis_index("samp")
     swap = [(0, 1), (1, 0)]
-    keymask = jnp.arange(total, dtype=jnp.int32) < valid_len[0]
-    score_scale = 1.0 / math.sqrt(HEAD_DIM)
 
     def shifted(value, axis, by):
         size = lax.axis_size(axis)
@@ -91,21 +150,31 @@
     own_first = side == core
     w_a = jnp.where(own_first, own_w, other_w)
     w_b = jnp.where(own_first, other_w, own_w)
-    w_pair = jnp.stack([w_a, w_b])
+    w_pair = jnp.stack([w_a, w_b]).transpose(0, 1, 3, 2).reshape(-1, width)
 
     paired = bias_weight.reshape(-1, heads // 8, 2, QUAD).transpose(0, 1, 3, 2).reshape(-1, heads)
     tile = bias_tile_of(pair_repr, asym_id, rel_embed, pair_gain, paired)
+    tile, tokens_in, part = lax.optimization_barrier((tile, tokens, part))
+    normed = normalize(tokens_in.astype(jnp.float32), token_gain[0]).astype(jnp.bfloat16)
+    half_samples = sample_count // 2
+    half_rows = half_samples * token_rows
+    halves = normed.reshape(2, half_rows, width)
+    col = lax.axis_index("col")
+    depth = out_weight.shape[1]
+    slice_rows = depth // cols
+    piece = lax.dynamic_slice_in_dim(out_weight[0], col * slice_rows, slice_rows, 0)
+    same = jnp.concatenate([jnp.where(side == 0, halves[0], halves[1]), piece])
+    cross = jnp.concatenate([jnp.where(side == 0, halves[1], halves[0]), piece])
     tile = tile.reshape(heads // 8, 1, QUAD, 2, tile_rows * tile_cols)
     tile = jnp.broadcast_to(tile, (heads // 8, 2, QUAD, 2, tile_rows * tile_cols))
     by_row = exchange(tile.reshape(rows, 2, tile_rows * tile_cols), "row")
+    by_row, _, _ = lax.optimization_barrier((by_row, same, cross))
     by_key = by_row.reshape(rows, 2, tile_rows, tile_cols).transpose(1, 3, 0, 2)
     by_key = by_key.reshape(2, tile_cols, total)
-    keep = jnp.where(core == 0, by_key[0], by_key[1])
-    got = lax.ppermute(jnp.where(core == 0, by_key[1], by_key[0]), "samp", swap)
-    chip_keys = jnp.where(
-        core == 0, jnp.concatenate([keep, got]), jnp.concatenate([got, keep])
-    )
-    col = lax.axis_index("col")
+    fanned = jnp.broadcast_to(by_key[None], (cols, *by_key.shape))
+    bias_a = exchange(fanned.reshape(2 * cols, tile_cols, total), ("col", "samp"))
+    bias_a = bias_a.reshape(total, total)
+    bias_b = lax.ppermute(bias_a, "samp", swap)
 
     def all_cols(block):
         size = block.shape[0]
@@ -121,60 +190,34 @@
                 whole = lax.dynamic_update_slice(whole, down, ((col + step) % cols * size, *start))
         return whole
 
-    bias_a = all_cols(chip_keys)
-    bias_b = lax.ppermute(bias_a, "samp", swap)
-    biases = jnp.stack([bias_a, bias_b])
-
-    normed = normalize(tokens.astype(jnp.float32), token_gain[0]).astype(jnp.bfloat16)
-    half_rows = sample_count // 2 * token_rows
-    halves = normed.reshape(2, half_rows, width)
-    depth = out_weight.shape[1]
-    slice_rows = depth // cols
-    piece = lax.dynamic_slice_in_dim(out_weight[0], col * slice_rows, slice_rows, 0)
-    same = jnp.concatenate([jnp.where(side == 0, halves[0], halves[1]), piece])
-    cross = jnp.concatenate([jnp.where(side == 0, halves[1], halves[0]), piece])
-    around = jnp.stack(
-        [
-            same,
-            shifted(cross, "row", -QUAD),
-            shifted(same, "row", 2 * QUAD),
-            shifted(cross, "row", QUAD),
-        ]
-    )
-    around = lax.dynamic_slice_in_dim(
-        jnp.concatenate([around, around]), (quads - z // QUAD) % quads, quads, 0
-    )
-    gathered = jnp.broadcast_to(around[None], (QUAD, *around.shape))
-    gathered = exchange(gathered, "row", adjacent)
-    pieces = gathered[:, :, half_rows:].transpose(1, 0, 2, 3).reshape(-1, width)
-    w_out = all_cols(pieces).reshape(cols, rows // 8, 2, QUAD, slice_rows, width)
-    w_out = w_out.transpose(1, 3, 2, 0, 4, 5).reshape(width, width)
-    gathered = gathered[:, :, :half_rows].reshape(
-        QUAD, quads, sample_count // 2, token_rows, width
-    )
-    gathered = gathered.transpose(2, 1, 0, 3, 4).reshape(sample_count // 2, total, width)
-
-    projected = jnp.einsum(
-        "snc,hpcw->pshnw", gathered, w_pair, preferred_element_type=jnp.float32
-    ).astype(jnp.bfloat16)
-    query, key, value = projected[0], projected[1], projected[2]
-    scores = (
-        jnp.einsum("shjd,shid->shji", key, query, preferred_element_type=jnp.float32) * score_scale
-        + biases[None]
-    )
-    mask = keymask[None, None, :, None]
-    scores = jnp.where(mask, scores, -1e30)
-    row_max = jnp.max(scores, axis=2, keepdims=True)
-    weights = jnp.where(mask, jnp.exp(scores - row_max), 0.0)
-    row_total = jnp.sum(weights, axis=2, keepdims=True)
-    probs = (weights / row_total).astype(jnp.bfloat16)
-    attended = jnp.einsum(
-        "shji,shjd->sihd", probs, value, preferred_element_type=jnp.float32
-    ).astype(jnp.bfloat16)
-    attended = jnp.where(core == 0, attended, attended[:, :, ::-1])
-
-    back = attended.reshape(sample_count // 2, rows, token_rows, 2 * HEAD_DIM)
-    back = exchange(back.transpose(1, 0, 2, 3), "row")
+    opposite = shifted(same, "row", 2 * QUAD)
+    before = shifted(cross, "row", QUAD)
+    after = shifted(cross, "row", -QUAD)
+    around = [same, after, opposite, before]
+    blocks = jnp.stack([item[:half_rows] for item in around])
+    blocks = jnp.broadcast_to(blocks[None], (QUAD, *blocks.shape))
+    blocks = exchange(blocks, "row", adjacent)
+
+    mine = jnp.concatenate([item[half_rows:] for item in around])
+    turned = [mine]
+    for by in range(1, QUAD):
+        turns = [(i, i // QUAD * QUAD + (i - by) % QUAD) for i in range(rows)]
+        turned.append(lax.ppermute(mine, "row", turns))
+    turned = jnp.stack(turned).reshape(QUAD, quads, slice_rows, width)
+    turned = lax.dynamic_slice_in_dim(
+        jnp.concatenate([turned, turned]), (QUAD - z % QUAD) % QUAD, QUAD, 0
+    )
+    turned = lax.dynamic_slice_in_dim(
+        jnp.concatenate([turned, turned], 1), (quads - z // QUAD) % quads, quads, 1
+    )
+    w_out = all_cols(turned.reshape(-1, width)).reshape(
+        cols, QUAD, rows // 8, 2, slice_rows, width
+    )
+    w_out = w_out.transpose(2, 1, 3, 0, 4, 5).reshape(width, width)
+
+    info = jnp.stack([valid_len[0], z // QUAD, core]).astype(jnp.int32)
+    attended = attend(info, blocks, w_pair, bias_a, bias_b, half_samples)
+    back = exchange(attended, "row")
     back = back.reshape(rows // 8, 2, QUAD, sample_count // 2, token_rows, 2 * HEAD_DIM)
     back = back.transpose(1, 3, 4, 0, 2, 5).reshape(sample_count * token_rows, width)
     update = jnp.dot(back, w_out, preferred_element_type=jnp.float32)

time: 210 us -> 225 us (1.071)
  waiting for transfers between devices: 52.5 us -> 67.9 us
  local copies, waits for them, and re-layouts: 10.6 us -> 25.2 us
  starting transfers between devices: 126 us -> 117 us
  matrix products: 9.53 us -> 2.17 us
  Pallas kernels: 0 us -> 5.59 us
  other arithmetic: 8.24 us -> 3.56 us
    ppermute x17 -> x10, starting transfers between devices: 92 us -> 37.4 us  [shifted(): lax.ppermute(value, axis, [(i, (i + by) % size) for i in range(size)])]
    all_to_all x3 -> x4, starting transfers between devices: 24.9 us -> 62.5 us  [exchange(): lax.all_to_all(blocks, axis, split_axis=0, concat_axis=0, axis_index_grou...]
    ppermute x1 -> x3, waiting for transfers between devices: 1.12 us -> 14.3 us  [per_device(): turned.append(lax.ppermute(mine, 'row', turns))]
    ppermute x1 -> x3, starting transfers between devices: 1.95 us -> 10.7 us  [per_device(): turned.append(lax.ppermute(mine, 'row', turns))]
    pallas_call x0 -> x1, Pallas kernels: none -> 5.59 us  [attend(): pl.pallas_call(functools.partial(attend_kernel, samples=samples, scale=1....]
    sub x1 -> x0, matrix products: 4.01 us -> none  [per_device(): weights = jnp.where(mask, jnp.exp(scores - row_max), 0.0)]
    unnamed x24 -> x27, local copies, waits for them, and re-layouts: 1.24 us -> 5 us
    ppermute x17 -> x10, waiting for transfers between devices: 22.2 us -> 25.8 us  [shifted(): lax.ppermute(value, axis, [(i, (i + by) % size) for i in range(size)])]
  transfers between devices with their start and end apart: 24 -> 20, of which waited for: 10 -> 7; matrix products, arithmetic and copies ran while one was open for 10% -> 10% of each run, Pallas kernels for 0% -> 3%
where the time goes in v3:
time: 225 us; the launch traced here: 223 us
  starting transfers between devices  117 us (52%)
  waiting for transfers between devices  67.9 us (30%)
  local copies, waits for them, and re-layouts  25.2 us (11%)
  Pallas kernels  5.59 us (2%)
  other arithmetic  3.56 us (2%)
    all_to_all x4, starting transfers between devices, exchange(): lax.all_to_all(blocks, axis, split_axis=0, concat_axis=0, axis_index_grou...  62.5 us
    ppermute x10, starting transfers between devices, shifted(): lax.ppermute(value, axis, [(i, (i + by) % size) for i in range(size)])  37.4 us
    ppermute x10, waiting for transfers between devices, shifted(): lax.ppermute(value, axis, [(i, (i + by) % size) for i in range(size)])  25.8 us
    ppermute x3, waiting for transfers between devices, per_device(): turned.append(lax.ppermute(mine, 'row', turns))  14.3 us
    all_to_all x4, waiting for transfers between devices, exchange(): lax.all_to_all(blocks, axis, split_axis=0, concat_axis=0, axis_index_grou...  14 us
    ppermute x1, waiting for transfers between devices, per_device(): far = lax.ppermute(part, 'row', [(i, i ^ QUAD) for i in range(rows)])  13.8 us
    ppermute x3, starting transfers between devices, per_device(): turned.append(lax.ppermute(mine, 'row', turns))  10.7 us
    pallas_call x1, Pallas kernels, attend(): pl.pallas_call(functools.partial(attend_kernel, samples=samples, scale=1....  5.59 us
  transfers between devices with their start and end apart: 20, of which 7 were waited for; matrix products, arithmetic and copies ran while one was open for 10% of the time, Pallas kernels for 3%

profile of v3, /device:TPU:80, one launch (start us, length us, event | category | flops | bytes accessed | tf_op | source)
XLA Modules:
  0.0 223.3 jit_solution(1273437387505079380)
XLA Ops:
  4.3 43.7 %all-to-all-start.1 = ((f32[16,2,1024]{2,1,0:T(2,128)}), f32[16,2,1024]{2,1,0:T(2,128)S(1)}, u32[]{:S(2)}, u32[]{:S(2)}) async-start(f32[16,2,1024]{2,1,0:T(2,128)} %bitcast.19), calls=%async_computation.1 | async-start | bytes 262144 | tf_op jit(solution)/shard_map/all_to_all | solution.py:26
  48.6 14.0 %all-to-all-done.1 = f32[16,2,1024]{2,1,0:T(2,128)S(1)} async-done(((f32[16,2,1024]{2,1,0:T(2,128)}), f32[16,2,1024]{2,1,0:T(2,128)S(1)}, u32[]{:S(2)}, u32[]{:S(2)}) %all-to-all-start.1) | async-done | bytes 131104 | tf_op jit(solution)/shard_map/all_to_all | solution.py:26
  64.1 7.6 %all-to-all-start.2 = ((f32[16,32,512]{2,1,0:T(8,128)}), f32[16,32,512]{2,1,0:T(8,128)S(1)}, u32[]{:S(2)}, u32[]{:S(2)}) async-start(f32[16,32,512]{2,1,0:T(8,128)} %bitcast.22), calls=%async_computation.2 | async-start | bytes 2097152 | tf_op jit(solution)/shard_map/all_to_all | solution.py:26
  71.8 4.1 %collective-permute-start.2 = (bf16[70,768]{1,0:T(8,128)(2,1)S(1)}, bf16[70,768]{1,0:T(8,128)(2,1)S(1)}, u32[]{:S(2)}, u32[]{:S(2)}) collective-permute-start(bf16[70,768]{1,0:T(8,128)(2,1)S(1)} %get-tuple-element.16), channel_id=1, source_target_pairs={{0,64},{16,80},{32,96},{48,112},{64,128},{80,144},{96,160},{112,17... | collective-permute-start | bytes 322568 | tf_op jit(solution)/shard_map/ppermute | solution.py:140
  75.8 6.8 %collective-permute-start.1 = (bf16[70,768]{1,0:T(8,128)(2,1)S(1)}, bf16[70,768]{1,0:T(8,128)(2,1)S(1)}, u32[]{:S(2)}, u32[]{:S(2)}) collective-permute-start(bf16[70,768]{1,0:T(8,128)(2,1)S(1)} %get-tuple-element.15), channel_id=1, source_target_pairs={{0,128},{16,144},{32,160},{48,176},{64,192},{80,208},{96,224},{112... | collective-permute-start | bytes 322568 | tf_op jit(solution)/shard_map/ppermute | solution.py:140
  82.7 3.3 %collective-permute-start = (bf16[70,768]{1,0:T(8,128)(2,1)S(1)}, bf16[70,768]{1,0:T(8,128)(2,1)S(1)}, u32[]{:S(2)}, u32[]{:S(2)}) collective-permute-start(bf16[70,768]{1,0:T(8,128)(2,1)S(1)} %get-tuple-element.16), channel_id=1, source_target_pairs={{0,192},{16,208},{32,224},{48,240},{64,0},{80,16},{96,32},{112,48}... | collective-permute-start | bytes 322568 | tf_op jit(solution)/shard_map/ppermute | solution.py:140
  86.0 14.9 %collective-permute-done.1 = bf16[70,768]{1,0:T(8,128)(2,1)S(1)} collective-permute-done((bf16[70,768]{1,0:T(8,128)(2,1)S(1)}, bf16[70,768]{1,0:T(8,128)(2,1)S(1)}, u32[]{:S(2)}, u32[]{:S(2)}) %collective-permute-start.1) | collective-permute-done | bytes 107552 | tf_op jit(solution)/shard_map/ppermute | solution.py:140
  100.8 5.4 %collective-permute-done = bf16[70,768]{1,0:T(8,128)(2,1)S(1)} collective-permute-done((bf16[70,768]{1,0:T(8,128)(2,1)S(1)}, bf16[70,768]{1,0:T(8,128)(2,1)S(1)}, u32[]{:S(2)}, u32[]{:S(2)}) %collective-permute-start) | collective-permute-done | bytes 107552 | tf_op jit(solution)/shard_map/ppermute | solution.py:140
  108.3 3.8 %all-to-all-start = ((bf16[4,4,64,768]{3,2,1,0:T(8,128)(2,1)}), bf16[4,4,64,768]{3,2,1,0:T(8,128)(2,1)S(1)}, u32[]{:S(2)}, u32[]{:S(2)}) async-start(bf16[4,4,64,768]{3,2,1,0:T(8,128)(2,1)} %broadcast_in_dim.17), calls=%async_computation | async-start | bytes 3145728 | tf_op jit(solution)/shard_map/all_to_all | solution.py:26
  112.1 2.9 %collective-permute-start.3 = (bf16[3,384,48]{1,2,0:T(8,128)(2,1)S(1)}, bf16[3,384,48]{1,2,0:T(8,128)(2,1)}, u32[]{:S(2)}, u32[]{:S(2)}) collective-permute-start(bf16[3,384,48]{1,2,0:T(8,128)(2,1)S(1)} %dynamic-slice_bitcast_fusion), channel_id=1, source_target_pairs={{0,64},{16,80},{32,96},{48,112},{64,0},{80,16},{96,32},{112,48},{1... | collective-permute-start | bytes 331784 | tf_op jit(solution)/shard_map/ppermute | solution.py:145
  115.9 5.7 %collective-permute-start.6 = (bf16[24,768]{1,0:T(8,128)(2,1)S(1)}, bf16[24,768]{1,0:T(8,128)(2,1)S(1)}, u32[]{:S(2)}, u32[]{:S(2)}) collective-permute-start(bf16[24,768]{1,0:T(8,128)(2,1)S(1)} %pad_maximum_fusion.4), channel_id=1, source_target_pairs={{0,48},{16,0},{32,16},{48,32},{64,112},{80,64},{96,80},{112,96},{1... | collective-permute-start | bytes 110600 | tf_op jit(solution)/shard_map/ppermute | solution.py:205
  123.6 3.0 %collective-permute-start.8 = (bf16[24,768]{1,0:T(8,128)(2,1)S(1)}, bf16[24,768]{1,0:T(8,128)(2,1)S(1)}, u32[]{:S(2)}, u32[]{:S(2)}) collective-permute-start(bf16[24,768]{1,0:T(8,128)(2,1)S(1)} %pad_maximum_fusion.4), channel_id=1, source_target_pairs={{0,16},{16,32},{32,48},{48,0},{64,80},{80,96},{96,112},{112,64},{1... | collective-permute-start | bytes 110600 | tf_op jit(solution)/shard_map/ppermute | solution.py:205
  127.2 13.8 %collective-permute-done.3 = bf16[3,384,48]{1,2,0:T(8,128)(2,1)} collective-permute-done((bf16[3,384,48]{1,2,0:T(8,128)(2,1)S(1)}, bf16[3,384,48]{1,2,0:T(8,128)(2,1)}, u32[]{:S(2)}, u32[]{:S(2)}) %collective-permute-start.3) | collective-permute-done | bytes 110624 | tf_op jit(solution)/shard_map/ppermute | solution.py:145
  143.0 14.3 %collective-permute-done.7 = bf16[24,768]{1,0:T(8,128)(2,1)S(1)} collective-permute-done((bf16[24,768]{1,0:T(8,128)(2,1)S(1)}, bf16[24,768]{1,0:T(8,128)(2,1)S(1)}, u32[]{:S(2)}, u32[]{:S(2)}) %collective-permute-start.7) | collective-permute-done | bytes 36896 | tf_op jit(solution)/shard_map/ppermute | solution.py:205
  164.8 3.6 %collective-permute-start.9 = (bf16[96,768]{1,0:T(8,128)(2,1)S(1)}, bf16[96,768]{1,0:T(8,128)(2,1)}, u32[]{:S(2)}, u32[]{:S(2)}) collective-permute-start(bf16[96,768]{1,0:T(8,128)(2,1)S(1)} %reshape.224), channel_id=1, source_target_pairs={{0,2},{2,4},{4,6},{6,8},{8,10},{10,12},{12,14},{14,0},{1,3},{3,5},... | collective-permute-start | bytes 442376 | tf_op jit(solution)/shard_map/ppermute | solution.py:140
  168.4 3.5 %collective-permute-start.10 = (bf16[96,768]{1,0:T(8,128)(2,1)S(1)}, bf16[96,768]{1,0:T(8,128)(2,1)}, u32[]{:S(2)}, u32[]{:S(2)}) collective-permute-start(bf16[96,768]{1,0:T(8,128)(2,1)S(1)} %reshape.224), channel_id=1, source_target_pairs={{0,14},{2,0},{4,2},{6,4},{8,6},{10,8},{12,10},{14,12},{1,15},{3,1}... | collective-permute-start | bytes 442376 | tf_op jit(solution)/shard_map/ppermute | solution.py:140
  174.3 2.4 %collective-permute-start.11 = (bf16[96,768]{1,0:T(8,128)(2,1)}, bf16[96,768]{1,0:T(8,128)(2,1)}, u32[]{:S(2)}, u32[]{:S(2)}) collective-permute-start(bf16[96,768]{1,0:T(8,128)(2,1)} %collective-permute-done.9), channel_id=1, source_target_pairs={{0,2},{2,4},{4,6},{6,8},{8,10},{10,12},{12,14},{14,0},{1,3},{3,5},... | collective-permute-start | bytes 442376 | tf_op jit(solution)/shard_map/ppermute | solution.py:140
  176.6 4.8 %collective-permute-start.12 = (bf16[96,768]{1,0:T(8,128)(2,1)}, bf16[96,768]{1,0:T(8,128)(2,1)S(1)}, u32[]{:S(2)}, u32[]{:S(2)}) collective-permute-start(bf16[96,768]{1,0:T(8,128)(2,1)} %collective-permute-done.10), channel_id=1, source_target_pairs={{0,14},{2,0},{4,2},{6,4},{8,6},{10,8},{12,10},{14,12},{1,15},{3,1}... | collective-permute-start | bytes 442376 | tf_op jit(solution)/shard_map/ppermute | solution.py:140
  181.4 5.6 %attend.1 = bf16[16,2,32,96]{3,2,1,0:T(8,128)(2,1)} custom-call(s32[3]{0:T(128)S(1)} %pad_add_fusion.info_ref, bf16[4,4,64,768]{3,2,1,0:T(8,128)(2,1)S(1)} %all-to-all-done.blocks_ref, bf16[288,768]{1,0:T(8,128)(2,1)S(1)} %bitcast.47, f32[512,512]{1,0:T(8,128)S(1)} %bitcast.46, f32[512,512]{1,0:T(8,128)} %collective-permute-done.5.bias_b_ref), custom_call_target="tpu_custom_call" | custom-call | flops 654311424 | bytes 6291456 | tf_op jit(solution)/shard_map/attend/pallas_call | solution.py:98
  187.0 7.4 %all-to-all-start.3 = ((bf16[16,2,32,96]{3,2,1,0:T(8,128)(2,1)}), bf16[16,2,32,96]{3,2,1,0:T(8,128)(2,1)S(1)}, u32[]{:S(2)}, u32[]{:S(2)}) async-start(bf16[16,2,32,96]{3,2,1,0:T(8,128)(2,1)} %attend.1), calls=%async_computation.3 | async-start | bytes 524288 | tf_op jit(solution)/shard_map/all_to_all | solution.py:26
  199.5 5.2 %collective-permute-start.14 = (bf16[96,768]{1,0:T(8,128)(2,1)S(1)}, bf16[96,768]{1,0:T(8,128)(2,1)S(1)}, u32[]{:S(2)}, u32[]{:S(2)}) collective-permute-start(bf16[96,768]{1,0:T(8,128)(2,1)S(1)} %collective-permute-done.12), channel_id=1, source_target_pairs={{0,14},{2,0},{4,2},{6,4},{8,6},{10,8},{12,10},{14,12},{1,15},{3,1}... | collective-permute-start | bytes 442376 | tf_op jit(solution)/shard_map/ppermute | solution.py:140
  210.3 5.0 %collective-permute-done.15 = bf16[96,768]{1,0:T(8,128)(2,1)S(1)} collective-permute-done((bf16[96,768]{1,0:T(8,128)(2,1)S(1)}, bf16[96,768]{1,0:T(8,128)(2,1)S(1)}, u32[]{:S(2)}, u32[]{:S(2)}) %collective-permute-start.15) | collective-permute-done | bytes 147488 | tf_op jit(solution)/shard_map/ppermute | solution.py:140
  215.9 2.2 reshape.225
  219.5 2.3 %reshape.228 = bf16[768,768,1]{1,0,2:T(8,128)(2,1)S(1)} reshape(bf16[2,4,2,8,6,768]{5,4,3,2,1,0:T(8,128)(2,1)} %copy.24) | data formatting | bytes 2359296 | tf_op jit(solution)/shard_map/reshape | solution.py:216
  (109 shorter events, 36.8 us)
Async XLA Ops:
  0.0 48.6 %copy-start = (bf16[1,48,768]{2,1,0:T(8,128)(2,1)S(1)}, bf16[1,48,768]{2,1,0:T(8,128)(2,1)}, u32[]{:S(2)}) copy-start(bf16[1,48,768]{2,1,0:T(8,128)(2,1)} %param.19) | copy-start | bytes 221188
  3.2 44.8 %copy-start.2 = (bf16[4,32,768]{2,1,0:T(8,128)(2,1)S(1)}, bf16[4,32,768]{2,1,0:T(8,128)(2,1)}, u32[]{:S(2)}) copy-start(bf16[4,32,768]{2,1,0:T(8,128)(2,1)} %param.16) | copy-start | bytes 589828
  3.2 45.1 %copy-start.7 = (f32[1,768]{1,0:T(1,128)S(1)}, f32[1,768]{1,0:T(1,128)}, u32[]{:S(2)}) copy-start(f32[1,768]{1,0:T(1,128)} %param.17) | copy-start | bytes 9220
  4.3 58.3 %all-to-all-start.1 = ((f32[16,2,1024]{2,1,0:T(2,128)}), f32[16,2,1024]{2,1,0:T(2,128)S(1)}, u32[]{:S(2)}, u32[]{:S(2)}) async-start(f32[16,2,1024]{2,1,0:T(2,128)} %bitcast.19), calls=%async_computation.1 | async-start | bytes 262144 | tf_op jit(solution)/shard_map/all_to_all | solution.py:26
  64.1 42.8 %all-to-all-start.2 = ((f32[16,32,512]{2,1,0:T(8,128)}), f32[16,32,512]{2,1,0:T(8,128)S(1)}, u32[]{:S(2)}, u32[]{:S(2)}) async-start(f32[16,32,512]{2,1,0:T(8,128)} %bitcast.22), calls=%async_computation.2 | async-start | bytes 2097152 | tf_op jit(solution)/shard_map/all_to_all | solution.py:26
  71.8 14.2 %collective-permute-start.2 = (bf16[70,768]{1,0:T(8,128)(2,1)S(1)}, bf16[70,768]{1,0:T(8,128)(2,1)S(1)}, u32[]{:S(2)}, u32[]{:S(2)}) collective-permute-start(bf16[70,768]{1,0:T(8,128)(2,1)S(1)} %get-tuple-element.16), channel_id=1, source_target_pairs={{0,64},{16,80},{32,96},{48,112},{64,128},{80,144},{96,160},{112,17... | collective-permute-start | bytes 322568 | tf_op jit(solution)/shard_map/ppermute | solution.py:140
  75.8 25.0 %collective-permute-start.1 = (bf16[70,768]{1,0:T(8,128)(2,1)S(1)}, bf16[70,768]{1,0:T(8,128)(2,1)S(1)}, u32[]{:S(2)}, u32[]{:S(2)}) collective-permute-start(bf16[70,768]{1,0:T(8,128)(2,1)S(1)} %get-tuple-element.15), channel_id=1, source_target_pairs={{0,128},{16,144},{32,160},{48,176},{64,192},{80,208},{96,224},{112... | collective-permute-start | bytes 322568 | tf_op jit(solution)/shard_map/ppermute | solution.py:140
  82.7 23.6 %collective-permute-start = (bf16[70,768]{1,0:T(8,128)(2,1)S(1)}, bf16[70,768]{1,0:T(8,128)(2,1)S(1)}, u32[]{:S(2)}, u32[]{:S(2)}) collective-permute-start(bf16[70,768]{1,0:T(8,128)(2,1)S(1)} %get-tuple-element.16), channel_id=1, source_target_pairs={{0,192},{16,208},{32,224},{48,240},{64,0},{80,16},{96,32},{112,48}... | collective-permute-start | bytes 322568 | tf_op jit(solution)/shard_map/ppermute | solution.py:140
  108.3 73.2 %all-to-all-start = ((bf16[4,4,64,768]{3,2,1,0:T(8,128)(2,1)}), bf16[4,4,64,768]{3,2,1,0:T(8,128)(2,1)S(1)}, u32[]{:S(2)}, u32[]{:S(2)}) async-start(bf16[4,4,64,768]{3,2,1,0:T(8,128)(2,1)} %broadcast_in_dim.17), calls=%async_computation | async-start | bytes 3145728 | tf_op jit(solution)/shard_map/all_to_all | solution.py:26
  112.1 28.9 %collective-permute-start.3 = (bf16[3,384,48]{1,2,0:T(8,128)(2,1)S(1)}, bf16[3,384,48]{1,2,0:T(8,128)(2,1)}, u32[]{:S(2)}, u32[]{:S(2)}) collective-permute-start(bf16[3,384,48]{1,2,0:T(8,128)(2,1)S(1)} %dynamic-slice_bitcast_fusion), channel_id=1, source_target_pairs={{0,64},{16,80},{32,96},{48,112},{64,0},{80,16},{96,32},{112,48},{1... | collective-permute-start | bytes 331784 | tf_op jit(solution)/shard_map/ppermute | solution.py:145
  115.9 27.0 %collective-permute-start.6 = (bf16[24,768]{1,0:T(8,128)(2,1)S(1)}, bf16[24,768]{1,0:T(8,128)(2,1)S(1)}, u32[]{:S(2)}, u32[]{:S(2)}) collective-permute-start(bf16[24,768]{1,0:T(8,128)(2,1)S(1)} %pad_maximum_fusion.4), channel_id=1, source_target_pairs={{0,48},{16,0},{32,16},{48,32},{64,112},{80,64},{96,80},{112,96},{1... | collective-permute-start | bytes 110600 | tf_op jit(solution)/shard_map/ppermute | solution.py:205
  121.6 35.7 %collective-permute-start.7 = (bf16[24,768]{1,0:T(8,128)(2,1)S(1)}, bf16[24,768]{1,0:T(8,128)(2,1)S(1)}, u32[]{:S(2)}, u32[]{:S(2)}) collective-permute-start(bf16[24,768]{1,0:T(8,128)(2,1)S(1)} %pad_maximum_fusion.4), channel_id=1, source_target_pairs={{0,32},{16,48},{32,0},{48,16},{64,96},{80,112},{96,64},{112,80},{1... | collective-permute-start | bytes 110600 | tf_op jit(solution)/shard_map/ppermute | solution.py:205
  123.6 33.7 %collective-permute-start.8 = (bf16[24,768]{1,0:T(8,128)(2,1)S(1)}, bf16[24,768]{1,0:T(8,128)(2,1)S(1)}, u32[]{:S(2)}, u32[]{:S(2)}) collective-permute-start(bf16[24,768]{1,0:T(8,128)(2,1)S(1)} %pad_maximum_fusion.4), channel_id=1, source_target_pairs={{0,16},{16,32},{32,48},{48,0},{64,80},{80,96},{96,112},{112,64},{1... | collective-permute-start | bytes 110600 | tf_op jit(solution)/shard_map/ppermute | solution.py:205
  141.0 31.0 %collective-permute-start.4 = (bf16[3,384,48]{1,2,0:T(8,128)(2,1)}, bf16[3,384,48]{1,2,0:T(8,128)(2,1)}, u32[]{:S(2)}, u32[]{:S(2)}) collective-permute-start(bf16[3,384,48]{1,2,0:T(8,128)(2,1)} %collective-permute-done.3), channel_id=1, source_target_pairs={{0,1},{1,0},{2,3},{3,2},{4,5},{5,4},{6,7},{7,6},{8,9},{9,8},{10,11... | collective-permute-start | bytes 331784 | tf_op jit(solution)/shard_map/ppermute | solution.py:146
  159.8 21.6 %collective-permute-start.5 = (f32[512,512]{1,0:T(8,128)S(1)}, f32[512,512]{1,0:T(8,128)}, u32[]{:S(2)}, u32[]{:S(2)}) collective-permute-start(f32[512,512]{1,0:T(8,128)S(1)} %bitcast.45), channel_id=1, source_target_pairs={{0,1},{1,0},{2,3},{3,2},{4,5},{5,4},{6,7},{7,6},{8,9},{9,8},{10,11... | collective-permute-start | bytes 3145736 | tf_op jit(solution)/shard_map/ppermute | solution.py:177
  164.8 9.5 %collective-permute-start.9 = (bf16[96,768]{1,0:T(8,128)(2,1)S(1)}, bf16[96,768]{1,0:T(8,128)(2,1)}, u32[]{:S(2)}, u32[]{:S(2)}) collective-permute-start(bf16[96,768]{1,0:T(8,128)(2,1)S(1)} %reshape.224), channel_id=1, source_target_pairs={{0,2},{2,4},{4,6},{6,8},{8,10},{10,12},{12,14},{14,0},{1,3},{3,5},... | collective-permute-start | bytes 442376 | tf_op jit(solution)/shard_map/ppermute | solution.py:140
  168.4 8.3 %collective-permute-start.10 = (bf16[96,768]{1,0:T(8,128)(2,1)S(1)}, bf16[96,768]{1,0:T(8,128)(2,1)}, u32[]{:S(2)}, u32[]{:S(2)}) collective-permute-start(bf16[96,768]{1,0:T(8,128)(2,1)S(1)} %reshape.224), channel_id=1, source_target_pairs={{0,14},{2,0},{4,2},{6,4},{8,6},{10,8},{12,10},{14,12},{1,15},{3,1}... | collective-permute-start | bytes 442376 | tf_op jit(solution)/shard_map/ppermute | solution.py:140
  172.0 9.4 %copy-start.1 = (bf16[768,768]{1,0:T(8,128)(2,1)}, bf16[768,768]{1,0:T(8,128)(2,1)S(1)}, u32[]{:S(2)}) copy-start(bf16[768,768]{1,0:T(8,128)(2,1)S(1)} %constant_dynamic-update-slice_fusion.15) | copy-start | bytes 3538948
  174.3 23.3 %collective-permute-start.11 = (bf16[96,768]{1,0:T(8,128)(2,1)}, bf16[96,768]{1,0:T(8,128)(2,1)}, u32[]{:S(2)}, u32[]{:S(2)}) collective-permute-start(bf16[96,768]{1,0:T(8,128)(2,1)} %collective-permute-done.9), channel_id=1, source_target_pairs={{0,2},{2,4},{4,6},{6,8},{8,10},{10,12},{12,14},{14,0},{1,3},{3,5},... | collective-permute-start | bytes 442376 | tf_op jit(solution)/shard_map/ppermute | solution.py:140
  176.6 22.9 %collective-permute-start.12 = (bf16[96,768]{1,0:T(8,128)(2,1)}, bf16[96,768]{1,0:T(8,128)(2,1)S(1)}, u32[]{:S(2)}, u32[]{:S(2)}) collective-permute-start(bf16[96,768]{1,0:T(8,128)(2,1)} %collective-permute-done.10), channel_id=1, source_target_pairs={{0,14},{2,0},{4,2},{6,4},{8,6},{10,8},{12,10},{14,12},{1,15},{3,1}... | collective-permute-start | bytes 442376 | tf_op jit(solution)/shard_map/ppermute | solution.py:140
  187.0 34.8 %all-to-all-start.3 = ((bf16[16,2,32,96]{3,2,1,0:T(8,128)(2,1)}), bf16[16,2,32,96]{3,2,1,0:T(8,128)(2,1)S(1)}, u32[]{:S(2)}, u32[]{:S(2)}) async-start(bf16[16,2,32,96]{3,2,1,0:T(8,128)(2,1)} %attend.1), calls=%async_computation.3 | async-start | bytes 524288 | tf_op jit(solution)/shard_map/all_to_all | solution.py:26
  197.6 9.4 %collective-permute-start.13 = (bf16[96,768]{1,0:T(8,128)(2,1)}, bf16[96,768]{1,0:T(8,128)(2,1)S(1)}, u32[]{:S(2)}, u32[]{:S(2)}) collective-permute-start(bf16[96,768]{1,0:T(8,128)(2,1)} %collective-permute-done.11), channel_id=1, source_target_pairs={{0,2},{2,4},{4,6},{6,8},{8,10},{10,12},{12,14},{14,0},{1,3},{3,5},... | collective-permute-start | bytes 442376 | tf_op jit(solution)/shard_map/ppermute | solution.py:140
  199.5 10.1 %collective-permute-start.14 = (bf16[96,768]{1,0:T(8,128)(2,1)S(1)}, bf16[96,768]{1,0:T(8,128)(2,1)S(1)}, u32[]{:S(2)}, u32[]{:S(2)}) collective-permute-start(bf16[96,768]{1,0:T(8,128)(2,1)S(1)} %collective-permute-done.12), channel_id=1, source_target_pairs={{0,14},{2,0},{4,2},{6,4},{8,6},{10,8},{12,10},{14,12},{1,15},{3,1}... | collective-permute-start | bytes 442376 | tf_op jit(solution)/shard_map/ppermute | solution.py:140
  207.0 8.3 %collective-permute-start.15 = (bf16[96,768]{1,0:T(8,128)(2,1)S(1)}, bf16[96,768]{1,0:T(8,128)(2,1)S(1)}, u32[]{:S(2)}, u32[]{:S(2)}) collective-permute-start(bf16[96,768]{1,0:T(8,128)(2,1)S(1)} %collective-permute-done.13), channel_id=1, source_target_pairs={{0,2},{2,4},{4,6},{6,8},{8,10},{10,12},{12,14},{14,0},{1,3},{3,5},... | collective-permute-start | bytes 442376 | tf_op jit(solution)/shard_map/ppermute | solution.py:140
  (8 other events, 28.4 us)

commit v4 on v3

--- a/solution.py
+++ b/solution.py
@@ -10,7 +10,6 @@
 
 
 HEAD_DIM = 48
-QUAD = 4
 
 epsilon = 1e-05
 
@@ -54,18 +53,20 @@
 
 
 def attend_kernel(info_ref, blocks_ref, w_ref, bias_a_ref, bias_b_ref, out_ref, *, samples, scale):
-    neighbours, quads, block_rows, _ = blocks_ref.shape
-    token_rows = block_rows // samples
+    pairs, pair_rows, _ = blocks_ref.shape
+    half_rows = pair_rows // 2
+    token_rows = half_rows // samples
     total = bias_a_ref.shape[0]
-    valid, quad, core = info_ref[0], info_ref[1], info_ref[2]
+    valid, side, core = info_ref[0], info_ref[1], info_ref[2]
     key_ok = lax.broadcasted_iota(jnp.int32, (total, 1), 0) < valid
     dot = functools.partial(lax.dot_general, preferred_element_type=jnp.float32)
+    starts = [side * half_rows, (1 - side) * half_rows]
     for u in range(samples):
         x = jnp.concatenate(
             [
-                blocks_ref[j, lax.rem(a - quad + quads, quads), pl.ds(u * token_rows, token_rows), :]
-                for a in range(quads)
-                for j in range(neighbours)
+                blocks_ref[k, pl.ds(pl.multiple_of(start + u * token_rows, token_rows), token_rows), :]
+                for k in range(pairs)
+                for start in starts
             ]
         )
         projected = dot(w_ref[...], x, (((1,), (1,)), ((), ()))).astype(jnp.bfloat16)
@@ -90,9 +91,9 @@
 
 
 def attend(info, blocks, w, bias_a, bias_b, samples):
-    _, _, block_rows, width = blocks.shape
+    width = blocks.shape[2]
     total = bias_a.shape[0]
-    token_rows = block_rows // samples
+    token_rows = blocks.shape[1] // 2 // samples
     vmem = pl.BlockSpec(memory_space=pltpu.VMEM)
     flops = 2 * samples * total * (width * w.shape[0] + 4 * total * HEAD_DIM)
     return pl.pallas_call(
@@ -127,11 +128,10 @@
     rows = lax.axis_size("row")
     cols = lax.axis_size("col")
     tile_rows, tile_cols, _ = pair_repr.shape
-    heads = bias_weight.shape[1]
-    quads = rows // QUAD
-    adjacent = [[QUAD * a + b for b in range(QUAD)] for a in range(quads)]
+    pairs = rows // 2
     z = lax.axis_index("row")
-    side = (z // QUAD) % 2
+    side = z % 2
+    col = lax.axis_index("col")
     core = lax.axis_index("samp")
     swap = [(0, 1), (1, 0)]
 
@@ -139,36 +139,49 @@
         size = lax.axis_size(axis)
         return lax.ppermute(value, axis, [(i, (i + by) % size) for i in range(size)])
 
-    own_w = qkv_weight[0]
-    half = width // 2
-    part = lax.dynamic_slice_in_dim(own_w, core * half, half, 1)
-    far = lax.ppermute(part, "row", [(i, i ^ QUAD) for i in range(rows)])
-    near = lax.ppermute(far, "samp", swap)
-    other_w = jnp.where(
-        core == 0, jnp.concatenate([far, near], 1), jnp.concatenate([near, far], 1)
-    )
-    own_first = side == core
-    w_a = jnp.where(own_first, own_w, other_w)
-    w_b = jnp.where(own_first, other_w, own_w)
-    w_pair = jnp.stack([w_a, w_b]).transpose(0, 1, 3, 2).reshape(-1, width)
-
-    paired = bias_weight.reshape(-1, heads // 8, 2, QUAD).transpose(0, 1, 3, 2).reshape(-1, heads)
-    tile = bias_tile_of(pair_repr, asym_id, rel_embed, pair_gain, paired)
-    tile, tokens_in, part = lax.optimization_barrier((tile, tokens, part))
-    normed = normalize(tokens_in.astype(jnp.float32), token_gain[0]).astype(jnp.bfloat16)
-    half_samples = sample_count // 2
-    half_rows = half_samples * token_rows
-    halves = normed.reshape(2, half_rows, width)
-    col = lax.axis_index("col")
+    def all_around(block, axis, by):
+        count = lax.axis_size(axis) // by
+        me = lax.axis_index(axis) // by
+        whole = jnp.zeros((count, *block.shape), block.dtype)
+
+        def put(whole, value, index):
+            start = (index % count, *[0] * block.ndim)
+            return lax.dynamic_update_slice(whole, value[None], start)
+
+        whole = put(whole, block, me)
+        up = down = block
+        for step in range(1, count // 2 + 1):
+            up = shifted(up, axis, by)
+            if step < count // 2:
+                down = shifted(down, axis, -by)
+            if step < count // 2:
+                whole = put(whole, down, me + step)
+            whole = put(whole, up, me - step)
+        return whole
+
     depth = out_weight.shape[1]
     slice_rows = depth // cols
     piece = lax.dynamic_slice_in_dim(out_weight[0], col * slice_rows, slice_rows, 0)
-    same = jnp.concatenate([jnp.where(side == 0, halves[0], halves[1]), piece])
-    cross = jnp.concatenate([jnp.where(side == 0, halves[1], halves[0]), piece])
-    tile = tile.reshape(heads // 8, 1, QUAD, 2, tile_rows * tile_cols)
-    tile = jnp.broadcast_to(tile, (heads // 8, 2, QUAD, 2, tile_rows * tile_cols))
+    pieces = exchange(jnp.broadcast_to(piece[None], (rows, *piece.shape)), "row")
+
+    normed = normalize(tokens.astype(jnp.float32), token_gain[0]).astype(jnp.bfloat16)
+    half_samples = sample_count // 2
+    halves = normed.reshape(2, half_samples * token_rows, width)
+    neighbour = [(i, i ^ 1) for i in range(rows)]
+    given = lax.ppermute(jnp.where(side == 0, halves[1], halves[0]), "row", neighbour)
+    block = jnp.concatenate([jnp.where(side == 0, halves[0], halves[1]), given])
+    blocks = all_around(block, "row", 2)
+
+    other_w = lax.ppermute(qkv_weight[0], "row", neighbour)
+    own_first = side == core
+    w_a = jnp.where(own_first, qkv_weight[0], other_w)
+    w_b = jnp.where(own_first, other_w, qkv_weight[0])
+    w_pair = jnp.stack([w_a, w_b]).transpose(0, 1, 3, 2).reshape(-1, width)
+
+    tile = bias_tile_of(pair_repr, asym_id, rel_embed, pair_gain, bias_weight)
+    tile = tile.reshape(pairs, 1, 2, tile_rows * tile_cols)
+    tile = jnp.broadcast_to(tile, (pairs, 2, 2, tile_rows * tile_cols))
     by_row = exchange(tile.reshape(rows, 2, tile_rows * tile_cols), "row")
-    by_row, _, _ = lax.optimization_barrier((by_row, same, cross))
     by_key = by_row.reshape(rows, 2, tile_rows, tile_cols).transpose(1, 3, 0, 2)
     by_key = by_key.reshape(2, tile_cols, total)
     fanned = jnp.broadcast_to(by_key[None], (cols, *by_key.shape))
@@ -176,50 +189,14 @@
     bias_a = bias_a.reshape(total, total)
     bias_b = lax.ppermute(bias_a, "samp", swap)
 
-    def all_cols(block):
-        size = block.shape[0]
-        whole = jnp.zeros((cols * size, *block.shape[1:]), block.dtype)
-        start = (0,) * (block.ndim - 1)
-        whole = lax.dynamic_update_slice(whole, block, (col * size, *start))
-        up = down = block
-        for step in range(1, cols // 2 + 1):
-            up = shifted(up, "col", 1)
-            whole = lax.dynamic_update_slice(whole, up, ((col - step) % cols * size, *start))
-            if step < cols // 2:
-                down = shifted(down, "col", -1)
-                whole = lax.dynamic_update_slice(whole, down, ((col + step) % cols * size, *start))
-        return whole
-
-    opposite = shifted(same, "row", 2 * QUAD)
-    before = shifted(cross, "row", QUAD)
-    after = shifted(cross, "row", -QUAD)
-    around = [same, after, opposite, before]
-    blocks = jnp.stack([item[:half_rows] for item in around])
-    blocks = jnp.broadcast_to(blocks[None], (QUAD, *blocks.shape))
-    blocks = exchange(blocks, "row", adjacent)
-
-    mine = jnp.concatenate([item[half_rows:] for item in around])
-    turned = [mine]
-    for by in range(1, QUAD):
-        turns = [(i, i // QUAD * QUAD + (i - by) % QUAD) for i in range(rows)]
-        turned.append(lax.ppermute(mine, "row", turns))
-    turned = jnp.stack(turned).reshape(QUAD, quads, slice_rows, width)
-    turned = lax.dynamic_slice_in_dim(
-        jnp.concatenate([turned, turned]), (QUAD - z % QUAD) % QUAD, QUAD, 0
-    )
-    turned = lax.dynamic_slice_in_dim(
-        jnp.concatenate([turned, turned], 1), (quads - z // QUAD) % quads, quads, 1
-    )
-    w_out = all_cols(turned.reshape(-1, width)).reshape(
-        cols, QUAD, rows // 8, 2, slice_rows, width
-    )
-    w_out = w_out.transpose(2, 1, 3, 0, 4, 5).reshape(width, width)
-
-    info = jnp.stack([valid_len[0], z // QUAD, core]).astype(jnp.int32)
+    w_out = all_around(pieces, "col", 1)
+    w_out = w_out.transpose(1, 0, 2, 3).reshape(width, width)
+
+    info = jnp.stack([valid_len[0], side, core]).astype(jnp.int32)
     attended = attend(info, blocks, w_pair, bias_a, bias_b, half_samples)
     back = exchange(attended, "row")
-    back = back.reshape(rows // 8, 2, QUAD, sample_count // 2, token_rows, 2 * HEAD_DIM)
-    back = back.transpose(1, 3, 4, 0, 2, 5).reshape(sample_count * token_rows, width)
+    back = back.reshape(pairs, 2, half_samples, token_rows, 2 * HEAD_DIM)
+    back = back.transpose(1, 2, 3, 0, 4).reshape(sample_count * token_rows, width)
     update = jnp.dot(back, w_out, preferred_element_type=jnp.float32)
     return (
         tokens.astype(jnp.float32) + update.reshape(sample_count, token_rows, width)

time: 225 us -> 195 us (0.87)
  waiting for transfers between devices: 67.9 us -> 48.2 us
  local copies, waits for them, and re-layouts: 25.2 us -> 18.7 us
    ppermute x5 -> x2, waiting for transfers between devices: 28.1 us -> 0.01 us  [the longest x1 0.01 us: per_device(): lax.ppermute(jnp.where(side == 0, halves[1], halves[0]), 'row', neighbour)]
    all_to_all x4, waiting for transfers between devices: 14 us -> 27.5 us  [exchange(): lax.all_to_all(blocks, axis, split_axis=0, concat_axis=0, axis_index_grou...]
    ppermute x5 -> x2, starting transfers between devices: 15.5 us -> 5.91 us  [the longest x1 3.64 us: per_device(): lax.ppermute(jnp.where(side == 0, halves[1], halves[0]), 'row', neighbour)]
    ppermute x10 -> x14, starting transfers between devices: 37.4 us -> 45.8 us  [shifted(): lax.ppermute(value, axis, [(i, (i + by) % size) for i in range(size)])]
    ppermute x10 -> x14, waiting for transfers between devices: 25.8 us -> 20.7 us  [shifted(): lax.ppermute(value, axis, [(i, (i + by) % size) for i in range(size)])]
    dynamic_update_slice x8 -> x15, local copies, waits for them, and re-layouts: 7.45 us -> 11.7 us  [put(): return lax.dynamic_update_slice(whole, value[None], start)]
    unnamed x27 -> x20, local copies, waits for them, and re-layouts: 5 us -> 0.82 us
    reshape x4 -> x1, local copies, waits for them, and re-layouts: 5.32 us -> 2.31 us  [per_device(): w_out = w_out.transpose(1, 0, 2, 3).reshape(width, width)]
  transfers between devices with their start and end apart: 20 -> 21, of which waited for: 7 -> 10; matrix products, arithmetic and copies ran while one was open for 10% -> 9% of each run, Pallas kernels for 3% -> 3%
where the time goes in v4:
time: 195 us; the launch traced here: 194 us
  starting transfers between devices  116 us (59%)
  waiting for transfers between devices  48.2 us (25%)
  local copies, waits for them, and re-layouts  18.7 us (10%)
  Pallas kernels  4.91 us (3%)
  other arithmetic  2.91 us (1%)
  matrix products  2.18 us (1%)
    all_to_all x4, starting transfers between devices, exchange(): lax.all_to_all(blocks, axis, split_axis=0, concat_axis=0, axis_index_grou...  62 us
    ppermute x14, starting transfers between devices, shifted(): lax.ppermute(value, axis, [(i, (i + by) % size) for i in range(size)])  45.8 us
    all_to_all x4, waiting for transfers between devices, exchange(): lax.all_to_all(blocks, axis, split_axis=0, concat_axis=0, axis_index_grou...  27.5 us
    ppermute x14, waiting for transfers between devices, shifted(): lax.ppermute(value, axis, [(i, (i + by) % size) for i in range(size)])  20.7 us
    dynamic_update_slice x15, local copies, waits for them, and re-layouts, put(): return lax.dynamic_update_slice(whole, value[None], start)  11.7 us
    pallas_call x1, Pallas kernels, attend(): pl.pallas_call(functools.partial(attend_kernel, samples=samples, scale=1....  4.91 us
  transfers between devices with their start and end apart: 21, of which 10 were waited for; matrix products, arithmetic and copies ran while one was open for 9% of the time, Pallas kernels for 3%

profile of v4, /device:TPU:80, one launch (start us, length us, event | category | flops | bytes accessed | tf_op | source)
XLA Modules:
  0.0 194.1 jit_solution(13041176410212076529)
XLA Ops:
  3.6 43.7 %all-to-all-start = ((f32[16,2,1024]{2,1,0:T(2,128)}), f32[16,2,1024]{2,1,0:T(2,128)S(1)}, u32[]{:S(2)}, u32[]{:S(2)}) async-start(f32[16,2,1024]{2,1,0:T(2,128)} %bitcast.19), calls=%async_computation | async-start | bytes 262144 | tf_op jit(solution)/shard_map/all_to_all | solution.py:25
  47.7 14.2 %all-to-all-done = f32[16,2,1024]{2,1,0:T(2,128)S(1)} async-done(((f32[16,2,1024]{2,1,0:T(2,128)}), f32[16,2,1024]{2,1,0:T(2,128)S(1)}, u32[]{:S(2)}, u32[]{:S(2)}) %all-to-all-start) | async-done | bytes 131104 | tf_op jit(solution)/shard_map/all_to_all | solution.py:25
  62.6 4.0 %all-to-all-start.3 = ((bf16[16,6,768]{2,1,0:T(8,128)(2,1)}), bf16[16,6,768]{2,1,0:T(8,128)(2,1)S(1)}, u32[]{:S(2)}, u32[]{:S(2)}) async-start(bf16[16,6,768]{2,1,0:T(8,128)(2,1)} %broadcast_in_dim.106), calls=%async_computation.3 | async-start | bytes 393216 | tf_op jit(solution)/shard_map/all_to_all | solution.py:25
  66.8 3.6 %collective-permute-start = (bf16[64,768]{1,0:T(8,128)(2,1)S(1)}, bf16[64,768]{1,0:T(8,128)(2,1)S(1)}, u32[]{:S(2)}, u32[]{:S(2)}) collective-permute-start(bf16[64,768]{1,0:T(8,128)(2,1)S(1)} %bitcast.93), channel_id=1, source_target_pairs={{0,16},{16,0},{32,48},{48,32},{64,80},{80,64},{96,112},{112,96},{1... | collective-permute-start | bytes 294920 | tf_op jit(solution)/shard_map/ppermute | solution.py:171
  70.4 2.3 %collective-permute-start.8 = (bf16[3,768,48]{1,2,0:T(8,128)(2,1)}, bf16[3,768,48]{1,2,0:T(8,128)(2,1)}, u32[]{:S(2)}, u32[]{:S(2)}) collective-permute-start(bf16[3,768,48]{1,2,0:T(8,128)(2,1)} %bitcast.12), channel_id=1, source_target_pairs={{0,16},{16,0},{32,48},{48,32},{64,80},{80,64},{96,112},{112,96},{1... | collective-permute-start | bytes 663560 | tf_op jit(solution)/shard_map/ppermute | solution.py:175
  74.2 8.2 %all-to-all-done.3 = bf16[16,6,768]{2,1,0:T(8,128)(2,1)S(1)} async-done(((bf16[16,6,768]{2,1,0:T(8,128)(2,1)}), bf16[16,6,768]{2,1,0:T(8,128)(2,1)S(1)}, u32[]{:S(2)}, u32[]{:S(2)}) %all-to-all-start.3) | async-done | bytes 147488 | tf_op jit(solution)/shard_map/all_to_all | solution.py:25
  83.4 7.6 %all-to-all-start.1 = ((f32[16,32,512]{2,1,0:T(8,128)}), f32[16,32,512]{2,1,0:T(8,128)S(1)}, u32[]{:S(2)}, u32[]{:S(2)}) async-start(f32[16,32,512]{2,1,0:T(8,128)} %bitcast.22), calls=%async_computation.1 | async-start | bytes 2097152 | tf_op jit(solution)/shard_map/all_to_all | solution.py:25
  91.1 4.1 %collective-permute-start.1 = (bf16[128,768]{1,0:T(8,128)(2,1)S(1)}, bf16[128,768]{1,0:T(8,128)(2,1)S(1)}, u32[]{:S(2)}, u32[]{:S(2)}) collective-permute-start(bf16[128,768]{1,0:T(8,128)(2,1)S(1)} %pad_maximum_fusion.1), channel_id=1, source_target_pairs={{0,224},{16,240},{32,0},{48,16},{64,32},{80,48},{96,64},{112,80},{... | collective-permute-start | bytes 589832 | tf_op jit(solution)/shard_map/ppermute | solution.py:140
  95.2 2.7 %collective-permute-start.2 = (bf16[128,768]{1,0:T(8,128)(2,1)S(1)}, bf16[128,768]{1,0:T(8,128)(2,1)S(1)}, u32[]{:S(2)}, u32[]{:S(2)}) collective-permute-start(bf16[128,768]{1,0:T(8,128)(2,1)S(1)} %pad_maximum_fusion.1), channel_id=1, source_target_pairs={{0,32},{16,48},{32,64},{48,80},{64,96},{80,112},{96,128},{112,144}... | collective-permute-start | bytes 589832 | tf_op jit(solution)/shard_map/ppermute | solution.py:140
  100.0 5.3 %collective-permute-done.1 = bf16[128,768]{1,0:T(8,128)(2,1)S(1)} collective-permute-done((bf16[128,768]{1,0:T(8,128)(2,1)S(1)}, bf16[128,768]{1,0:T(8,128)(2,1)S(1)}, u32[]{:S(2)}, u32[]{:S(2)}) %collective-permute-start.1) | collective-permute-done | bytes 196640 | tf_op jit(solution)/shard_map/ppermute | solution.py:140
  105.2 4.4 %collective-permute-start.3 = (bf16[128,768]{1,0:T(8,128)(2,1)S(1)}, bf16[128,768]{1,0:T(8,128)(2,1)S(1)}, u32[]{:S(2)}, u32[]{:S(2)}) collective-permute-start(bf16[128,768]{1,0:T(8,128)(2,1)S(1)} %collective-permute-done.1), channel_id=1, source_target_pairs={{0,224},{16,240},{32,0},{48,16},{64,32},{80,48},{96,64},{112,80},{... | collective-permute-start | bytes 589832 | tf_op jit(solution)/shard_map/ppermute | solution.py:140
  112.3 4.1 %collective-permute-done.3 = bf16[128,768]{1,0:T(8,128)(2,1)S(1)} collective-permute-done((bf16[128,768]{1,0:T(8,128)(2,1)S(1)}, bf16[128,768]{1,0:T(8,128)(2,1)S(1)}, u32[]{:S(2)}, u32[]{:S(2)}) %collective-permute-start.3) | collective-permute-done | bytes 196640 | tf_op jit(solution)/shard_map/ppermute | solution.py:140
  116.4 5.0 %collective-permute-start.5 = (bf16[128,768]{1,0:T(8,128)(2,1)S(1)}, bf16[128,768]{1,0:T(8,128)(2,1)S(1)}, u32[]{:S(2)}, u32[]{:S(2)}) collective-permute-start(bf16[128,768]{1,0:T(8,128)(2,1)S(1)} %collective-permute-done.3), channel_id=1, source_target_pairs={{0,224},{16,240},{32,0},{48,16},{64,32},{80,48},{96,64},{112,80},{... | collective-permute-start | bytes 589832 | tf_op jit(solution)/shard_map/ppermute | solution.py:140
  121.4 2.7 %collective-permute-done.4 = bf16[128,768]{1,0:T(8,128)(2,1)S(1)} collective-permute-done((bf16[128,768]{1,0:T(8,128)(2,1)S(1)}, bf16[128,768]{1,0:T(8,128)(2,1)S(1)}, u32[]{:S(2)}, u32[]{:S(2)}) %collective-permute-start.4) | collective-permute-done | bytes 196640 | tf_op jit(solution)/shard_map/ppermute | solution.py:140
  126.1 4.8 %collective-permute-start.10 = (bf16[16,6,768]{2,1,0:T(8,128)(2,1)S(1)}, bf16[16,6,768]{2,1,0:T(8,128)(2,1)}, u32[]{:S(2)}, u32[]{:S(2)}) collective-permute-start(bf16[16,6,768]{2,1,0:T(8,128)(2,1)S(1)} %all-to-all-done.3), channel_id=1, source_target_pairs={{0,14},{2,0},{4,2},{6,4},{8,6},{10,8},{12,10},{14,12},{1,15},{3,1}... | collective-permute-start | bytes 442376 | tf_op jit(solution)/shard_map/ppermute | solution.py:140
  133.1 3.9 %collective-permute-done.6 = bf16[128,768]{1,0:T(8,128)(2,1)} collective-permute-done((bf16[128,768]{1,0:T(8,128)(2,1)S(1)}, bf16[128,768]{1,0:T(8,128)(2,1)}, u32[]{:S(2)}, u32[]{:S(2)}) %collective-permute-start.6) | collective-permute-done | bytes 196640 | tf_op jit(solution)/shard_map/ppermute | solution.py:140
  137.0 2.5 %collective-permute-start.7 = (bf16[128,768]{1,0:T(8,128)(2,1)}, bf16[128,768]{1,0:T(8,128)(2,1)}, u32[]{:S(2)}, u32[]{:S(2)}) collective-permute-start(bf16[128,768]{1,0:T(8,128)(2,1)} %collective-permute-done.6), channel_id=1, source_target_pairs={{0,32},{16,48},{32,64},{48,80},{64,96},{80,112},{96,128},{112,144}... | collective-permute-start | bytes 589832 | tf_op jit(solution)/shard_map/ppermute | solution.py:140
  142.5 5.2 %collective-permute-start.12 = (bf16[16,6,768]{2,1,0:T(8,128)(2,1)}, bf16[16,6,768]{2,1,0:T(8,128)(2,1)}, u32[]{:S(2)}, u32[]{:S(2)}) collective-permute-start(bf16[16,6,768]{2,1,0:T(8,128)(2,1)} %collective-permute-done.10), channel_id=1, source_target_pairs={{0,14},{2,0},{4,2},{6,4},{8,6},{10,8},{12,10},{14,12},{1,15},{3,1}... | collective-permute-start | bytes 442376 | tf_op jit(solution)/shard_map/ppermute | solution.py:140
  153.0 5.4 %collective-permute-start.14 = (bf16[16,6,768]{2,1,0:T(8,128)(2,1)}, bf16[16,6,768]{2,1,0:T(8,128)(2,1)}, u32[]{:S(2)}, u32[]{:S(2)}) collective-permute-start(bf16[16,6,768]{2,1,0:T(8,128)(2,1)} %collective-permute-done.12), channel_id=1, source_target_pairs={{0,14},{2,0},{4,2},{6,4},{8,6},{10,8},{12,10},{14,12},{1,15},{3,1}... | collective-permute-start | bytes 442376 | tf_op jit(solution)/shard_map/ppermute | solution.py:140
  163.0 4.9 %attend.1 = bf16[16,2,32,96]{3,2,1,0:T(8,128)(2,1)} custom-call(s32[3]{0:T(128)S(1)} %pad_add_fusion.info_ref, bf16[8,128,768]{2,1,0:T(8,128)(2,1)S(1)} %bitcast_dynamic-update-slice_fusion.8.blocks_ref, bf16[288,768]{1,0:T(8,128)(2,1)S(1)} %bitcast.87, f32[512,512]{1,0:T(8,128)S(1)} %bitcast.86, f32[512,512]{1,0:T(8,128)S(1)} %collective-permute-done.9.bias_b_ref), custom_call_target="tpu_custom_call" | custom-call | flops 654311424 | bytes 6291456 | tf_op jit(solution)/shard_map/attend/pallas_call | solution.py:99
  167.9 6.7 %all-to-all-start.2 = ((bf16[16,2,32,96]{3,2,1,0:T(8,128)(2,1)}), bf16[16,2,32,96]{3,2,1,0:T(8,128)(2,1)S(1)}, u32[]{:S(2)}, u32[]{:S(2)}) async-start(bf16[16,2,32,96]{3,2,1,0:T(8,128)(2,1)} %attend.1), calls=%async_computation.2 | async-start | bytes 524288 | tf_op jit(solution)/shard_map/all_to_all | solution.py:25
  180.5 4.0 %collective-permute-done.16 = bf16[16,6,768]{2,1,0:T(8,128)(2,1)S(1)} collective-permute-done((bf16[16,6,768]{2,1,0:T(8,128)(2,1)}, bf16[16,6,768]{2,1,0:T(8,128)(2,1)S(1)}, u32[]{:S(2)}, u32[]{:S(2)}) %collective-permute-start.16) | collective-permute-done | bytes 147488 | tf_op jit(solution)/shard_map/ppermute | solution.py:140
  185.2 2.3 %reshape.124 = bf16[768,768,1]{1,0,2:T(8,128)(2,1)S(1)} reshape(bf16[16,8,6,768]{3,2,1,0:T(8,128)(2,1)} %bitcast.88) | data formatting | bytes 2359296 | tf_op jit(solution)/shard_map/reshape | solution.py:193
  187.6 5.1 %all-to-all-done.2 = bf16[16,2,32,96]{3,2,1,0:T(8,128)(2,1)S(1)} async-done(((bf16[16,2,32,96]{3,2,1,0:T(8,128)(2,1)}), bf16[16,2,32,96]{3,2,1,0:T(8,128)(2,1)S(1)}, u32[]{:S(2)}, u32[]{:S(2)}) %all-to-all-start.2) | async-done | bytes 196640 | tf_op jit(solution)/shard_map/all_to_all | solution.py:25
  (91 shorter events, 36.0 us)
Async XLA Ops:
  0.0 47.5 %copy-start = (bf16[1,48,768]{2,1,0:T(8,128)(2,1)S(1)}, bf16[1,48,768]{2,1,0:T(8,128)(2,1)}, u32[]{:S(2)}) copy-start(bf16[1,48,768]{2,1,0:T(8,128)(2,1)} %param.19) | copy-start | bytes 221188
  1.3 46.0 %copy-start.2 = (bf16[4,32,768]{2,1,0:T(8,128)(2,1)S(1)}, bf16[4,32,768]{2,1,0:T(8,128)(2,1)}, u32[]{:S(2)}) copy-start(bf16[4,32,768]{2,1,0:T(8,128)(2,1)} %param.16) | copy-start | bytes 589828
  1.3 46.1 %copy-start.7 = (f32[1,768]{1,0:T(1,128)S(1)}, f32[1,768]{1,0:T(1,128)}, u32[]{:S(2)}) copy-start(f32[1,768]{1,0:T(1,128)} %param.17) | copy-start | bytes 9220
  3.6 58.3 %all-to-all-start = ((f32[16,2,1024]{2,1,0:T(2,128)}), f32[16,2,1024]{2,1,0:T(2,128)S(1)}, u32[]{:S(2)}, u32[]{:S(2)}) async-start(f32[16,2,1024]{2,1,0:T(2,128)} %bitcast.19), calls=%async_computation | async-start | bytes 262144 | tf_op jit(solution)/shard_map/all_to_all | solution.py:25
  62.6 19.7 %all-to-all-start.3 = ((bf16[16,6,768]{2,1,0:T(8,128)(2,1)}), bf16[16,6,768]{2,1,0:T(8,128)(2,1)S(1)}, u32[]{:S(2)}, u32[]{:S(2)}) async-start(bf16[16,6,768]{2,1,0:T(8,128)(2,1)} %broadcast_in_dim.106), calls=%async_computation.3 | async-start | bytes 393216 | tf_op jit(solution)/shard_map/all_to_all | solution.py:25
  66.8 24.3 %collective-permute-start = (bf16[64,768]{1,0:T(8,128)(2,1)S(1)}, bf16[64,768]{1,0:T(8,128)(2,1)S(1)}, u32[]{:S(2)}, u32[]{:S(2)}) collective-permute-start(bf16[64,768]{1,0:T(8,128)(2,1)S(1)} %bitcast.93), channel_id=1, source_target_pairs={{0,16},{16,0},{32,48},{48,32},{64,80},{80,64},{96,112},{112,96},{1... | collective-permute-start | bytes 294920 | tf_op jit(solution)/shard_map/ppermute | solution.py:171
  70.4 28.4 %collective-permute-start.8 = (bf16[3,768,48]{1,2,0:T(8,128)(2,1)}, bf16[3,768,48]{1,2,0:T(8,128)(2,1)}, u32[]{:S(2)}, u32[]{:S(2)}) collective-permute-start(bf16[3,768,48]{1,2,0:T(8,128)(2,1)} %bitcast.12), channel_id=1, source_target_pairs={{0,16},{16,0},{32,48},{48,32},{64,80},{80,64},{96,112},{112,96},{1... | collective-permute-start | bytes 663560 | tf_op jit(solution)/shard_map/ppermute | solution.py:175
  83.4 56.1 %all-to-all-start.1 = ((f32[16,32,512]{2,1,0:T(8,128)}), f32[16,32,512]{2,1,0:T(8,128)S(1)}, u32[]{:S(2)}, u32[]{:S(2)}) async-start(f32[16,32,512]{2,1,0:T(8,128)} %bitcast.22), calls=%async_computation.1 | async-start | bytes 2097152 | tf_op jit(solution)/shard_map/all_to_all | solution.py:25
  91.1 14.1 %collective-permute-start.1 = (bf16[128,768]{1,0:T(8,128)(2,1)S(1)}, bf16[128,768]{1,0:T(8,128)(2,1)S(1)}, u32[]{:S(2)}, u32[]{:S(2)}) collective-permute-start(bf16[128,768]{1,0:T(8,128)(2,1)S(1)} %pad_maximum_fusion.1), channel_id=1, source_target_pairs={{0,224},{16,240},{32,0},{48,16},{64,32},{80,48},{96,64},{112,80},{... | collective-permute-start | bytes 589832 | tf_op jit(solution)/shard_map/ppermute | solution.py:140
  95.2 15.1 %collective-permute-start.2 = (bf16[128,768]{1,0:T(8,128)(2,1)S(1)}, bf16[128,768]{1,0:T(8,128)(2,1)S(1)}, u32[]{:S(2)}, u32[]{:S(2)}) collective-permute-start(bf16[128,768]{1,0:T(8,128)(2,1)S(1)} %pad_maximum_fusion.1), channel_id=1, source_target_pairs={{0,32},{16,48},{32,64},{48,80},{64,96},{80,112},{96,128},{112,144}... | collective-permute-start | bytes 589832 | tf_op jit(solution)/shard_map/ppermute | solution.py:140
  105.2 11.1 %collective-permute-start.3 = (bf16[128,768]{1,0:T(8,128)(2,1)S(1)}, bf16[128,768]{1,0:T(8,128)(2,1)S(1)}, u32[]{:S(2)}, u32[]{:S(2)}) collective-permute-start(bf16[128,768]{1,0:T(8,128)(2,1)S(1)} %collective-permute-done.1), channel_id=1, source_target_pairs={{0,224},{16,240},{32,0},{48,16},{64,32},{80,48},{96,64},{112,80},{... | collective-permute-start | bytes 589832 | tf_op jit(solution)/shard_map/ppermute | solution.py:140
  110.3 13.8 %collective-permute-start.4 = (bf16[128,768]{1,0:T(8,128)(2,1)S(1)}, bf16[128,768]{1,0:T(8,128)(2,1)S(1)}, u32[]{:S(2)}, u32[]{:S(2)}) collective-permute-start(bf16[128,768]{1,0:T(8,128)(2,1)S(1)} %collective-permute-done.2), channel_id=1, source_target_pairs={{0,32},{16,48},{32,64},{48,80},{64,96},{80,112},{96,128},{112,144}... | collective-permute-start | bytes 589832 | tf_op jit(solution)/shard_map/ppermute | solution.py:140
  116.4 23.1 %collective-permute-start.5 = (bf16[128,768]{1,0:T(8,128)(2,1)S(1)}, bf16[128,768]{1,0:T(8,128)(2,1)S(1)}, u32[]{:S(2)}, u32[]{:S(2)}) collective-permute-start(bf16[128,768]{1,0:T(8,128)(2,1)S(1)} %collective-permute-done.3), channel_id=1, source_target_pairs={{0,224},{16,240},{32,0},{48,16},{64,32},{80,48},{96,64},{112,80},{... | collective-permute-start | bytes 589832 | tf_op jit(solution)/shard_map/ppermute | solution.py:140
  124.1 12.8 %collective-permute-start.6 = (bf16[128,768]{1,0:T(8,128)(2,1)S(1)}, bf16[128,768]{1,0:T(8,128)(2,1)}, u32[]{:S(2)}, u32[]{:S(2)}) collective-permute-start(bf16[128,768]{1,0:T(8,128)(2,1)S(1)} %collective-permute-done.4), channel_id=1, source_target_pairs={{0,32},{16,48},{32,64},{48,80},{64,96},{80,112},{96,128},{112,144}... | collective-permute-start | bytes 589832 | tf_op jit(solution)/shard_map/ppermute | solution.py:140
  126.1 16.4 %collective-permute-start.10 = (bf16[16,6,768]{2,1,0:T(8,128)(2,1)S(1)}, bf16[16,6,768]{2,1,0:T(8,128)(2,1)}, u32[]{:S(2)}, u32[]{:S(2)}) collective-permute-start(bf16[16,6,768]{2,1,0:T(8,128)(2,1)S(1)} %all-to-all-done.3), channel_id=1, source_target_pairs={{0,14},{2,0},{4,2},{6,4},{8,6},{10,8},{12,10},{14,12},{1,15},{3,1}... | collective-permute-start | bytes 442376 | tf_op jit(solution)/shard_map/ppermute | solution.py:140
  130.9 16.7 %collective-permute-start.11 = (bf16[16,6,768]{2,1,0:T(8,128)(2,1)S(1)}, bf16[16,6,768]{2,1,0:T(8,128)(2,1)}, u32[]{:S(2)}, u32[]{:S(2)}) collective-permute-start(bf16[16,6,768]{2,1,0:T(8,128)(2,1)S(1)} %all-to-all-done.3), channel_id=1, source_target_pairs={{0,2},{2,4},{4,6},{6,8},{8,10},{10,12},{12,14},{14,0},{1,3},{3,5},... | collective-permute-start | bytes 442376 | tf_op jit(solution)/shard_map/ppermute | solution.py:140
  137.0 25.1 %collective-permute-start.7 = (bf16[128,768]{1,0:T(8,128)(2,1)}, bf16[128,768]{1,0:T(8,128)(2,1)}, u32[]{:S(2)}, u32[]{:S(2)}) collective-permute-start(bf16[128,768]{1,0:T(8,128)(2,1)} %collective-permute-done.6), channel_id=1, source_target_pairs={{0,32},{16,48},{32,64},{48,80},{64,96},{80,112},{96,128},{112,144}... | collective-permute-start | bytes 589832 | tf_op jit(solution)/shard_map/ppermute | solution.py:140
  139.6 23.4 %collective-permute-start.9 = (f32[512,512]{1,0:T(8,128)S(1)}, f32[512,512]{1,0:T(8,128)S(1)}, u32[]{:S(2)}, u32[]{:S(2)}) collective-permute-start(f32[512,512]{1,0:T(8,128)S(1)} %bitcast.85), channel_id=1, source_target_pairs={{0,1},{1,0},{2,3},{3,2},{4,5},{5,4},{6,7},{7,6},{8,9},{9,8},{10,11... | collective-permute-start | bytes 3145736 | tf_op jit(solution)/shard_map/ppermute | solution.py:190
  142.5 10.5 %collective-permute-start.12 = (bf16[16,6,768]{2,1,0:T(8,128)(2,1)}, bf16[16,6,768]{2,1,0:T(8,128)(2,1)}, u32[]{:S(2)}, u32[]{:S(2)}) collective-permute-start(bf16[16,6,768]{2,1,0:T(8,128)(2,1)} %collective-permute-done.10), channel_id=1, source_target_pairs={{0,14},{2,0},{4,2},{6,4},{8,6},{10,8},{12,10},{14,12},{1,15},{3,1}... | collective-permute-start | bytes 442376 | tf_op jit(solution)/shard_map/ppermute | solution.py:140
  147.7 10.7 %collective-permute-start.13 = (bf16[16,6,768]{2,1,0:T(8,128)(2,1)}, bf16[16,6,768]{2,1,0:T(8,128)(2,1)S(1)}, u32[]{:S(2)}, u32[]{:S(2)}) collective-permute-start(bf16[16,6,768]{2,1,0:T(8,128)(2,1)} %collective-permute-done.11), channel_id=1, source_target_pairs={{0,2},{2,4},{4,6},{6,8},{8,10},{10,12},{12,14},{14,0},{1,3},{3,5},... | collective-permute-start | bytes 442376 | tf_op jit(solution)/shard_map/ppermute | solution.py:140
  153.0 24.3 %collective-permute-start.14 = (bf16[16,6,768]{2,1,0:T(8,128)(2,1)}, bf16[16,6,768]{2,1,0:T(8,128)(2,1)}, u32[]{:S(2)}, u32[]{:S(2)}) collective-permute-start(bf16[16,6,768]{2,1,0:T(8,128)(2,1)} %collective-permute-done.12), channel_id=1, source_target_pairs={{0,14},{2,0},{4,2},{6,4},{8,6},{10,8},{12,10},{14,12},{1,15},{3,1}... | collective-permute-start | bytes 442376 | tf_op jit(solution)/shard_map/ppermute | solution.py:140
  158.4 16.9 %collective-permute-start.15 = (bf16[16,6,768]{2,1,0:T(8,128)(2,1)S(1)}, bf16[16,6,768]{2,1,0:T(8,128)(2,1)}, u32[]{:S(2)}, u32[]{:S(2)}) collective-permute-start(bf16[16,6,768]{2,1,0:T(8,128)(2,1)S(1)} %collective-permute-done.13), channel_id=1, source_target_pairs={{0,2},{2,4},{4,6},{6,8},{8,10},{10,12},{12,14},{14,0},{1,3},{3,5},... | collective-permute-start | bytes 442376 | tf_op jit(solution)/shard_map/ppermute | solution.py:140
  167.9 24.8 %all-to-all-start.2 = ((bf16[16,2,32,96]{3,2,1,0:T(8,128)(2,1)}), bf16[16,2,32,96]{3,2,1,0:T(8,128)(2,1)S(1)}, u32[]{:S(2)}, u32[]{:S(2)}) async-start(bf16[16,2,32,96]{3,2,1,0:T(8,128)(2,1)} %attend.1), calls=%async_computation.2 | async-start | bytes 524288 | tf_op jit(solution)/shard_map/all_to_all | solution.py:25
  175.3 9.2 %collective-permute-start.16 = (bf16[16,6,768]{2,1,0:T(8,128)(2,1)}, bf16[16,6,768]{2,1,0:T(8,128)(2,1)S(1)}, u32[]{:S(2)}, u32[]{:S(2)}) collective-permute-start(bf16[16,6,768]{2,1,0:T(8,128)(2,1)} %collective-permute-done.15), channel_id=1, source_target_pairs={{0,2},{2,4},{4,6},{6,8},{8,10},{10,12},{12,14},{14,0},{1,3},{3,5},... | collective-permute-start | bytes 442376 | tf_op jit(solution)/shard_map/ppermute | solution.py:140
  (7 other events, 19.5 us)

commit v5 on v4

--- a/solution.py
+++ b/solution.py
@@ -52,14 +52,43 @@
     return projected
 
 
-def attend_kernel(info_ref, blocks_ref, w_ref, bias_a_ref, bias_b_ref, out_ref, *, samples, scale):
+def normalize_kernel(side_ref, tokens_ref, gain_ref, keep_ref, give_ref):
+    samples, token_rows, width = tokens_ref.shape
+    values = tokens_ref[...].reshape(samples * token_rows, width).astype(jnp.float32)
+    normed = normalize(values, gain_ref[...]).astype(jnp.bfloat16)
+    half = samples * token_rows // 2
+    even = side_ref[0] == 0
+    keep_ref[...] = jnp.where(even, normed[:half], normed[half:])
+    give_ref[...] = jnp.where(even, normed[half:], normed[:half])
+
+
+def normalized_halves(side, tokens, gain):
+    samples, token_rows, width = tokens.shape
+    half = jax.ShapeDtypeStruct((samples * token_rows // 2, width), jnp.bfloat16)
+    vmem = pl.BlockSpec(memory_space=pltpu.VMEM)
+    return pl.pallas_call(
+        normalize_kernel,
+        out_shape=(half, half),
+        in_specs=[pl.BlockSpec(memory_space=pltpu.SMEM), vmem, vmem],
+        out_specs=(vmem, vmem),
+        cost_estimate=pl.CostEstimate(
+            flops=10 * tokens.size, bytes_accessed=4 * tokens.size, transcendentals=0
+        ),
+        name="normalize",
+    )(side, tokens, gain)
+
+
+def attend_kernel(info_1_ref, info_2_ref, *refs, samples, scale):
+    *block_refs, w_ref, bias_a_ref, bias_b_ref, out_ref, blocks_ref = refs
     pairs, pair_rows, _ = blocks_ref.shape
     half_rows = pair_rows // 2
     token_rows = half_rows // samples
     total = bias_a_ref.shape[0]
-    valid, side, core = info_ref[0], info_ref[1], info_ref[2]
+    valid, side, core, pair = info_1_ref[0], info_1_ref[1], info_2_ref[0], info_2_ref[1]
     key_ok = lax.broadcasted_iota(jnp.int32, (total, 1), 0) < valid
     dot = functools.partial(lax.dot_general, preferred_element_type=jnp.float32)
+    for step, block_ref in enumerate(block_refs):
+        blocks_ref[lax.rem(pair - step + pairs, pairs)] = block_ref[...]
     starts = [side * half_rows, (1 - side) * half_rows]
     for u in range(samples):
         x = jnp.concatenate(
@@ -90,10 +119,10 @@
             out_ref[i, u] = both[i * token_rows : (i + 1) * token_rows]
 
 
-def attend(info, blocks, w, bias_a, bias_b, samples):
-    width = blocks.shape[2]
+def attend(info_1, info_2, blocks, w, bias_a, bias_b, samples):
+    pair_rows, width = blocks[0].shape
     total = bias_a.shape[0]
-    token_rows = blocks.shape[1] // 2 // samples
+    token_rows = pair_rows // 2 // samples
     vmem = pl.BlockSpec(memory_space=pltpu.VMEM)
     flops = 2 * samples * total * (width * w.shape[0] + 4 * total * HEAD_DIM)
     return pl.pallas_call(
@@ -101,14 +130,15 @@
         out_shape=jax.ShapeDtypeStruct(
             (total // token_rows, samples, token_rows, 2 * HEAD_DIM), jnp.bfloat16
         ),
-        in_specs=[pl.BlockSpec(memory_space=pltpu.SMEM), vmem, vmem, vmem, vmem],
+        in_specs=[pl.BlockSpec(memory_space=pltpu.SMEM)] * 2 + [vmem] * (len(blocks) + 3),
         out_specs=vmem,
+        scratch_shapes=[pltpu.VMEM((len(blocks), pair_rows, width), jnp.bfloat16)],
         compiler_params=pltpu.CompilerParams(vmem_limit_bytes=48 * 1024 * 1024),
         cost_estimate=pl.CostEstimate(
             flops=flops, bytes_accessed=6 * 1024 * 1024, transcendentals=samples * 2 * total * total
         ),
         name="attend",
-    )(info, blocks, w, bias_a, bias_b)
+    )(info_1, info_2, *blocks, w, bias_a, bias_b)
 
 
 def per_device(
@@ -134,43 +164,32 @@
     col = lax.axis_index("col")
     core = lax.axis_index("samp")
     swap = [(0, 1), (1, 0)]
-
     def shifted(value, axis, by):
         size = lax.axis_size(axis)
         return lax.ppermute(value, axis, [(i, (i + by) % size) for i in range(size)])
 
-    def all_around(block, axis, by):
-        count = lax.axis_size(axis) // by
-        me = lax.axis_index(axis) // by
-        whole = jnp.zeros((count, *block.shape), block.dtype)
-
-        def put(whole, value, index):
-            start = (index % count, *[0] * block.ndim)
-            return lax.dynamic_update_slice(whole, value[None], start)
-
-        whole = put(whole, block, me)
-        up = down = block
-        for step in range(1, count // 2 + 1):
-            up = shifted(up, axis, by)
-            if step < count // 2:
-                down = shifted(down, axis, -by)
-            if step < count // 2:
-                whole = put(whole, down, me + step)
-            whole = put(whole, up, me - step)
-        return whole
+    info_1 = jnp.stack([valid_len[0], side]).astype(jnp.int32)
+    info_2 = jnp.stack([core, z // 2, valid_len[0]]).astype(jnp.int32)
 
     depth = out_weight.shape[1]
-    slice_rows = depth // cols
-    piece = lax.dynamic_slice_in_dim(out_weight[0], col * slice_rows, slice_rows, 0)
+    slice_rows, half_width = depth // cols, width // 2
+    piece = lax.dynamic_slice(
+        out_weight[0], (col * slice_rows, core * half_width), (slice_rows, half_width)
+    )
     pieces = exchange(jnp.broadcast_to(piece[None], (rows, *piece.shape)), "row")
 
-    normed = normalize(tokens.astype(jnp.float32), token_gain[0]).astype(jnp.bfloat16)
     half_samples = sample_count // 2
-    halves = normed.reshape(2, half_samples * token_rows, width)
+    keep, give = normalized_halves(side.reshape(1), tokens, token_gain)
     neighbour = [(i, i ^ 1) for i in range(rows)]
-    given = lax.ppermute(jnp.where(side == 0, halves[1], halves[0]), "row", neighbour)
-    block = jnp.concatenate([jnp.where(side == 0, halves[0], halves[1]), given])
-    blocks = all_around(block, "row", 2)
+    given = lax.ppermute(give, "row", neighbour)
+    up = down = jnp.concatenate([keep, given])
+    blocks = [up] + [None] * (pairs - 1)
+    for step in range(1, pairs // 2 + 1):
+        up = shifted(up, "row", 2)
+        if step < pairs // 2:
+            down = shifted(down, "row", -2)
+            blocks[-step] = down
+        blocks[step] = up
 
     other_w = lax.ppermute(qkv_weight[0], "row", neighbour)
     own_first = side == core
@@ -189,11 +208,22 @@
     bias_a = bias_a.reshape(total, total)
     bias_b = lax.ppermute(bias_a, "samp", swap)
 
-    w_out = all_around(pieces, "col", 1)
-    w_out = w_out.transpose(1, 0, 2, 3).reshape(width, width)
-
-    info = jnp.stack([valid_len[0], side, core]).astype(jnp.int32)
-    attended = attend(info, blocks, w_pair, bias_a, bias_b, half_samples)
+    w_half, bit, place = pieces, cols // 2, 0
+    while bit:
+        other = lax.ppermute(w_half, "col", [(i, i ^ bit) for i in range(cols)])
+        low = (col & bit) == 0
+        w_half = jnp.stack(
+            [jnp.where(low, w_half, other), jnp.where(low, other, w_half)], axis=place
+        )
+        bit, place = bit // 2, place + 1
+    other = lax.ppermute(w_half, "samp", swap)
+    w_out = jnp.concatenate(
+        [jnp.where(core == 0, w_half, other), jnp.where(core == 0, other, w_half)], axis=-1
+    )
+    w_out = w_out.reshape(cols, rows, slice_rows, width).transpose(1, 0, 2, 3)
+    w_out = w_out.reshape(width, width)
+
+    attended = attend(info_1, info_2, blocks, w_pair, bias_a, bias_b, half_samples)
     back = exchange(attended, "row")
     back = back.reshape(pairs, 2, half_samples, token_rows, 2 * HEAD_DIM)
     back = back.transpose(1, 2, 3, 0, 4).reshape(sample_count * token_rows, width)

time: 195 us -> 201 us (1.031)
  waiting for transfers between devices: 48.2 us -> 69.9 us
  local copies, waits for them, and re-layouts: 18.7 us -> 6.46 us
  starting transfers between devices: 116 us -> 108 us
  other arithmetic: 2.91 us -> 5.83 us
    ppermute x14 -> x7, starting transfers between devices: 45.8 us -> 25.6 us  [shifted(): lax.ppermute(value, axis, [(i, (i + by) % size) for i in range(size)])]
    ppermute x1 -> x5, waiting for transfers between devices: 0.01 us -> 17.2 us  [the longest x3 17.2 us: per_device(): other = lax.ppermute(w_half, 'col', [(i, i ^ bit) for i in range(cols)])]
    all_to_all x4, waiting for transfers between devices: 27.5 us -> 42.2 us  [exchange(): lax.all_to_all(blocks, axis, split_axis=0, concat_axis=0, axis_index_grou...]
    ppermute x1 -> x5, starting transfers between devices: 3.64 us -> 16.6 us  [the longest x3 11.8 us: per_device(): other = lax.ppermute(w_half, 'col', [(i, i ^ bit) for i in range(cols)])]
    dynamic_update_slice x15 -> x0, local copies, waits for them, and re-layouts: 11.7 us -> none  [put(): return lax.dynamic_update_slice(whole, value[None], start)]
    ppermute x14 -> x7, waiting for transfers between devices: 20.7 us -> 10.5 us  [shifted(): lax.ppermute(value, axis, [(i, (i + by) % size) for i in range(size)])]
    another operation x1 -> x8, other arithmetic: 0.08 us -> 2.31 us  [the longest x6 2.16 us: per_device(): jnp.stack([jnp.where(low, w_half, other), jnp.where(low, other, w_half)],...]
  transfers between devices with their start and end apart: 21 -> 18, of which waited for: 10 -> 9; matrix products, arithmetic and copies ran while one was open for 9% -> 3% of each run, Pallas kernels for 3% -> 3%
where the time goes in v5:
time: 201 us; the launch traced here: 200 us
  starting transfers between devices  108 us (54%)
  waiting for transfers between devices  69.9 us (35%)
  Pallas kernels  6.86 us (3%)
  local copies, waits for them, and re-layouts  6.46 us (3%)
  other arithmetic  5.83 us (3%)
  matrix products  2.17 us (1%)
    all_to_all x4, starting transfers between devices, exchange(): lax.all_to_all(blocks, axis, split_axis=0, concat_axis=0, axis_index_grou...  60.7 us
    all_to_all x4, waiting for transfers between devices, exchange(): lax.all_to_all(blocks, axis, split_axis=0, concat_axis=0, axis_index_grou...  42.2 us
    ppermute x7, starting transfers between devices, shifted(): lax.ppermute(value, axis, [(i, (i + by) % size) for i in range(size)])  25.6 us
    ppermute x3, waiting for transfers between devices, per_device(): other = lax.ppermute(w_half, 'col', [(i, i ^ bit) for i in range(cols)])  17.2 us
    ppermute x3, starting transfers between devices, per_device(): other = lax.ppermute(w_half, 'col', [(i, i ^ bit) for i in range(cols)])  11.8 us
    ppermute x7, waiting for transfers between devices, shifted(): lax.ppermute(value, axis, [(i, (i + by) % size) for i in range(size)])  10.5 us
    pallas_call x1, Pallas kernels, attend(): pl.pallas_call(functools.partial(attend_kernel, samples=samples, scale=1....  5.02 us
  transfers between devices with their start and end apart: 18, of which 9 were waited for; matrix products, arithmetic and copies ran while one was open for 3% of the time, Pallas kernels for 3%

profile of v5, /device:TPU:80, one launch (start us, length us, event | category | flops | bytes accessed | tf_op | source)
XLA Modules:
  0.0 200.2 jit_solution(8541601999920777925)
XLA Ops:
  3.6 43.7 %all-to-all-start = ((f32[16,2,1024]{2,1,0:T(2,128)}), f32[16,2,1024]{2,1,0:T(2,128)S(1)}, u32[]{:S(2)}, u32[]{:S(2)}) async-start(f32[16,2,1024]{2,1,0:T(2,128)} %bitcast.10), calls=%async_computation | async-start | bytes 262144 | tf_op jit(solution)/shard_map/all_to_all | solution.py:25
  47.4 14.5 %all-to-all-done = f32[16,2,1024]{2,1,0:T(2,128)S(1)} async-done(((f32[16,2,1024]{2,1,0:T(2,128)}), f32[16,2,1024]{2,1,0:T(2,128)S(1)}, u32[]{:S(2)}, u32[]{:S(2)}) %all-to-all-start) | async-done | bytes 131104 | tf_op jit(solution)/shard_map/all_to_all | solution.py:25
  62.5 4.0 %all-to-all-start.3 = ((bf16[16,6,384]{2,1,0:T(8,128)(2,1)}), bf16[16,6,384]{2,1,0:T(8,128)(2,1)S(1)}, u32[]{:S(2)}, u32[]{:S(2)}) async-start(bf16[16,6,384]{2,1,0:T(8,128)(2,1)} %broadcast_in_dim.40), calls=%async_computation.3 | async-start | bytes 196608 | tf_op jit(solution)/shard_map/all_to_all | solution.py:25
  66.9 12.9 %all-to-all-done.3 = bf16[16,6,384]{2,1,0:T(8,128)(2,1)S(1)} async-done(((bf16[16,6,384]{2,1,0:T(8,128)(2,1)}), bf16[16,6,384]{2,1,0:T(8,128)(2,1)S(1)}, u32[]{:S(2)}, u32[]{:S(2)}) %all-to-all-start.3) | async-done | bytes 73760 | tf_op jit(solution)/shard_map/all_to_all | solution.py:25
  80.9 7.6 %all-to-all-start.1 = ((f32[16,32,512]{2,1,0:T(8,128)}), f32[16,32,512]{2,1,0:T(8,128)S(1)}, u32[]{:S(2)}, u32[]{:S(2)}) async-start(f32[16,32,512]{2,1,0:T(8,128)} %bitcast.13), calls=%async_computation.1 | async-start | bytes 2097152 | tf_op jit(solution)/shard_map/all_to_all | solution.py:25
  90.4 2.9 %collective-permute-start = (bf16[64,768]{1,0:T(8,128)(2,1)}, bf16[64,768]{1,0:T(8,128)(2,1)S(1)}, u32[]{:S(2)}, u32[]{:S(2)}) collective-permute-start(bf16[64,768]{1,0:T(8,128)(2,1)} %get-tuple-element.8), channel_id=1, source_target_pairs={{0,16},{16,0},{32,48},{48,32},{64,80},{80,64},{96,112},{112,96},{1... | collective-permute-start | bytes 294920 | tf_op jit(solution)/shard_map/ppermute | solution.py:184
  94.2 7.6 %collective-permute-start.10 = (bf16[16,6,384]{2,0,1:T(8,128)(2,1)S(1)}, bf16[16,6,384]{2,0,1:T(8,128)(2,1)S(1)}, u32[]{:S(2)}, u32[]{:S(2)}) collective-permute-start(bf16[16,6,384]{2,0,1:T(8,128)(2,1)S(1)} %copy.42), channel_id=1, source_target_pairs={{0,8},{2,10},{4,12},{6,14},{8,0},{10,2},{12,4},{14,6},{1,9},{3,11}... | collective-permute-start | bytes 221192 | tf_op jit(solution)/shard_map/ppermute | solution.py:213
  101.8 2.7 %collective-permute-start.1 = (bf16[128,768]{1,0:T(8,128)(2,1)S(1)}, bf16[128,768]{1,0:T(8,128)(2,1)S(1)}, u32[]{:S(2)}, u32[]{:S(2)}) collective-permute-start(bf16[128,768]{1,0:T(8,128)(2,1)S(1)} %constant_dynamic-update-slice_fusion.refs_0_), channel_id=1, source_target_pairs={{0,32},{16,48},{32,64},{48,80},{64,96},{80,112},{96,128},{112,144}... | collective-permute-start | bytes 589832 | tf_op jit(solution)/shard_map/ppermute | solution.py:169
  104.5 15.4 %collective-permute-done.10 = bf16[16,6,384]{2,0,1:T(8,128)(2,1)S(1)} collective-permute-done((bf16[16,6,384]{2,0,1:T(8,128)(2,1)S(1)}, bf16[16,6,384]{2,0,1:T(8,128)(2,1)S(1)}, u32[]{:S(2)}, u32[]{:S(2)}) %collective-permute-start.10) | collective-permute-done | bytes 73760 | tf_op jit(solution)/shard_map/ppermute | solution.py:213
  120.0 2.2 %collective-permute-start.11 = (bf16[2,16,6,384]{3,1,2,0:T(8,128)(2,1)S(1)}, bf16[2,16,6,384]{3,1,2,0:T(8,128)(2,1)S(1)}, u32[]{:S(2)}, u32[]{:S(2)}) collective-permute-start(bf16[2,16,6,384]{3,1,2,0:T(8,128)(2,1)S(1)} %pad_maximum_fusion.4), channel_id=1, source_target_pairs={{0,4},{2,6},{4,0},{6,2},{8,12},{10,14},{12,8},{14,10},{1,5},{3,7},... | collective-permute-start | bytes 442376 | tf_op jit(solution)/shard_map/ppermute | solution.py:213
  122.2 3.1 %collective-permute-start.5 = (bf16[128,768]{1,0:T(8,128)(2,1)S(1)}, bf16[128,768]{1,0:T(8,128)(2,1)S(1)}, u32[]{:S(2)}, u32[]{:S(2)}) collective-permute-start(bf16[128,768]{1,0:T(8,128)(2,1)S(1)} %constant_dynamic-update-slice_fusion.refs_0_), channel_id=1, source_target_pairs={{0,224},{16,240},{32,0},{48,16},{64,32},{80,48},{96,64},{112,80},{... | collective-permute-start | bytes 589832 | tf_op jit(solution)/shard_map/ppermute | solution.py:169
  125.3 3.7 %collective-permute-start.2 = (bf16[128,768]{1,0:T(8,128)(2,1)S(1)}, bf16[128,768]{1,0:T(8,128)(2,1)S(1)}, u32[]{:S(2)}, u32[]{:S(2)}) collective-permute-start(bf16[128,768]{1,0:T(8,128)(2,1)S(1)} %collective-permute-done.1.refs_1_), channel_id=1, source_target_pairs={{0,32},{16,48},{32,64},{48,80},{64,96},{80,112},{96,128},{112,144}... | collective-permute-start | bytes 589832 | tf_op jit(solution)/shard_map/ppermute | solution.py:169
  130.9 2.0 collective-permute-start.9
  132.9 2.0 %collective-permute-start.12 = (bf16[2,2,16,6,384]{4,2,3,1,0:T(8,128)(2,1)S(1)}, bf16[2,2,16,6,384]{4,2,3,1,0:T(8,128)(2,1)}, u32[]{:S(2)}, u32[]{:S(2)}) collective-permute-start(bf16[2,2,16,6,384]{4,2,3,1,0:T(8,128)(2,1)S(1)} %pad_maximum_fusion.3), channel_id=1, source_target_pairs={{0,2},{2,0},{4,6},{6,4},{8,10},{10,8},{12,14},{14,12},{1,3},{3,1},... | collective-permute-start | bytes 884744 | tf_op jit(solution)/shard_map/ppermute | solution.py:213
  134.9 2.9 %collective-permute-start.8 = (bf16[3,768,48]{1,2,0:T(8,128)(2,1)}, bf16[3,768,48]{1,2,0:T(8,128)(2,1)}, u32[]{:S(2)}, u32[]{:S(2)}) collective-permute-start(bf16[3,768,48]{1,2,0:T(8,128)(2,1)} %bitcast.61), channel_id=1, source_target_pairs={{0,16},{16,0},{32,48},{48,32},{64,80},{80,64},{96,112},{112,96},{1... | collective-permute-start | bytes 663560 | tf_op jit(solution)/shard_map/ppermute | solution.py:194
  138.5 5.3 %collective-permute-start.6 = (bf16[128,768]{1,0:T(8,128)(2,1)S(1)}, bf16[128,768]{1,0:T(8,128)(2,1)S(1)}, u32[]{:S(2)}, u32[]{:S(2)}) collective-permute-start(bf16[128,768]{1,0:T(8,128)(2,1)S(1)} %collective-permute-done.5.refs_7_), channel_id=1, source_target_pairs={{0,224},{16,240},{32,0},{48,16},{64,32},{80,48},{96,64},{112,80},{... | collective-permute-start | bytes 589832 | tf_op jit(solution)/shard_map/ppermute | solution.py:169
  143.9 2.0 collective-permute-start.3
  146.0 3.0 %collective-permute-done.6.refs_6_ = bf16[128,768]{1,0:T(8,128)(2,1)S(1)} collective-permute-done((bf16[128,768]{1,0:T(8,128)(2,1)S(1)}, bf16[128,768]{1,0:T(8,128)(2,1)S(1)}, u32[]{:S(2)}, u32[]{:S(2)}) %collective-permute-start.6) | collective-permute-done | bytes 196640 | tf_op jit(solution)/shard_map/ppermute | solution.py:169
  149.0 6.2 %collective-permute-start.7 = (bf16[128,768]{1,0:T(8,128)(2,1)S(1)}, bf16[128,768]{1,0:T(8,128)(2,1)S(1)}, u32[]{:S(2)}, u32[]{:S(2)}) collective-permute-start(bf16[128,768]{1,0:T(8,128)(2,1)S(1)} %collective-permute-done.6.refs_6_), channel_id=1, source_target_pairs={{0,224},{16,240},{32,0},{48,16},{64,32},{80,48},{96,64},{112,80},{... | collective-permute-start | bytes 589832 | tf_op jit(solution)/shard_map/ppermute | solution.py:169
  156.8 2.6 %collective-permute-start.4 = (bf16[128,768]{1,0:T(8,128)(2,1)S(1)}, bf16[128,768]{1,0:T(8,128)(2,1)S(1)}, u32[]{:S(2)}, u32[]{:S(2)}) collective-permute-start(bf16[128,768]{1,0:T(8,128)(2,1)S(1)} %collective-permute-done.3.refs_3_), channel_id=1, source_target_pairs={{0,32},{16,48},{32,64},{48,80},{64,96},{80,112},{96,128},{112,144}... | collective-permute-start | bytes 589832 | tf_op jit(solution)/shard_map/ppermute | solution.py:169
  165.2 5.1 %collective-permute-done.4.refs_4_ = bf16[128,768]{1,0:T(8,128)(2,1)S(1)} collective-permute-done((bf16[128,768]{1,0:T(8,128)(2,1)S(1)}, bf16[128,768]{1,0:T(8,128)(2,1)S(1)}, u32[]{:S(2)}, u32[]{:S(2)}) %collective-permute-start.4) | collective-permute-done | bytes 196640 | tf_op jit(solution)/shard_map/ppermute | solution.py:169
  170.4 5.0 %attend.1 = bf16[16,2,32,96]{3,2,1,0:T(8,128)(2,1)} custom-call(s32[2]{0:T(128)S(1)} %pad_add_fusion.info_1_ref, s32[3]{0:T(128)S(1)} %pad_add_fusion.1.info_2_ref, bf16[128,768]{1,0:T(8,128)(2,1)S(1)} %constant_dynamic-update-slice_fusion.refs_0_, bf16[128,768]{1,0:T(8,128)(2,1)S(1)} %collective-permute-done.1.refs_1_, ...), custom_call_target="tpu_custom_call" | custom-call | flops 654311424 | bytes 6291456 | tf_op jit(solution)/shard_map/attend/pallas_call | solution.py:128
  175.4 5.4 %all-to-all-start.2 = ((bf16[16,2,32,96]{3,2,1,0:T(8,128)(2,1)}), bf16[16,2,32,96]{3,2,1,0:T(8,128)(2,1)}, u32[]{:S(2)}, u32[]{:S(2)}) async-start(bf16[16,2,32,96]{3,2,1,0:T(8,128)(2,1)} %attend.1), calls=%async_computation.2 | async-start | bytes 524288 | tf_op jit(solution)/shard_map/all_to_all | solution.py:25
  183.0 14.8 %all-to-all-done.2 = bf16[16,2,32,96]{3,2,1,0:T(8,128)(2,1)} async-done(((bf16[16,2,32,96]{3,2,1,0:T(8,128)(2,1)}), bf16[16,2,32,96]{3,2,1,0:T(8,128)(2,1)}, u32[]{:S(2)}, u32[]{:S(2)}) %all-to-all-start.2) | async-done | bytes 196640 | tf_op jit(solution)/shard_map/all_to_all | solution.py:25
  (71 shorter events, 22.5 us)
Async XLA Ops:
  0.0 47.3 %copy-start = (bf16[1,48,768]{2,1,0:T(8,128)(2,1)S(1)}, bf16[1,48,768]{2,1,0:T(8,128)(2,1)}, u32[]{:S(2)}) copy-start(bf16[1,48,768]{2,1,0:T(8,128)(2,1)} %param.19) | copy-start | bytes 221188
  0.0 1.5 copy-start.5
  3.6 58.3 %all-to-all-start = ((f32[16,2,1024]{2,1,0:T(2,128)}), f32[16,2,1024]{2,1,0:T(2,128)S(1)}, u32[]{:S(2)}, u32[]{:S(2)}) async-start(f32[16,2,1024]{2,1,0:T(2,128)} %bitcast.10), calls=%async_computation | async-start | bytes 262144 | tf_op jit(solution)/shard_map/all_to_all | solution.py:25
  62.5 17.3 %all-to-all-start.3 = ((bf16[16,6,384]{2,1,0:T(8,128)(2,1)}), bf16[16,6,384]{2,1,0:T(8,128)(2,1)S(1)}, u32[]{:S(2)}, u32[]{:S(2)}) async-start(bf16[16,6,384]{2,1,0:T(8,128)(2,1)} %broadcast_in_dim.40), calls=%async_computation.3 | async-start | bytes 196608 | tf_op jit(solution)/shard_map/all_to_all | solution.py:25
  80.9 50.0 %all-to-all-start.1 = ((f32[16,32,512]{2,1,0:T(8,128)}), f32[16,32,512]{2,1,0:T(8,128)S(1)}, u32[]{:S(2)}, u32[]{:S(2)}) async-start(f32[16,32,512]{2,1,0:T(8,128)} %bitcast.13), calls=%async_computation.1 | async-start | bytes 2097152 | tf_op jit(solution)/shard_map/all_to_all | solution.py:25
  90.4 11.4 %collective-permute-start = (bf16[64,768]{1,0:T(8,128)(2,1)}, bf16[64,768]{1,0:T(8,128)(2,1)S(1)}, u32[]{:S(2)}, u32[]{:S(2)}) collective-permute-start(bf16[64,768]{1,0:T(8,128)(2,1)} %get-tuple-element.8), channel_id=1, source_target_pairs={{0,16},{16,0},{32,48},{48,32},{64,80},{80,64},{96,112},{112,96},{1... | collective-permute-start | bytes 294920 | tf_op jit(solution)/shard_map/ppermute | solution.py:184
  94.2 25.7 %collective-permute-start.10 = (bf16[16,6,384]{2,0,1:T(8,128)(2,1)S(1)}, bf16[16,6,384]{2,0,1:T(8,128)(2,1)S(1)}, u32[]{:S(2)}, u32[]{:S(2)}) collective-permute-start(bf16[16,6,384]{2,0,1:T(8,128)(2,1)S(1)} %copy.42), channel_id=1, source_target_pairs={{0,8},{2,10},{4,12},{6,14},{8,0},{10,2},{12,4},{14,6},{1,9},{3,11}... | collective-permute-start | bytes 221192 | tf_op jit(solution)/shard_map/ppermute | solution.py:213
  101.8 23.5 %collective-permute-start.1 = (bf16[128,768]{1,0:T(8,128)(2,1)S(1)}, bf16[128,768]{1,0:T(8,128)(2,1)S(1)}, u32[]{:S(2)}, u32[]{:S(2)}) collective-permute-start(bf16[128,768]{1,0:T(8,128)(2,1)S(1)} %constant_dynamic-update-slice_fusion.refs_0_), channel_id=1, source_target_pairs={{0,32},{16,48},{32,64},{48,80},{64,96},{80,112},{96,128},{112,144}... | collective-permute-start | bytes 589832 | tf_op jit(solution)/shard_map/ppermute | solution.py:169
  120.0 10.9 %collective-permute-start.11 = (bf16[2,16,6,384]{3,1,2,0:T(8,128)(2,1)S(1)}, bf16[2,16,6,384]{3,1,2,0:T(8,128)(2,1)S(1)}, u32[]{:S(2)}, u32[]{:S(2)}) collective-permute-start(bf16[2,16,6,384]{3,1,2,0:T(8,128)(2,1)S(1)} %pad_maximum_fusion.4), channel_id=1, source_target_pairs={{0,4},{2,6},{4,0},{6,2},{8,12},{10,14},{12,8},{14,10},{1,5},{3,7},... | collective-permute-start | bytes 442376 | tf_op jit(solution)/shard_map/ppermute | solution.py:213
  122.2 16.3 %collective-permute-start.5 = (bf16[128,768]{1,0:T(8,128)(2,1)S(1)}, bf16[128,768]{1,0:T(8,128)(2,1)S(1)}, u32[]{:S(2)}, u32[]{:S(2)}) collective-permute-start(bf16[128,768]{1,0:T(8,128)(2,1)S(1)} %constant_dynamic-update-slice_fusion.refs_0_), channel_id=1, source_target_pairs={{0,224},{16,240},{32,0},{48,16},{64,32},{80,48},{96,64},{112,80},{... | collective-permute-start | bytes 589832 | tf_op jit(solution)/shard_map/ppermute | solution.py:169
  125.3 18.6 %collective-permute-start.2 = (bf16[128,768]{1,0:T(8,128)(2,1)S(1)}, bf16[128,768]{1,0:T(8,128)(2,1)S(1)}, u32[]{:S(2)}, u32[]{:S(2)}) collective-permute-start(bf16[128,768]{1,0:T(8,128)(2,1)S(1)} %collective-permute-done.1.refs_1_), channel_id=1, source_target_pairs={{0,32},{16,48},{32,64},{48,80},{64,96},{80,112},{96,128},{112,144}... | collective-permute-start | bytes 589832 | tf_op jit(solution)/shard_map/ppermute | solution.py:169
  130.9 28.5 %copy-start.1 = (bf16[2,1,16,6,384]{4,2,3,1,0:T(8,128)(2,1)}, bf16[2,1,16,6,384]{4,2,3,1,0:T(8,128)(2,1)S(1)}, u32[]{:S(2)}) copy-start(bf16[2,1,16,6,384]{4,2,3,1,0:T(8,128)(2,1)S(1)} %get-tuple-element.15) | copy-start | bytes 442372
  130.9 28.5 %copy-start.2 = (bf16[2,1,16,6,384]{4,2,3,1,0:T(8,128)(2,1)}, bf16[2,1,16,6,384]{4,2,3,1,0:T(8,128)(2,1)S(1)}, u32[]{:S(2)}) copy-start(bf16[2,1,16,6,384]{4,2,3,1,0:T(8,128)(2,1)S(1)} %get-tuple-element.16) | copy-start | bytes 442372
  130.9 39.5 %collective-permute-start.9 = (f32[512,512]{1,0:T(8,128)S(1)}, f32[512,512]{1,0:T(8,128)S(1)}, u32[]{:S(2)}, u32[]{:S(2)}) collective-permute-start(f32[512,512]{1,0:T(8,128)S(1)} %bitcast.56), channel_id=1, source_target_pairs={{0,1},{1,0},{2,3},{3,2},{4,5},{5,4},{6,7},{7,6},{8,9},{9,8},{10,11... | collective-permute-start | bytes 3145736 | tf_op jit(solution)/shard_map/ppermute | solution.py:209
  132.9 26.5 %collective-permute-start.12 = (bf16[2,2,16,6,384]{4,2,3,1,0:T(8,128)(2,1)S(1)}, bf16[2,2,16,6,384]{4,2,3,1,0:T(8,128)(2,1)}, u32[]{:S(2)}, u32[]{:S(2)}) collective-permute-start(bf16[2,2,16,6,384]{4,2,3,1,0:T(8,128)(2,1)S(1)} %pad_maximum_fusion.3), channel_id=1, source_target_pairs={{0,2},{2,0},{4,6},{6,4},{8,10},{10,8},{12,14},{14,12},{1,3},{3,1},... | collective-permute-start | bytes 884744 | tf_op jit(solution)/shard_map/ppermute | solution.py:213
  134.9 28.5 %collective-permute-start.8 = (bf16[3,768,48]{1,2,0:T(8,128)(2,1)}, bf16[3,768,48]{1,2,0:T(8,128)(2,1)}, u32[]{:S(2)}, u32[]{:S(2)}) collective-permute-start(bf16[3,768,48]{1,2,0:T(8,128)(2,1)} %bitcast.61), channel_id=1, source_target_pairs={{0,16},{16,0},{32,48},{48,32},{64,80},{80,64},{96,112},{112,96},{1... | collective-permute-start | bytes 663560 | tf_op jit(solution)/shard_map/ppermute | solution.py:194
  138.5 10.4 %collective-permute-start.6 = (bf16[128,768]{1,0:T(8,128)(2,1)S(1)}, bf16[128,768]{1,0:T(8,128)(2,1)S(1)}, u32[]{:S(2)}, u32[]{:S(2)}) collective-permute-start(bf16[128,768]{1,0:T(8,128)(2,1)S(1)} %collective-permute-done.5.refs_7_), channel_id=1, source_target_pairs={{0,224},{16,240},{32,0},{48,16},{64,32},{80,48},{96,64},{112,80},{... | collective-permute-start | bytes 589832 | tf_op jit(solution)/shard_map/ppermute | solution.py:169
  143.9 13.0 %collective-permute-start.3 = (bf16[128,768]{1,0:T(8,128)(2,1)S(1)}, bf16[128,768]{1,0:T(8,128)(2,1)S(1)}, u32[]{:S(2)}, u32[]{:S(2)}) collective-permute-start(bf16[128,768]{1,0:T(8,128)(2,1)S(1)} %collective-permute-done.2.refs_2_), channel_id=1, source_target_pairs={{0,32},{16,48},{32,64},{48,80},{64,96},{80,112},{96,128},{112,144}... | collective-permute-start | bytes 589832 | tf_op jit(solution)/shard_map/ppermute | solution.py:169
  146.0 17.4 %copy-start.4 = (bf16[1,3,768,48]{2,3,1,0:T(8,128)(2,1)S(1)}, bf16[1,3,768,48]{2,3,1,0:T(8,128)(2,1)}, u32[]{:S(2)}) copy-start(bf16[1,3,768,48]{2,3,1,0:T(8,128)(2,1)} %param.18) | copy-start | bytes 663556
  149.0 16.3 %collective-permute-start.7 = (bf16[128,768]{1,0:T(8,128)(2,1)S(1)}, bf16[128,768]{1,0:T(8,128)(2,1)S(1)}, u32[]{:S(2)}, u32[]{:S(2)}) collective-permute-start(bf16[128,768]{1,0:T(8,128)(2,1)S(1)} %collective-permute-done.6.refs_6_), channel_id=1, source_target_pairs={{0,224},{16,240},{32,0},{48,16},{64,32},{80,48},{96,64},{112,80},{... | collective-permute-start | bytes 589832 | tf_op jit(solution)/shard_map/ppermute | solution.py:169
  156.8 13.5 %collective-permute-start.4 = (bf16[128,768]{1,0:T(8,128)(2,1)S(1)}, bf16[128,768]{1,0:T(8,128)(2,1)S(1)}, u32[]{:S(2)}, u32[]{:S(2)}) collective-permute-start(bf16[128,768]{1,0:T(8,128)(2,1)S(1)} %collective-permute-done.3.refs_3_), channel_id=1, source_target_pairs={{0,32},{16,48},{32,64},{48,80},{64,96},{80,112},{96,128},{112,144}... | collective-permute-start | bytes 589832 | tf_op jit(solution)/shard_map/ppermute | solution.py:169
  161.5 19.3 %collective-permute-start.13 = (bf16[2,2,2,16,6,384]{5,3,4,2,1,0:T(8,128)(2,1)}, bf16[2,2,2,16,6,384]{5,3,4,2,1,0:T(8,128)(2,1)}, u32[]{:S(2)}, u32[]{:S(2)}) collective-permute-start(bf16[2,2,2,16,6,384]{5,3,4,2,1,0:T(8,128)(2,1)} %pad_maximum_fusion.1), channel_id=1, source_target_pairs={{0,1},{1,0},{2,3},{3,2},{4,5},{5,4},{6,7},{7,6},{8,9},{9,8},{10,11... | collective-permute-start | bytes 1769480 | tf_op jit(solution)/shard_map/ppermute | solution.py:219
  175.4 22.4 %all-to-all-start.2 = ((bf16[16,2,32,96]{3,2,1,0:T(8,128)(2,1)}), bf16[16,2,32,96]{3,2,1,0:T(8,128)(2,1)}, u32[]{:S(2)}, u32[]{:S(2)}) async-start(bf16[16,2,32,96]{3,2,1,0:T(8,128)(2,1)} %attend.1), calls=%async_computation.2 | async-start | bytes 524288 | tf_op jit(solution)/shard_map/all_to_all | solution.py:25
  182.6 16.6 %copy-start.3 = (bf16[4,32,768]{2,1,0:T(8,128)(2,1)S(1)}, bf16[4,32,768]{2,1,0:T(8,128)(2,1)}, u32[]{:S(2)}) copy-start(bf16[4,32,768]{2,1,0:T(8,128)(2,1)} %tokens_ref.1) | copy-start | bytes 589828
  (3 other events, 4.3 us)

commit v6 on v5

--- a/solution.py
+++ b/solution.py
@@ -208,14 +208,8 @@
     bias_a = bias_a.reshape(total, total)
     bias_b = lax.ppermute(bias_a, "samp", swap)
 
-    w_half, bit, place = pieces, cols // 2, 0
-    while bit:
-        other = lax.ppermute(w_half, "col", [(i, i ^ bit) for i in range(cols)])
-        low = (col & bit) == 0
-        w_half = jnp.stack(
-            [jnp.where(low, w_half, other), jnp.where(low, other, w_half)], axis=place
-        )
-        bit, place = bit // 2, place + 1
+    pieces = pieces.reshape(1, rows * slice_rows, half_width)
+    w_half = exchange(jnp.broadcast_to(pieces, (cols, *pieces.shape[1:])), "col")
     other = lax.ppermute(w_half, "samp", swap)
     w_out = jnp.concatenate(
         [jnp.where(core == 0, w_half, other), jnp.where(core == 0, other, w_half)], axis=-1

time: 201 us -> 216 us (1.075)
  waiting for transfers between devices: 69.9 us -> 89.7 us
  starting transfers between devices: 108 us -> 102 us
    all_to_all x4 -> x5, waiting for transfers between devices: 42.2 us -> 69.4 us  [exchange(): lax.all_to_all(blocks, axis, split_axis=0, concat_axis=0, axis_index_grou...]
    ppermute x3 -> x0, waiting for transfers between devices: 17.2 us -> none  [per_device(): other = lax.ppermute(w_half, 'col', [(i, i ^ bit) for i in range(cols)])]
    ppermute x3 -> x0, starting transfers between devices: 11.8 us -> none  [per_device(): other = lax.ppermute(w_half, 'col', [(i, i ^ bit) for i in range(cols)])]
    ppermute x7, waiting for transfers between devices: 10.5 us -> 19.9 us  [shifted(): lax.ppermute(value, axis, [(i, (i + by) % size) for i in range(size)])]
    all_to_all x4 -> x5, starting transfers between devices: 60.7 us -> 65 us  [exchange(): lax.all_to_all(blocks, axis, split_axis=0, concat_axis=0, axis_index_grou...]
    another operation x6 -> x0, other arithmetic: 2.16 us -> none  [per_device(): jnp.stack([jnp.where(low, w_half, other), jnp.where(low, other, w_half)],...]
  transfers between devices with their start and end apart: 18 -> 16, of which waited for: 9 -> 10; matrix products, arithmetic and copies ran while one was open for 3% -> 3% of each run, Pallas kernels for 3% -> 3%
where the time goes in v6:
time: 216 us; the launch traced here: 215 us
  starting transfers between devices  102 us (47%)
  waiting for transfers between devices  89.7 us (42%)
  local copies, waits for them, and re-layouts  8.41 us (4%)
  Pallas kernels  7.22 us (3%)
  other arithmetic  4.03 us (2%)
  matrix products  2.17 us (1%)
    all_to_all x5, waiting for transfers between devices, exchange(): lax.all_to_all(blocks, axis, split_axis=0, concat_axis=0, axis_index_grou...  69.4 us
    all_to_all x5, starting transfers between devices, exchange(): lax.all_to_all(blocks, axis, split_axis=0, concat_axis=0, axis_index_grou...  65 us
    ppermute x7, starting transfers between devices, shifted(): lax.ppermute(value, axis, [(i, (i + by) % size) for i in range(size)])  26.9 us
    ppermute x7, waiting for transfers between devices, shifted(): lax.ppermute(value, axis, [(i, (i + by) % size) for i in range(size)])  19.9 us
    pallas_call x1, Pallas kernels, attend(): pl.pallas_call(functools.partial(attend_kernel, samples=samples, scale=1....  5.39 us
  transfers between devices with their start and end apart: 16, of which 10 were waited for; matrix products, arithmetic and copies ran while one was open for 3% of the time, Pallas kernels for 3%

profile of v6, /device:TPU:80, one launch (start us, length us, event | category | flops | bytes accessed | tf_op | source)
XLA Modules:
  0.0 214.7 jit_solution(9184672902121344964)
XLA Ops:
  3.6 43.7 %all-to-all-start = ((f32[16,2,1024]{2,1,0:T(2,128)}), f32[16,2,1024]{2,1,0:T(2,128)S(1)}, u32[]{:S(2)}, u32[]{:S(2)}) async-start(f32[16,2,1024]{2,1,0:T(2,128)} %bitcast.10), calls=%async_computation | async-start | bytes 262144 | tf_op jit(solution)/shard_map/all_to_all | solution.py:25
  47.4 14.5 %all-to-all-done = f32[16,2,1024]{2,1,0:T(2,128)S(1)} async-done(((f32[16,2,1024]{2,1,0:T(2,128)}), f32[16,2,1024]{2,1,0:T(2,128)S(1)}, u32[]{:S(2)}, u32[]{:S(2)}) %all-to-all-start) | async-done | bytes 131104 | tf_op jit(solution)/shard_map/all_to_all | solution.py:25
  62.5 4.0 %all-to-all-start.3 = ((bf16[16,6,384]{2,1,0:T(8,128)(2,1)}), bf16[16,6,384]{2,1,0:T(8,128)(2,1)S(1)}, u32[]{:S(2)}, u32[]{:S(2)}) async-start(bf16[16,6,384]{2,1,0:T(8,128)(2,1)} %broadcast_in_dim.47), calls=%async_computation.3 | async-start | bytes 196608 | tf_op jit(solution)/shard_map/all_to_all | solution.py:25
  66.9 12.9 %all-to-all-done.3 = bf16[16,6,384]{2,1,0:T(8,128)(2,1)S(1)} async-done(((bf16[16,6,384]{2,1,0:T(8,128)(2,1)}), bf16[16,6,384]{2,1,0:T(8,128)(2,1)S(1)}, u32[]{:S(2)}, u32[]{:S(2)}) %all-to-all-start.3) | async-done | bytes 73760 | tf_op jit(solution)/shard_map/all_to_all | solution.py:25
  80.9 7.6 %all-to-all-start.1 = ((f32[16,32,512]{2,1,0:T(8,128)}), f32[16,32,512]{2,1,0:T(8,128)S(1)}, u32[]{:S(2)}, u32[]{:S(2)}) async-start(f32[16,32,512]{2,1,0:T(8,128)} %bitcast.13), calls=%async_computation.1 | async-start | bytes 2097152 | tf_op jit(solution)/shard_map/all_to_all | solution.py:25
  88.6 26.2 %all-to-all-done.1 = f32[16,32,512]{2,1,0:T(8,128)S(1)} async-done(((f32[16,32,512]{2,1,0:T(8,128)}), f32[16,32,512]{2,1,0:T(8,128)S(1)}, u32[]{:S(2)}, u32[]{:S(2)}) %all-to-all-start.1) | async-done | bytes 1048608 | tf_op jit(solution)/shard_map/all_to_all | solution.py:25
  115.7 4.8 %all-to-all-start.4 = ((bf16[8,96,384]{2,1,0:T(8,128)(2,1)}), bf16[8,96,384]{2,1,0:T(8,128)(2,1)}, u32[]{:S(2)}, u32[]{:S(2)}) async-start(bf16[8,96,384]{2,1,0:T(8,128)(2,1)} %broadcast_in_dim.49), calls=%async_computation.4 | async-start | bytes 1179648 | tf_op jit(solution)/shard_map/all_to_all | solution.py:25
  122.4 2.9 %collective-permute-start = (bf16[64,768]{1,0:T(8,128)(2,1)}, bf16[64,768]{1,0:T(8,128)(2,1)S(1)}, u32[]{:S(2)}, u32[]{:S(2)}) collective-permute-start(bf16[64,768]{1,0:T(8,128)(2,1)} %get-tuple-element.8), channel_id=1, source_target_pairs={{0,16},{16,0},{32,48},{48,32},{64,80},{80,64},{96,112},{112,96},{1... | collective-permute-start | bytes 294920 | tf_op jit(solution)/shard_map/ppermute | solution.py:184
  126.2 3.1 %collective-permute-start.9 = (f32[512,512]{1,0:T(8,128)S(1)}, f32[512,512]{1,0:T(8,128)S(1)}, u32[]{:S(2)}, u32[]{:S(2)}) collective-permute-start(f32[512,512]{1,0:T(8,128)S(1)} %bitcast.40), channel_id=1, source_target_pairs={{0,1},{1,0},{2,3},{3,2},{4,5},{5,4},{6,7},{7,6},{8,9},{9,8},{10,11... | collective-permute-start | bytes 3145736 | tf_op jit(solution)/shard_map/ppermute | solution.py:209
  129.7 2.7 %collective-permute-start.1 = (bf16[128,768]{1,0:T(8,128)(2,1)S(1)}, bf16[128,768]{1,0:T(8,128)(2,1)S(1)}, u32[]{:S(2)}, u32[]{:S(2)}) collective-permute-start(bf16[128,768]{1,0:T(8,128)(2,1)S(1)} %constant_dynamic-update-slice_fusion.refs_0_), channel_id=1, source_target_pairs={{0,32},{16,48},{32,64},{48,80},{64,96},{80,112},{96,128},{112,144}... | collective-permute-start | bytes 589832 | tf_op jit(solution)/shard_map/ppermute | solution.py:169
  132.5 5.3 %collective-permute-start.5 = (bf16[128,768]{1,0:T(8,128)(2,1)S(1)}, bf16[128,768]{1,0:T(8,128)(2,1)S(1)}, u32[]{:S(2)}, u32[]{:S(2)}) collective-permute-start(bf16[128,768]{1,0:T(8,128)(2,1)S(1)} %constant_dynamic-update-slice_fusion.refs_0_), channel_id=1, source_target_pairs={{0,224},{16,240},{32,0},{48,16},{64,32},{80,48},{96,64},{112,80},{... | collective-permute-start | bytes 589832 | tf_op jit(solution)/shard_map/ppermute | solution.py:169
  137.7 7.7 %collective-permute-done.1.refs_1_ = bf16[128,768]{1,0:T(8,128)(2,1)S(1)} collective-permute-done((bf16[128,768]{1,0:T(8,128)(2,1)S(1)}, bf16[128,768]{1,0:T(8,128)(2,1)S(1)}, u32[]{:S(2)}, u32[]{:S(2)}) %collective-permute-start.1) | collective-permute-done | bytes 196640 | tf_op jit(solution)/shard_map/ppermute | solution.py:169
  147.4 2.4 %collective-permute-start.8 = (bf16[3,768,48]{1,2,0:T(8,128)(2,1)}, bf16[3,768,48]{1,2,0:T(8,128)(2,1)}, u32[]{:S(2)}, u32[]{:S(2)}) collective-permute-start(bf16[3,768,48]{1,2,0:T(8,128)(2,1)} %bitcast.3), channel_id=1, source_target_pairs={{0,16},{16,0},{32,48},{48,32},{64,80},{80,64},{96,112},{112,96},{1... | collective-permute-start | bytes 663560 | tf_op jit(solution)/shard_map/ppermute | solution.py:194
  150.5 6.0 %collective-permute-start.6 = (bf16[128,768]{1,0:T(8,128)(2,1)S(1)}, bf16[128,768]{1,0:T(8,128)(2,1)S(1)}, u32[]{:S(2)}, u32[]{:S(2)}) collective-permute-start(bf16[128,768]{1,0:T(8,128)(2,1)S(1)} %collective-permute-done.5.refs_7_), channel_id=1, source_target_pairs={{0,224},{16,240},{32,0},{48,16},{64,32},{80,48},{96,64},{112,80},{... | collective-permute-start | bytes 589832 | tf_op jit(solution)/shard_map/ppermute | solution.py:169
  156.5 4.9 %collective-permute-done.2.refs_2_ = bf16[128,768]{1,0:T(8,128)(2,1)S(1)} collective-permute-done((bf16[128,768]{1,0:T(8,128)(2,1)S(1)}, bf16[128,768]{1,0:T(8,128)(2,1)S(1)}, u32[]{:S(2)}, u32[]{:S(2)}) %collective-permute-start.2) | collective-permute-done | bytes 196640 | tf_op jit(solution)/shard_map/ppermute | solution.py:169
  163.9 7.0 %collective-permute-start.7 = (bf16[128,768]{1,0:T(8,128)(2,1)S(1)}, bf16[128,768]{1,0:T(8,128)(2,1)S(1)}, u32[]{:S(2)}, u32[]{:S(2)}) collective-permute-start(bf16[128,768]{1,0:T(8,128)(2,1)S(1)} %collective-permute-done.6.refs_6_), channel_id=1, source_target_pairs={{0,224},{16,240},{32,0},{48,16},{64,32},{80,48},{96,64},{112,80},{... | collective-permute-start | bytes 589832 | tf_op jit(solution)/shard_map/ppermute | solution.py:169
  171.0 2.5 %collective-permute-done.3.refs_3_ = bf16[128,768]{1,0:T(8,128)(2,1)S(1)} collective-permute-done((bf16[128,768]{1,0:T(8,128)(2,1)S(1)}, bf16[128,768]{1,0:T(8,128)(2,1)S(1)}, u32[]{:S(2)}, u32[]{:S(2)}) %collective-permute-start.3) | collective-permute-done | bytes 196640 | tf_op jit(solution)/shard_map/ppermute | solution.py:169
  173.5 1.9 collective-permute-start.4
  175.5 2.1 copy.23
  177.6 1.9 collective-permute-start.10
  180.7 4.3 %collective-permute-done.4.refs_4_ = bf16[128,768]{1,0:T(8,128)(2,1)} collective-permute-done((bf16[128,768]{1,0:T(8,128)(2,1)S(1)}, bf16[128,768]{1,0:T(8,128)(2,1)}, u32[]{:S(2)}, u32[]{:S(2)}) %collective-permute-start.4) | collective-permute-done | bytes 196640 | tf_op jit(solution)/shard_map/ppermute | solution.py:169
  185.0 5.4 %attend.1 = bf16[16,2,32,96]{3,2,1,0:T(8,128)(2,1)} custom-call(s32[2]{0:T(128)S(1)} %pad_add_fusion.info_1_ref, s32[3]{0:T(128)S(1)} %pad_add_fusion.1.info_2_ref, bf16[128,768]{1,0:T(8,128)(2,1)S(1)} %constant_dynamic-update-slice_fusion.refs_0_, bf16[128,768]{1,0:T(8,128)(2,1)S(1)} %collective-permute-done.1.refs_1_, ...), custom_call_target="tpu_custom_call" | custom-call | flops 654311424 | bytes 6291456 | tf_op jit(solution)/shard_map/attend/pallas_call | solution.py:128
  190.3 4.8 %all-to-all-start.2 = ((bf16[16,2,32,96]{3,2,1,0:T(8,128)(2,1)}), bf16[16,2,32,96]{3,2,1,0:T(8,128)(2,1)S(1)}, u32[]{:S(2)}, u32[]{:S(2)}) async-start(bf16[16,2,32,96]{3,2,1,0:T(8,128)(2,1)} %attend.1), calls=%async_computation.2 | async-start | bytes 524288 | tf_op jit(solution)/shard_map/all_to_all | solution.py:25
  197.5 15.8 %all-to-all-done.2 = bf16[16,2,32,96]{3,2,1,0:T(8,128)(2,1)S(1)} async-done(((bf16[16,2,32,96]{3,2,1,0:T(8,128)(2,1)}), bf16[16,2,32,96]{3,2,1,0:T(8,128)(2,1)S(1)}, u32[]{:S(2)}, u32[]{:S(2)}) %all-to-all-start.2) | async-done | bytes 196640 | tf_op jit(solution)/shard_map/all_to_all | solution.py:25
  (57 shorter events, 19.1 us)
Async XLA Ops:
  0.0 47.3 %copy-start = (bf16[1,48,768]{2,1,0:T(8,128)(2,1)S(1)}, bf16[1,48,768]{2,1,0:T(8,128)(2,1)}, u32[]{:S(2)}) copy-start(bf16[1,48,768]{2,1,0:T(8,128)(2,1)} %param.19) | copy-start | bytes 221188
  0.0 1.3 copy-start.4
  0.0 1.5 copy-start.2
  1.1 1.5 copy-start.3
  1.1 1.5 copy-start.5
  3.6 58.3 %all-to-all-start = ((f32[16,2,1024]{2,1,0:T(2,128)}), f32[16,2,1024]{2,1,0:T(2,128)S(1)}, u32[]{:S(2)}, u32[]{:S(2)}) async-start(f32[16,2,1024]{2,1,0:T(2,128)} %bitcast.10), calls=%async_computation | async-start | bytes 262144 | tf_op jit(solution)/shard_map/all_to_all | solution.py:25
  62.5 17.3 %all-to-all-start.3 = ((bf16[16,6,384]{2,1,0:T(8,128)(2,1)}), bf16[16,6,384]{2,1,0:T(8,128)(2,1)S(1)}, u32[]{:S(2)}, u32[]{:S(2)}) async-start(bf16[16,6,384]{2,1,0:T(8,128)(2,1)} %broadcast_in_dim.47), calls=%async_computation.3 | async-start | bytes 196608 | tf_op jit(solution)/shard_map/all_to_all | solution.py:25
  80.9 33.9 %all-to-all-start.1 = ((f32[16,32,512]{2,1,0:T(8,128)}), f32[16,32,512]{2,1,0:T(8,128)S(1)}, u32[]{:S(2)}, u32[]{:S(2)}) async-start(f32[16,32,512]{2,1,0:T(8,128)} %bitcast.13), calls=%async_computation.1 | async-start | bytes 2097152 | tf_op jit(solution)/shard_map/all_to_all | solution.py:25
  115.7 59.7 %all-to-all-start.4 = ((bf16[8,96,384]{2,1,0:T(8,128)(2,1)}), bf16[8,96,384]{2,1,0:T(8,128)(2,1)}, u32[]{:S(2)}, u32[]{:S(2)}) async-start(bf16[8,96,384]{2,1,0:T(8,128)(2,1)} %broadcast_in_dim.49), calls=%async_computation.4 | async-start | bytes 1179648 | tf_op jit(solution)/shard_map/all_to_all | solution.py:25
  122.4 7.3 %collective-permute-start = (bf16[64,768]{1,0:T(8,128)(2,1)}, bf16[64,768]{1,0:T(8,128)(2,1)S(1)}, u32[]{:S(2)}, u32[]{:S(2)}) collective-permute-start(bf16[64,768]{1,0:T(8,128)(2,1)} %get-tuple-element.8), channel_id=1, source_target_pairs={{0,16},{16,0},{32,48},{48,32},{64,80},{80,64},{96,112},{112,96},{1... | collective-permute-start | bytes 294920 | tf_op jit(solution)/shard_map/ppermute | solution.py:184
  126.2 58.8 %collective-permute-start.9 = (f32[512,512]{1,0:T(8,128)S(1)}, f32[512,512]{1,0:T(8,128)S(1)}, u32[]{:S(2)}, u32[]{:S(2)}) collective-permute-start(f32[512,512]{1,0:T(8,128)S(1)} %bitcast.40), channel_id=1, source_target_pairs={{0,1},{1,0},{2,3},{3,2},{4,5},{5,4},{6,7},{7,6},{8,9},{9,8},{10,11... | collective-permute-start | bytes 3145736 | tf_op jit(solution)/shard_map/ppermute | solution.py:209
  129.7 15.8 %collective-permute-start.1 = (bf16[128,768]{1,0:T(8,128)(2,1)S(1)}, bf16[128,768]{1,0:T(8,128)(2,1)S(1)}, u32[]{:S(2)}, u32[]{:S(2)}) collective-permute-start(bf16[128,768]{1,0:T(8,128)(2,1)S(1)} %constant_dynamic-update-slice_fusion.refs_0_), channel_id=1, source_target_pairs={{0,32},{16,48},{32,64},{48,80},{64,96},{80,112},{96,128},{112,144}... | collective-permute-start | bytes 589832 | tf_op jit(solution)/shard_map/ppermute | solution.py:169
  132.5 18.1 %collective-permute-start.5 = (bf16[128,768]{1,0:T(8,128)(2,1)S(1)}, bf16[128,768]{1,0:T(8,128)(2,1)S(1)}, u32[]{:S(2)}, u32[]{:S(2)}) collective-permute-start(bf16[128,768]{1,0:T(8,128)(2,1)S(1)} %constant_dynamic-update-slice_fusion.refs_0_), channel_id=1, source_target_pairs={{0,224},{16,240},{32,0},{48,16},{64,32},{80,48},{96,64},{112,80},{... | collective-permute-start | bytes 589832 | tf_op jit(solution)/shard_map/ppermute | solution.py:169
  145.5 15.9 %collective-permute-start.2 = (bf16[128,768]{1,0:T(8,128)(2,1)S(1)}, bf16[128,768]{1,0:T(8,128)(2,1)S(1)}, u32[]{:S(2)}, u32[]{:S(2)}) collective-permute-start(bf16[128,768]{1,0:T(8,128)(2,1)S(1)} %collective-permute-done.1.refs_1_), channel_id=1, source_target_pairs={{0,32},{16,48},{32,64},{48,80},{64,96},{80,112},{96,128},{112,144}... | collective-permute-start | bytes 589832 | tf_op jit(solution)/shard_map/ppermute | solution.py:169
  147.4 32.1 %collective-permute-start.8 = (bf16[3,768,48]{1,2,0:T(8,128)(2,1)}, bf16[3,768,48]{1,2,0:T(8,128)(2,1)}, u32[]{:S(2)}, u32[]{:S(2)}) collective-permute-start(bf16[3,768,48]{1,2,0:T(8,128)(2,1)} %bitcast.3), channel_id=1, source_target_pairs={{0,16},{16,0},{32,48},{48,32},{64,80},{80,64},{96,112},{112,96},{1... | collective-permute-start | bytes 663560 | tf_op jit(solution)/shard_map/ppermute | solution.py:194
  150.5 13.4 %collective-permute-start.6 = (bf16[128,768]{1,0:T(8,128)(2,1)S(1)}, bf16[128,768]{1,0:T(8,128)(2,1)S(1)}, u32[]{:S(2)}, u32[]{:S(2)}) collective-permute-start(bf16[128,768]{1,0:T(8,128)(2,1)S(1)} %collective-permute-done.5.refs_7_), channel_id=1, source_target_pairs={{0,224},{16,240},{32,0},{48,16},{64,32},{80,48},{96,64},{112,80},{... | collective-permute-start | bytes 589832 | tf_op jit(solution)/shard_map/ppermute | solution.py:169
  161.4 12.1 %collective-permute-start.3 = (bf16[128,768]{1,0:T(8,128)(2,1)S(1)}, bf16[128,768]{1,0:T(8,128)(2,1)S(1)}, u32[]{:S(2)}, u32[]{:S(2)}) collective-permute-start(bf16[128,768]{1,0:T(8,128)(2,1)S(1)} %collective-permute-done.2.refs_2_), channel_id=1, source_target_pairs={{0,32},{16,48},{32,64},{48,80},{64,96},{80,112},{96,128},{112,144}... | collective-permute-start | bytes 589832 | tf_op jit(solution)/shard_map/ppermute | solution.py:169
  163.9 16.7 %collective-permute-start.7 = (bf16[128,768]{1,0:T(8,128)(2,1)S(1)}, bf16[128,768]{1,0:T(8,128)(2,1)S(1)}, u32[]{:S(2)}, u32[]{:S(2)}) collective-permute-start(bf16[128,768]{1,0:T(8,128)(2,1)S(1)} %collective-permute-done.6.refs_6_), channel_id=1, source_target_pairs={{0,224},{16,240},{32,0},{48,16},{64,32},{80,48},{96,64},{112,80},{... | collective-permute-start | bytes 589832 | tf_op jit(solution)/shard_map/ppermute | solution.py:169
  173.5 11.4 %collective-permute-start.4 = (bf16[128,768]{1,0:T(8,128)(2,1)S(1)}, bf16[128,768]{1,0:T(8,128)(2,1)}, u32[]{:S(2)}, u32[]{:S(2)}) collective-permute-start(bf16[128,768]{1,0:T(8,128)(2,1)S(1)} %collective-permute-done.3.refs_3_), channel_id=1, source_target_pairs={{0,32},{16,48},{32,64},{48,80},{64,96},{80,112},{96,128},{112,144}... | collective-permute-start | bytes 589832 | tf_op jit(solution)/shard_map/ppermute | solution.py:169
  177.6 17.6 %collective-permute-start.10 = (bf16[8,96,384]{2,0,1:T(8,128)(2,1)}, bf16[8,96,384]{2,0,1:T(8,128)(2,1)}, u32[]{:S(2)}, u32[]{:S(2)}) collective-permute-start(bf16[8,96,384]{2,0,1:T(8,128)(2,1)} %copy.23), channel_id=1, source_target_pairs={{0,1},{1,0},{2,3},{3,2},{4,5},{5,4},{6,7},{7,6},{8,9},{9,8},{10,11... | collective-permute-start | bytes 1769480 | tf_op jit(solution)/shard_map/ppermute | solution.py:213
  190.3 23.0 %all-to-all-start.2 = ((bf16[16,2,32,96]{3,2,1,0:T(8,128)(2,1)}), bf16[16,2,32,96]{3,2,1,0:T(8,128)(2,1)S(1)}, u32[]{:S(2)}, u32[]{:S(2)}) async-start(bf16[16,2,32,96]{3,2,1,0:T(8,128)(2,1)} %attend.1), calls=%async_computation.2 | async-start | bytes 524288 | tf_op jit(solution)/shard_map/all_to_all | solution.py:25
  197.1 16.6 %copy-start.1 = (bf16[4,32,768]{2,1,0:T(8,128)(2,1)S(1)}, bf16[4,32,768]{2,1,0:T(8,128)(2,1)}, u32[]{:S(2)}) copy-start(bf16[4,32,768]{2,1,0:T(8,128)(2,1)} %tokens_ref.1) | copy-start | bytes 589828

commit v7 on v5

--- a/solution.py
+++ b/solution.py
@@ -176,7 +176,6 @@
     piece = lax.dynamic_slice(
         out_weight[0], (col * slice_rows, core * half_width), (slice_rows, half_width)
     )
-    pieces = exchange(jnp.broadcast_to(piece[None], (rows, *piece.shape)), "row")
 
     half_samples = sample_count // 2
     keep, give = normalized_halves(side.reshape(1), tokens, token_gain)
@@ -198,17 +197,23 @@
     w_pair = jnp.stack([w_a, w_b]).transpose(0, 1, 3, 2).reshape(-1, width)
 
     tile = bias_tile_of(pair_repr, asym_id, rel_embed, pair_gain, bias_weight)
-    tile = tile.reshape(pairs, 1, 2, tile_rows * tile_cols)
-    tile = jnp.broadcast_to(tile, (pairs, 2, 2, tile_rows * tile_cols))
-    by_row = exchange(tile.reshape(rows, 2, tile_rows * tile_cols), "row")
-    by_key = by_row.reshape(rows, 2, tile_rows, tile_cols).transpose(1, 3, 0, 2)
+    lanes = 128
+    tile = tile.reshape(pairs, 1, -1, lanes)
+    tile_lines = tile.shape[2]
+    tile = jnp.broadcast_to(tile, (pairs, 2, tile_lines, lanes)).reshape(rows, tile_lines, lanes)
+    piece = piece.astype(jnp.float32).reshape(1, -1, lanes)
+    piece = jnp.broadcast_to(piece, (rows, *piece.shape[1:]))
+    by_row = exchange(jnp.concatenate([tile, piece], 1), "row")
+    pieces = by_row[:, tile_lines:].astype(jnp.bfloat16)
+    by_key = by_row[:, :tile_lines].reshape(rows, 2, tile_rows, tile_cols).transpose(1, 3, 0, 2)
     by_key = by_key.reshape(2, tile_cols, total)
     fanned = jnp.broadcast_to(by_key[None], (cols, *by_key.shape))
     bias_a = exchange(fanned.reshape(2 * cols, tile_cols, total), ("col", "samp"))
     bias_a = bias_a.reshape(total, total)
     bias_b = lax.ppermute(bias_a, "samp", swap)
 
-    w_half, bit, place = pieces, cols // 2, 0
+    w_half = pieces.reshape(rows * slice_rows, half_width)
+    bit, place = cols // 2, 0
     while bit:
         other = lax.ppermute(w_half, "col", [(i, i ^ bit) for i in range(cols)])
         low = (col & bit) == 0

time: 201 us -> 195 us (0.970)
  blocking collectives: 0 us -> 64.3 us
  starting transfers between devices: 108 us -> 65 us
  waiting for transfers between devices: 69.9 us -> 40.6 us
    all_to_all x0 -> x1, blocking collectives: none -> 64.3 us  [exchange(): lax.all_to_all(blocks, axis, split_axis=0, concat_axis=0, axis_index_grou...]
    all_to_all x4 -> x2, starting transfers between devices: 60.7 us -> 13.2 us  [exchange(): lax.all_to_all(blocks, axis, split_axis=0, concat_axis=0, axis_index_grou...]
    all_to_all x4 -> x2, waiting for transfers between devices: 42.2 us -> 13.7 us  [exchange(): lax.all_to_all(blocks, axis, split_axis=0, concat_axis=0, axis_index_grou...]
    ppermute x7, starting transfers between devices: 25.6 us -> 28.3 us  [shifted(): lax.ppermute(value, axis, [(i, (i + by) % size) for i in range(size)])]
    ppermute x3, waiting for transfers between devices: 17.2 us -> 14.7 us  [per_device(): other = lax.ppermute(w_half, 'col', [(i, i ^ bit) for i in range(cols)])]
  transfers between devices with their start and end apart: 18 -> 16, of which waited for: 9 -> 6; matrix products, arithmetic and copies ran while one was open for 3% -> 4% of each run, Pallas kernels for 3% -> 4%
where the time goes in v7:
time: 195 us; the launch traced here: 194 us
  starting transfers between devices  65 us (33%)
  blocking collectives  64.3 us (33%)
  waiting for transfers between devices  40.6 us (21%)
  local copies, waits for them, and re-layouts  7.03 us (4%)
  Pallas kernels  6.81 us (3%)
  other arithmetic  6.61 us (3%)
  matrix products  2.17 us (1%)
    all_to_all x1, blocking collectives, exchange(): lax.all_to_all(blocks, axis, split_axis=0, concat_axis=0, axis_index_grou...  64.3 us
    ppermute x7, starting transfers between devices, shifted(): lax.ppermute(value, axis, [(i, (i + by) % size) for i in range(size)])  28.3 us
    ppermute x3, waiting for transfers between devices, per_device(): other = lax.ppermute(w_half, 'col', [(i, i ^ bit) for i in range(cols)])  14.7 us
    all_to_all x2, waiting for transfers between devices, exchange(): lax.all_to_all(blocks, axis, split_axis=0, concat_axis=0, axis_index_grou...  13.7 us
    all_to_all x2, starting transfers between devices, exchange(): lax.all_to_all(blocks, axis, split_axis=0, concat_axis=0, axis_index_grou...  13.2 us
    ppermute x3, starting transfers between devices, per_device(): other = lax.ppermute(w_half, 'col', [(i, i ^ bit) for i in range(cols)])  12.4 us
    ppermute x7, waiting for transfers between devices, shifted(): lax.ppermute(value, axis, [(i, (i + by) % size) for i in range(size)])  12.2 us
    pallas_call x1, Pallas kernels, attend(): pl.pallas_call(functools.partial(attend_kernel, samples=samples, scale=1....  4.97 us
  transfers between devices with their start and end apart: 16, of which 6 were waited for; matrix products, arithmetic and copies ran while one was open for 4% of the time, Pallas kernels for 4%

profile of v7, /device:TPU:80, one launch (start us, length us, event | category | flops | bytes accessed | tf_op | source)
XLA Modules:
  0.0 193.7 jit_solution(6201521876974998953)
XLA Ops:
  3.7 64.3 %all_to_all.15 = f32[16,34,128]{2,1,0:T(8,128)S(1)} all-to-all(f32[16,34,128]{2,1,0:T(8,128)S(1)} %pad_maximum_fusion.3), channel_id=1, replica_groups=mesh['job'=2,'row'=16,'col'=8,'samp'=2] {'row'}, dimensions={0} | all-to-all | bytes 557056 | tf_op jit(solution)/shard_map/all_to_all | solution.py:25
  69.8 7.6 %all-to-all-start.1 = ((f32[16,32,512]{2,1,0:T(8,128)}), f32[16,32,512]{2,1,0:T(8,128)S(1)}, u32[]{:S(2)}, u32[]{:S(2)}) async-start(f32[16,32,512]{2,1,0:T(8,128)} %bitcast.12), calls=%async_computation.1 | async-start | bytes 2097152 | tf_op jit(solution)/shard_map/all_to_all | solution.py:25
  77.4 1.8 normalize.1
  79.2 3.0 %collective-permute-start = (bf16[64,768]{1,0:T(8,128)(2,1)}, bf16[64,768]{1,0:T(8,128)(2,1)S(1)}, u32[]{:S(2)}, u32[]{:S(2)}) collective-permute-start(bf16[64,768]{1,0:T(8,128)(2,1)} %get-tuple-element.8), channel_id=1, source_target_pairs={{0,16},{16,0},{32,48},{48,32},{64,80},{80,64},{96,112},{112,96},{1... | collective-permute-start | bytes 294920 | tf_op jit(solution)/shard_map/ppermute | solution.py:183
  83.2 7.6 %collective-permute-start.10 = (bf16[96,384]{1,0:T(8,128)(2,1)S(1)}, bf16[96,384]{1,0:T(8,128)(2,1)S(1)}, u32[]{:S(2)}, u32[]{:S(2)}) collective-permute-start(bf16[96,384]{1,0:T(8,128)(2,1)S(1)} %reshape.114), channel_id=1, source_target_pairs={{0,8},{2,10},{4,12},{6,14},{8,0},{10,2},{12,4},{14,6},{1,9},{3,11}... | collective-permute-start | bytes 221192 | tf_op jit(solution)/shard_map/ppermute | solution.py:218
  90.8 4.4 %collective-permute-start.1 = (bf16[128,768]{1,0:T(8,128)(2,1)S(1)}, bf16[128,768]{1,0:T(8,128)(2,1)S(1)}, u32[]{:S(2)}, u32[]{:S(2)}) collective-permute-start(bf16[128,768]{1,0:T(8,128)(2,1)S(1)} %constant_dynamic-update-slice_fusion.refs_0_), channel_id=1, source_target_pairs={{0,32},{16,48},{32,64},{48,80},{64,96},{80,112},{96,128},{112,144}... | collective-permute-start | bytes 589832 | tf_op jit(solution)/shard_map/ppermute | solution.py:169
  95.3 13.5 %collective-permute-done.10 = bf16[96,384]{1,0:T(8,128)(2,1)S(1)} collective-permute-done((bf16[96,384]{1,0:T(8,128)(2,1)S(1)}, bf16[96,384]{1,0:T(8,128)(2,1)S(1)}, u32[]{:S(2)}, u32[]{:S(2)}) %collective-permute-start.10) | collective-permute-done | bytes 73760 | tf_op jit(solution)/shard_map/ppermute | solution.py:218
  108.8 2.2 %collective-permute-start.11 = (bf16[2,96,384]{2,1,0:T(8,128)(2,1)S(1)}, bf16[2,96,384]{2,1,0:T(8,128)(2,1)S(1)}, u32[]{:S(2)}, u32[]{:S(2)}) collective-permute-start(bf16[2,96,384]{2,1,0:T(8,128)(2,1)S(1)} %pad_maximum_fusion.5), channel_id=1, source_target_pairs={{0,4},{2,6},{4,0},{6,2},{8,12},{10,14},{12,8},{14,10},{1,5},{3,7},... | collective-permute-start | bytes 442376 | tf_op jit(solution)/shard_map/ppermute | solution.py:218
  111.1 5.4 %collective-permute-start.5 = (bf16[128,768]{1,0:T(8,128)(2,1)S(1)}, bf16[128,768]{1,0:T(8,128)(2,1)S(1)}, u32[]{:S(2)}, u32[]{:S(2)}) collective-permute-start(bf16[128,768]{1,0:T(8,128)(2,1)S(1)} %constant_dynamic-update-slice_fusion.refs_0_), channel_id=1, source_target_pairs={{0,224},{16,240},{32,0},{48,16},{64,32},{80,48},{96,64},{112,80},{... | collective-permute-start | bytes 589832 | tf_op jit(solution)/shard_map/ppermute | solution.py:169
  116.5 2.0 %collective-permute-start.2 = (bf16[128,768]{1,0:T(8,128)(2,1)S(1)}, bf16[128,768]{1,0:T(8,128)(2,1)S(1)}, u32[]{:S(2)}, u32[]{:S(2)}) collective-permute-start(bf16[128,768]{1,0:T(8,128)(2,1)S(1)} %collective-permute-done.1.refs_1_), channel_id=1, source_target_pairs={{0,32},{16,48},{32,64},{48,80},{64,96},{80,112},{96,128},{112,144}... | collective-permute-start | bytes 589832 | tf_op jit(solution)/shard_map/ppermute | solution.py:169
  118.4 1.2 collective-permute-done.11
  119.7 2.0 %collective-permute-start.9 = (f32[512,512]{1,0:T(8,128)S(1)}, f32[512,512]{1,0:T(8,128)S(1)}, u32[]{:S(2)}, u32[]{:S(2)}) collective-permute-start(f32[512,512]{1,0:T(8,128)S(1)} %bitcast.48), channel_id=1, source_target_pairs={{0,1},{1,0},{2,3},{3,2},{4,5},{5,4},{6,7},{7,6},{8,9},{9,8},{10,11... | collective-permute-start | bytes 3145736 | tf_op jit(solution)/shard_map/ppermute | solution.py:213
  121.7 2.6 %collective-permute-start.12 = (bf16[2,2,96,384]{3,2,0,1:T(8,128)(2,1)S(1)}, bf16[2,2,96,384]{3,2,0,1:T(8,128)(2,1)}, u32[]{:S(2)}, u32[]{:S(2)}) collective-permute-start(bf16[2,2,96,384]{3,2,0,1:T(8,128)(2,1)S(1)} %pad_maximum_fusion.4), channel_id=1, source_target_pairs={{0,2},{2,0},{4,6},{6,4},{8,10},{10,8},{12,14},{14,12},{1,3},{3,1},... | collective-permute-start | bytes 884744 | tf_op jit(solution)/shard_map/ppermute | solution.py:218
  124.3 4.2 %collective-permute-start.8 = (bf16[3,768,48]{1,2,0:T(8,128)(2,1)}, bf16[3,768,48]{1,2,0:T(8,128)(2,1)}, u32[]{:S(2)}, u32[]{:S(2)}) collective-permute-start(bf16[3,768,48]{1,2,0:T(8,128)(2,1)} %bitcast.54), channel_id=1, source_target_pairs={{0,16},{16,0},{32,48},{48,32},{64,80},{80,64},{96,112},{112,96},{1... | collective-permute-start | bytes 663560 | tf_op jit(solution)/shard_map/ppermute | solution.py:193
  129.3 6.1 %collective-permute-start.6 = (bf16[128,768]{1,0:T(8,128)(2,1)S(1)}, bf16[128,768]{1,0:T(8,128)(2,1)S(1)}, u32[]{:S(2)}, u32[]{:S(2)}) collective-permute-start(bf16[128,768]{1,0:T(8,128)(2,1)S(1)} %collective-permute-done.5.refs_7_), channel_id=1, source_target_pairs={{0,224},{16,240},{32,0},{48,16},{64,32},{80,48},{96,64},{112,80},{... | collective-permute-start | bytes 589832 | tf_op jit(solution)/shard_map/ppermute | solution.py:169
  135.4 2.0 %collective-permute-start.3 = (bf16[128,768]{1,0:T(8,128)(2,1)S(1)}, bf16[128,768]{1,0:T(8,128)(2,1)S(1)}, u32[]{:S(2)}, u32[]{:S(2)}) collective-permute-start(bf16[128,768]{1,0:T(8,128)(2,1)S(1)} %collective-permute-done.2.refs_2_), channel_id=1, source_target_pairs={{0,32},{16,48},{32,64},{48,80},{64,96},{80,112},{96,128},{112,144}... | collective-permute-start | bytes 589832 | tf_op jit(solution)/shard_map/ppermute | solution.py:169
  137.5 6.2 %collective-permute-done.6.refs_6_ = bf16[128,768]{1,0:T(8,128)(2,1)S(1)} collective-permute-done((bf16[128,768]{1,0:T(8,128)(2,1)S(1)}, bf16[128,768]{1,0:T(8,128)(2,1)S(1)}, u32[]{:S(2)}, u32[]{:S(2)}) %collective-permute-start.6) | collective-permute-done | bytes 196640 | tf_op jit(solution)/shard_map/ppermute | solution.py:169
  143.7 6.5 %collective-permute-start.7 = (bf16[128,768]{1,0:T(8,128)(2,1)S(1)}, bf16[128,768]{1,0:T(8,128)(2,1)S(1)}, u32[]{:S(2)}, u32[]{:S(2)}) collective-permute-start(bf16[128,768]{1,0:T(8,128)(2,1)S(1)} %collective-permute-done.6.refs_6_), channel_id=1, source_target_pairs={{0,224},{16,240},{32,0},{48,16},{64,32},{80,48},{96,64},{112,80},{... | collective-permute-start | bytes 589832 | tf_op jit(solution)/shard_map/ppermute | solution.py:169
  150.2 2.0 %collective-permute-start.4 = (bf16[128,768]{1,0:T(8,128)(2,1)S(1)}, bf16[128,768]{1,0:T(8,128)(2,1)S(1)}, u32[]{:S(2)}, u32[]{:S(2)}) collective-permute-start(bf16[128,768]{1,0:T(8,128)(2,1)S(1)} %collective-permute-done.3.refs_3_), channel_id=1, source_target_pairs={{0,32},{16,48},{32,64},{48,80},{64,96},{80,112},{96,128},{112,144}... | collective-permute-start | bytes 589832 | tf_op jit(solution)/shard_map/ppermute | solution.py:169
  154.2 1.9 %collective-permute-start.13 = (bf16[2,2,2,96,384]{4,3,0,1,2:T(8,128)(2,1)}, bf16[2,2,2,96,384]{4,3,0,1,2:T(8,128)(2,1)}, u32[]{:S(2)}, u32[]{:S(2)}) collective-permute-start(bf16[2,2,2,96,384]{4,3,0,1,2:T(8,128)(2,1)} %pad_maximum_fusion.1), channel_id=1, source_target_pairs={{0,1},{1,0},{2,3},{3,2},{4,5},{5,4},{6,7},{7,6},{8,9},{9,8},{10,11... | collective-permute-start | bytes 1769480 | tf_op jit(solution)/shard_map/ppermute | solution.py:224
  158.2 5.0 %collective-permute-done.4.refs_4_ = bf16[128,768]{1,0:T(8,128)(2,1)S(1)} collective-permute-done((bf16[128,768]{1,0:T(8,128)(2,1)S(1)}, bf16[128,768]{1,0:T(8,128)(2,1)S(1)}, u32[]{:S(2)}, u32[]{:S(2)}) %collective-permute-start.4) | collective-permute-done | bytes 196640 | tf_op jit(solution)/shard_map/ppermute | solution.py:169
  163.2 5.0 %attend.1 = bf16[16,2,32,96]{3,2,1,0:T(8,128)(2,1)} custom-call(s32[2]{0:T(128)S(1)} %pad_add_fusion.info_1_ref, s32[3]{0:T(128)S(1)} %pad_add_fusion.1.info_2_ref, bf16[128,768]{1,0:T(8,128)(2,1)S(1)} %constant_dynamic-update-slice_fusion.refs_0_, bf16[128,768]{1,0:T(8,128)(2,1)S(1)} %collective-permute-done.1.refs_1_, ...), custom_call_target="tpu_custom_call" | custom-call | flops 654311424 | bytes 6291456 | tf_op jit(solution)/shard_map/attend/pallas_call | solution.py:128
  168.2 5.6 %all-to-all-start.2 = ((bf16[16,2,32,96]{3,2,1,0:T(8,128)(2,1)}), bf16[16,2,32,96]{3,2,1,0:T(8,128)(2,1)}, u32[]{:S(2)}, u32[]{:S(2)}) async-start(bf16[16,2,32,96]{3,2,1,0:T(8,128)(2,1)} %attend.1), calls=%async_computation.2 | async-start | bytes 524288 | tf_op jit(solution)/shard_map/all_to_all | solution.py:25
  177.6 13.7 %all-to-all-done.2 = bf16[16,2,32,96]{3,2,1,0:T(8,128)(2,1)} async-done(((bf16[16,2,32,96]{3,2,1,0:T(8,128)(2,1)}), bf16[16,2,32,96]{3,2,1,0:T(8,128)(2,1)}, u32[]{:S(2)}, u32[]{:S(2)}) %all-to-all-start.2) | async-done | bytes 196640 | tf_op jit(solution)/shard_map/all_to_all | solution.py:25
  (72 shorter events, 16.8 us)
Async XLA Ops:
  0.0 2.3 %copy-start = (bf16[128,128]{1,0:T(8,128)(2,1)S(1)}, bf16[128,128]{1,0:T(8,128)(2,1)}, u32[]{:S(2)}) copy-start(bf16[128,128]{1,0:T(8,128)(2,1)} %param.13) | copy-start | bytes 98308
  0.0 2.0 %copy-start.6 = (s32[512]{0:T(512)S(1)}, s32[512]{0:T(512)}, u32[]{:S(2)}) copy-start(s32[512]{0:T(512)} %param.11) | copy-start | bytes 6148
  1.8 1.5 copy-start.5
  1.8 1.5 copy-start.7
  69.8 50.0 %all-to-all-start.1 = ((f32[16,32,512]{2,1,0:T(8,128)}), f32[16,32,512]{2,1,0:T(8,128)S(1)}, u32[]{:S(2)}, u32[]{:S(2)}) async-start(f32[16,32,512]{2,1,0:T(8,128)} %bitcast.12), calls=%async_computation.1 | async-start | bytes 2097152 | tf_op jit(solution)/shard_map/all_to_all | solution.py:25
  79.2 11.6 %collective-permute-start = (bf16[64,768]{1,0:T(8,128)(2,1)}, bf16[64,768]{1,0:T(8,128)(2,1)S(1)}, u32[]{:S(2)}, u32[]{:S(2)}) collective-permute-start(bf16[64,768]{1,0:T(8,128)(2,1)} %get-tuple-element.8), channel_id=1, source_target_pairs={{0,16},{16,0},{32,48},{48,32},{64,80},{80,64},{96,112},{112,96},{1... | collective-permute-start | bytes 294920 | tf_op jit(solution)/shard_map/ppermute | solution.py:183
  83.2 25.5 %collective-permute-start.10 = (bf16[96,384]{1,0:T(8,128)(2,1)S(1)}, bf16[96,384]{1,0:T(8,128)(2,1)S(1)}, u32[]{:S(2)}, u32[]{:S(2)}) collective-permute-start(bf16[96,384]{1,0:T(8,128)(2,1)S(1)} %reshape.114), channel_id=1, source_target_pairs={{0,8},{2,10},{4,12},{6,14},{8,0},{10,2},{12,4},{14,6},{1,9},{3,11}... | collective-permute-start | bytes 221192 | tf_op jit(solution)/shard_map/ppermute | solution.py:218
  90.8 25.6 %collective-permute-start.1 = (bf16[128,768]{1,0:T(8,128)(2,1)S(1)}, bf16[128,768]{1,0:T(8,128)(2,1)S(1)}, u32[]{:S(2)}, u32[]{:S(2)}) collective-permute-start(bf16[128,768]{1,0:T(8,128)(2,1)S(1)} %constant_dynamic-update-slice_fusion.refs_0_), channel_id=1, source_target_pairs={{0,32},{16,48},{32,64},{48,80},{64,96},{80,112},{96,128},{112,144}... | collective-permute-start | bytes 589832 | tf_op jit(solution)/shard_map/ppermute | solution.py:169
  108.8 10.9 %collective-permute-start.11 = (bf16[2,96,384]{2,1,0:T(8,128)(2,1)S(1)}, bf16[2,96,384]{2,1,0:T(8,128)(2,1)S(1)}, u32[]{:S(2)}, u32[]{:S(2)}) collective-permute-start(bf16[2,96,384]{2,1,0:T(8,128)(2,1)S(1)} %pad_maximum_fusion.5), channel_id=1, source_target_pairs={{0,4},{2,6},{4,0},{6,2},{8,12},{10,14},{12,8},{14,10},{1,5},{3,7},... | collective-permute-start | bytes 442376 | tf_op jit(solution)/shard_map/ppermute | solution.py:218
  111.1 18.2 %collective-permute-start.5 = (bf16[128,768]{1,0:T(8,128)(2,1)S(1)}, bf16[128,768]{1,0:T(8,128)(2,1)S(1)}, u32[]{:S(2)}, u32[]{:S(2)}) collective-permute-start(bf16[128,768]{1,0:T(8,128)(2,1)S(1)} %constant_dynamic-update-slice_fusion.refs_0_), channel_id=1, source_target_pairs={{0,224},{16,240},{32,0},{48,16},{64,32},{80,48},{96,64},{112,80},{... | collective-permute-start | bytes 589832 | tf_op jit(solution)/shard_map/ppermute | solution.py:169
  116.5 18.9 %collective-permute-start.2 = (bf16[128,768]{1,0:T(8,128)(2,1)S(1)}, bf16[128,768]{1,0:T(8,128)(2,1)S(1)}, u32[]{:S(2)}, u32[]{:S(2)}) collective-permute-start(bf16[128,768]{1,0:T(8,128)(2,1)S(1)} %collective-permute-done.1.refs_1_), channel_id=1, source_target_pairs={{0,32},{16,48},{32,64},{48,80},{64,96},{80,112},{96,128},{112,144}... | collective-permute-start | bytes 589832 | tf_op jit(solution)/shard_map/ppermute | solution.py:169
  119.7 32.5 %copy-start.1 = (bf16[2,1,96,384]{3,2,0,1:T(8,128)(2,1)}, bf16[2,1,96,384]{3,2,0,1:T(8,128)(2,1)S(1)}, u32[]{:S(2)}) copy-start(bf16[2,1,96,384]{3,2,0,1:T(8,128)(2,1)S(1)} %get-tuple-element.15) | copy-start | bytes 442372
  119.7 32.5 %copy-start.2 = (bf16[2,1,96,384]{3,2,0,1:T(8,128)(2,1)}, bf16[2,1,96,384]{3,2,0,1:T(8,128)(2,1)S(1)}, u32[]{:S(2)}) copy-start(bf16[2,1,96,384]{3,2,0,1:T(8,128)(2,1)S(1)} %get-tuple-element.16) | copy-start | bytes 442372
  119.7 43.5 %collective-permute-start.9 = (f32[512,512]{1,0:T(8,128)S(1)}, f32[512,512]{1,0:T(8,128)S(1)}, u32[]{:S(2)}, u32[]{:S(2)}) collective-permute-start(f32[512,512]{1,0:T(8,128)S(1)} %bitcast.48), channel_id=1, source_target_pairs={{0,1},{1,0},{2,3},{3,2},{4,5},{5,4},{6,7},{7,6},{8,9},{9,8},{10,11... | collective-permute-start | bytes 3145736 | tf_op jit(solution)/shard_map/ppermute | solution.py:213
  121.7 30.4 %collective-permute-start.12 = (bf16[2,2,96,384]{3,2,0,1:T(8,128)(2,1)S(1)}, bf16[2,2,96,384]{3,2,0,1:T(8,128)(2,1)}, u32[]{:S(2)}, u32[]{:S(2)}) collective-permute-start(bf16[2,2,96,384]{3,2,0,1:T(8,128)(2,1)S(1)} %pad_maximum_fusion.4), channel_id=1, source_target_pairs={{0,2},{2,0},{4,6},{6,4},{8,10},{10,8},{12,14},{14,12},{1,3},{3,1},... | collective-permute-start | bytes 884744 | tf_op jit(solution)/shard_map/ppermute | solution.py:218
  124.3 31.9 %collective-permute-start.8 = (bf16[3,768,48]{1,2,0:T(8,128)(2,1)}, bf16[3,768,48]{1,2,0:T(8,128)(2,1)}, u32[]{:S(2)}, u32[]{:S(2)}) collective-permute-start(bf16[3,768,48]{1,2,0:T(8,128)(2,1)} %bitcast.54), channel_id=1, source_target_pairs={{0,16},{16,0},{32,48},{48,32},{64,80},{80,64},{96,112},{112,96},{1... | collective-permute-start | bytes 663560 | tf_op jit(solution)/shard_map/ppermute | solution.py:193
  129.3 14.4 %collective-permute-start.6 = (bf16[128,768]{1,0:T(8,128)(2,1)S(1)}, bf16[128,768]{1,0:T(8,128)(2,1)S(1)}, u32[]{:S(2)}, u32[]{:S(2)}) collective-permute-start(bf16[128,768]{1,0:T(8,128)(2,1)S(1)} %collective-permute-done.5.refs_7_), channel_id=1, source_target_pairs={{0,224},{16,240},{32,0},{48,16},{64,32},{80,48},{96,64},{112,80},{... | collective-permute-start | bytes 589832 | tf_op jit(solution)/shard_map/ppermute | solution.py:169
  135.4 14.8 %collective-permute-start.3 = (bf16[128,768]{1,0:T(8,128)(2,1)S(1)}, bf16[128,768]{1,0:T(8,128)(2,1)S(1)}, u32[]{:S(2)}, u32[]{:S(2)}) collective-permute-start(bf16[128,768]{1,0:T(8,128)(2,1)S(1)} %collective-permute-done.2.refs_2_), channel_id=1, source_target_pairs={{0,32},{16,48},{32,64},{48,80},{64,96},{80,112},{96,128},{112,144}... | collective-permute-start | bytes 589832 | tf_op jit(solution)/shard_map/ppermute | solution.py:169
  137.5 18.7 %copy-start.4 = (bf16[1,3,768,48]{2,3,1,0:T(8,128)(2,1)S(1)}, bf16[1,3,768,48]{2,3,1,0:T(8,128)(2,1)}, u32[]{:S(2)}) copy-start(bf16[1,3,768,48]{2,3,1,0:T(8,128)(2,1)} %param.18) | copy-start | bytes 663556
  143.7 14.5 %collective-permute-start.7 = (bf16[128,768]{1,0:T(8,128)(2,1)S(1)}, bf16[128,768]{1,0:T(8,128)(2,1)S(1)}, u32[]{:S(2)}, u32[]{:S(2)}) collective-permute-start(bf16[128,768]{1,0:T(8,128)(2,1)S(1)} %collective-permute-done.6.refs_6_), channel_id=1, source_target_pairs={{0,224},{16,240},{32,0},{48,16},{64,32},{80,48},{96,64},{112,80},{... | collective-permute-start | bytes 589832 | tf_op jit(solution)/shard_map/ppermute | solution.py:169
  150.2 13.0 %collective-permute-start.4 = (bf16[128,768]{1,0:T(8,128)(2,1)S(1)}, bf16[128,768]{1,0:T(8,128)(2,1)S(1)}, u32[]{:S(2)}, u32[]{:S(2)}) collective-permute-start(bf16[128,768]{1,0:T(8,128)(2,1)S(1)} %collective-permute-done.3.refs_3_), channel_id=1, source_target_pairs={{0,32},{16,48},{32,64},{48,80},{64,96},{80,112},{96,128},{112,144}... | collective-permute-start | bytes 589832 | tf_op jit(solution)/shard_map/ppermute | solution.py:169
  154.2 19.5 %collective-permute-start.13 = (bf16[2,2,2,96,384]{4,3,0,1,2:T(8,128)(2,1)}, bf16[2,2,2,96,384]{4,3,0,1,2:T(8,128)(2,1)}, u32[]{:S(2)}, u32[]{:S(2)}) collective-permute-start(bf16[2,2,2,96,384]{4,3,0,1,2:T(8,128)(2,1)} %pad_maximum_fusion.1), channel_id=1, source_target_pairs={{0,1},{1,0},{2,3},{3,2},{4,5},{5,4},{6,7},{7,6},{8,9},{9,8},{10,11... | collective-permute-start | bytes 1769480 | tf_op jit(solution)/shard_map/ppermute | solution.py:224
  168.2 23.1 %all-to-all-start.2 = ((bf16[16,2,32,96]{3,2,1,0:T(8,128)(2,1)}), bf16[16,2,32,96]{3,2,1,0:T(8,128)(2,1)}, u32[]{:S(2)}, u32[]{:S(2)}) async-start(bf16[16,2,32,96]{3,2,1,0:T(8,128)(2,1)} %attend.1), calls=%async_computation.2 | async-start | bytes 524288 | tf_op jit(solution)/shard_map/all_to_all | solution.py:25
  177.1 15.5 %copy-start.3 = (bf16[4,32,768]{2,1,0:T(8,128)(2,1)S(1)}, bf16[4,32,768]{2,1,0:T(8,128)(2,1)}, u32[]{:S(2)}) copy-start(bf16[4,32,768]{2,1,0:T(8,128)(2,1)} %tokens_ref.1) | copy-start | bytes 589828

commit v8 on v7

--- a/solution.py
+++ b/solution.py
@@ -201,11 +201,9 @@
     tile = tile.reshape(pairs, 1, -1, lanes)
     tile_lines = tile.shape[2]
     tile = jnp.broadcast_to(tile, (pairs, 2, tile_lines, lanes)).reshape(rows, tile_lines, lanes)
-    piece = piece.astype(jnp.float32).reshape(1, -1, lanes)
-    piece = jnp.broadcast_to(piece, (rows, *piece.shape[1:]))
-    by_row = exchange(jnp.concatenate([tile, piece], 1), "row")
-    pieces = by_row[:, tile_lines:].astype(jnp.bfloat16)
-    by_key = by_row[:, :tile_lines].reshape(rows, 2, tile_rows, tile_cols).transpose(1, 3, 0, 2)
+    by_row = exchange(tile, "row")
+    by_key = by_row.reshape(rows, 2, tile_rows, tile_cols).transpose(1, 3, 0, 2)
+    pieces = exchange(jnp.broadcast_to(piece[None], (rows, *piece.shape)), "row")
     by_key = by_key.reshape(2, tile_cols, total)
     fanned = jnp.broadcast_to(by_key[None], (cols, *by_key.shape))
     bias_a = exchange(fanned.reshape(2 * cols, tile_cols, total), ("col", "samp"))

time: 195 us -> 201 us (1.031)
  blocking collectives: 64.3 us -> 0 us
  starting transfers between devices: 65 us -> 108 us
  waiting for transfers between devices: 40.6 us -> 67.9 us
    all_to_all x1 -> x0, blocking collectives: 64.3 us -> none  [exchange(): lax.all_to_all(blocks, axis, split_axis=0, concat_axis=0, axis_index_grou...]
    all_to_all x2 -> x4, starting transfers between devices: 13.2 us -> 60.7 us  [exchange(): lax.all_to_all(blocks, axis, split_axis=0, concat_axis=0, axis_index_grou...]
    all_to_all x2 -> x4, waiting for transfers between devices: 13.7 us -> 40.2 us  [exchange(): lax.all_to_all(blocks, axis, split_axis=0, concat_axis=0, axis_index_grou...]
    ppermute x7, starting transfers between devices: 28.3 us -> 25.6 us  [shifted(): lax.ppermute(value, axis, [(i, (i + by) % size) for i in range(size)])]
    ppermute x3, waiting for transfers between devices: 14.7 us -> 17.2 us  [per_device(): other = lax.ppermute(w_half, 'col', [(i, i ^ bit) for i in range(cols)])]
  transfers between devices with their start and end apart: 16 -> 18, of which waited for: 6 -> 9; matrix products, arithmetic and copies ran while one was open for 4% -> 4% of each run, Pallas kernels for 4% -> 3%
where the time goes in v8:
time: 201 us; the launch traced here: 200 us
  starting transfers between devices  108 us (54%)
  waiting for transfers between devices  67.9 us (34%)
  local copies, waits for them, and re-layouts  8.34 us (4%)
  Pallas kernels  6.86 us (3%)
  other arithmetic  5.82 us (3%)
  matrix products  2.17 us (1%)
    all_to_all x4, starting transfers between devices, exchange(): lax.all_to_all(blocks, axis, split_axis=0, concat_axis=0, axis_index_grou...  60.7 us
    all_to_all x4, waiting for transfers between devices, exchange(): lax.all_to_all(blocks, axis, split_axis=0, concat_axis=0, axis_index_grou...  40.2 us
    ppermute x7, starting transfers between devices, shifted(): lax.ppermute(value, axis, [(i, (i + by) % size) for i in range(size)])  25.6 us
    ppermute x3, waiting for transfers between devices, per_device(): other = lax.ppermute(w_half, 'col', [(i, i ^ bit) for i in range(cols)])  17.2 us
    ppermute x3, starting transfers between devices, per_device(): other = lax.ppermute(w_half, 'col', [(i, i ^ bit) for i in range(cols)])  11.8 us
    ppermute x7, waiting for transfers between devices, shifted(): lax.ppermute(value, axis, [(i, (i + by) % size) for i in range(size)])  10.5 us
    pallas_call x1, Pallas kernels, attend(): pl.pallas_call(functools.partial(attend_kernel, samples=samples, scale=1....  5.02 us
  transfers between devices with their start and end apart: 18, of which 9 were waited for; matrix products, arithmetic and copies ran while one was open for 4% of the time, Pallas kernels for 3%

profile of v8, /device:TPU:80, one launch (start us, length us, event | category | flops | bytes accessed | tf_op | source)
XLA Modules:
  0.0 200.1 jit_solution(16029766066544700622)
XLA Ops:
  3.5 43.7 %all-to-all-start = ((f32[16,16,128]{2,1,0:T(8,128)}), f32[16,16,128]{2,1,0:T(8,128)S(1)}, u32[]{:S(2)}, u32[]{:S(2)}) async-start(f32[16,16,128]{2,1,0:T(8,128)} %bitcast.10), calls=%async_computation | async-start | bytes 262144 | tf_op jit(solution)/shard_map/all_to_all | solution.py:25
  47.3 14.5 %all-to-all-done = f32[16,16,128]{2,1,0:T(8,128)S(1)} async-done(((f32[16,16,128]{2,1,0:T(8,128)}), f32[16,16,128]{2,1,0:T(8,128)S(1)}, u32[]{:S(2)}, u32[]{:S(2)}) %all-to-all-start) | async-done | bytes 131104 | tf_op jit(solution)/shard_map/all_to_all | solution.py:25
  62.5 4.0 %all-to-all-start.3 = ((bf16[16,6,384]{2,1,0:T(8,128)(2,1)}), bf16[16,6,384]{2,1,0:T(8,128)(2,1)S(1)}, u32[]{:S(2)}, u32[]{:S(2)}) async-start(bf16[16,6,384]{2,1,0:T(8,128)(2,1)} %broadcast_in_dim.40), calls=%async_computation.3 | async-start | bytes 196608 | tf_op jit(solution)/shard_map/all_to_all | solution.py:25
  67.2 12.6 %all-to-all-done.3 = bf16[16,6,384]{2,1,0:T(8,128)(2,1)S(1)} async-done(((bf16[16,6,384]{2,1,0:T(8,128)(2,1)}), bf16[16,6,384]{2,1,0:T(8,128)(2,1)S(1)}, u32[]{:S(2)}, u32[]{:S(2)}) %all-to-all-start.3) | async-done | bytes 73760 | tf_op jit(solution)/shard_map/all_to_all | solution.py:25
  80.9 7.6 %all-to-all-start.1 = ((f32[16,32,512]{2,1,0:T(8,128)}), f32[16,32,512]{2,1,0:T(8,128)S(1)}, u32[]{:S(2)}, u32[]{:S(2)}) async-start(f32[16,32,512]{2,1,0:T(8,128)} %bitcast.12), calls=%async_computation.1 | async-start | bytes 2097152 | tf_op jit(solution)/shard_map/all_to_all | solution.py:25
  90.3 2.9 %collective-permute-start = (bf16[64,768]{1,0:T(8,128)(2,1)}, bf16[64,768]{1,0:T(8,128)(2,1)S(1)}, u32[]{:S(2)}, u32[]{:S(2)}) collective-permute-start(bf16[64,768]{1,0:T(8,128)(2,1)} %get-tuple-element.8), channel_id=1, source_target_pairs={{0,16},{16,0},{32,48},{48,32},{64,80},{80,64},{96,112},{112,96},{1... | collective-permute-start | bytes 294920 | tf_op jit(solution)/shard_map/ppermute | solution.py:183
  94.1 7.6 %collective-permute-start.10 = (bf16[96,384]{1,0:T(8,128)(2,1)S(1)}, bf16[96,384]{1,0:T(8,128)(2,1)S(1)}, u32[]{:S(2)}, u32[]{:S(2)}) collective-permute-start(bf16[96,384]{1,0:T(8,128)(2,1)S(1)} %reshape.107), channel_id=1, source_target_pairs={{0,8},{2,10},{4,12},{6,14},{8,0},{10,2},{12,4},{14,6},{1,9},{3,11}... | collective-permute-start | bytes 221192 | tf_op jit(solution)/shard_map/ppermute | solution.py:216
  101.7 2.7 %collective-permute-start.1 = (bf16[128,768]{1,0:T(8,128)(2,1)S(1)}, bf16[128,768]{1,0:T(8,128)(2,1)S(1)}, u32[]{:S(2)}, u32[]{:S(2)}) collective-permute-start(bf16[128,768]{1,0:T(8,128)(2,1)S(1)} %constant_dynamic-update-slice_fusion.refs_0_), channel_id=1, source_target_pairs={{0,32},{16,48},{32,64},{48,80},{64,96},{80,112},{96,128},{112,144}... | collective-permute-start | bytes 589832 | tf_op jit(solution)/shard_map/ppermute | solution.py:169
  104.5 15.4 %collective-permute-done.10 = bf16[96,384]{1,0:T(8,128)(2,1)S(1)} collective-permute-done((bf16[96,384]{1,0:T(8,128)(2,1)S(1)}, bf16[96,384]{1,0:T(8,128)(2,1)S(1)}, u32[]{:S(2)}, u32[]{:S(2)}) %collective-permute-start.10) | collective-permute-done | bytes 73760 | tf_op jit(solution)/shard_map/ppermute | solution.py:216
  119.9 2.2 %collective-permute-start.11 = (bf16[2,96,384]{2,1,0:T(8,128)(2,1)S(1)}, bf16[2,96,384]{2,1,0:T(8,128)(2,1)S(1)}, u32[]{:S(2)}, u32[]{:S(2)}) collective-permute-start(bf16[2,96,384]{2,1,0:T(8,128)(2,1)S(1)} %pad_maximum_fusion.4), channel_id=1, source_target_pairs={{0,4},{2,6},{4,0},{6,2},{8,12},{10,14},{12,8},{14,10},{1,5},{3,7},... | collective-permute-start | bytes 442376 | tf_op jit(solution)/shard_map/ppermute | solution.py:216
  122.2 3.1 %collective-permute-start.5 = (bf16[128,768]{1,0:T(8,128)(2,1)S(1)}, bf16[128,768]{1,0:T(8,128)(2,1)S(1)}, u32[]{:S(2)}, u32[]{:S(2)}) collective-permute-start(bf16[128,768]{1,0:T(8,128)(2,1)S(1)} %constant_dynamic-update-slice_fusion.refs_0_), channel_id=1, source_target_pairs={{0,224},{16,240},{32,0},{48,16},{64,32},{80,48},{96,64},{112,80},{... | collective-permute-start | bytes 589832 | tf_op jit(solution)/shard_map/ppermute | solution.py:169
  125.3 3.7 %collective-permute-start.2 = (bf16[128,768]{1,0:T(8,128)(2,1)S(1)}, bf16[128,768]{1,0:T(8,128)(2,1)S(1)}, u32[]{:S(2)}, u32[]{:S(2)}) collective-permute-start(bf16[128,768]{1,0:T(8,128)(2,1)S(1)} %collective-permute-done.1.refs_1_), channel_id=1, source_target_pairs={{0,32},{16,48},{32,64},{48,80},{64,96},{80,112},{96,128},{112,144}... | collective-permute-start | bytes 589832 | tf_op jit(solution)/shard_map/ppermute | solution.py:169
  130.8 2.0 collective-permute-start.9
  132.8 2.0 %collective-permute-start.12 = (bf16[2,2,96,384]{3,2,0,1:T(8,128)(2,1)S(1)}, bf16[2,2,96,384]{3,2,0,1:T(8,128)(2,1)}, u32[]{:S(2)}, u32[]{:S(2)}) collective-permute-start(bf16[2,2,96,384]{3,2,0,1:T(8,128)(2,1)S(1)} %pad_maximum_fusion.3), channel_id=1, source_target_pairs={{0,2},{2,0},{4,6},{6,4},{8,10},{10,8},{12,14},{14,12},{1,3},{3,1},... | collective-permute-start | bytes 884744 | tf_op jit(solution)/shard_map/ppermute | solution.py:216
  134.9 2.9 %collective-permute-start.8 = (bf16[3,768,48]{1,2,0:T(8,128)(2,1)}, bf16[3,768,48]{1,2,0:T(8,128)(2,1)}, u32[]{:S(2)}, u32[]{:S(2)}) collective-permute-start(bf16[3,768,48]{1,2,0:T(8,128)(2,1)} %bitcast.55), channel_id=1, source_target_pairs={{0,16},{16,0},{32,48},{48,32},{64,80},{80,64},{96,112},{112,96},{1... | collective-permute-start | bytes 663560 | tf_op jit(solution)/shard_map/ppermute | solution.py:193
  138.5 5.3 %collective-permute-start.6 = (bf16[128,768]{1,0:T(8,128)(2,1)S(1)}, bf16[128,768]{1,0:T(8,128)(2,1)S(1)}, u32[]{:S(2)}, u32[]{:S(2)}) collective-permute-start(bf16[128,768]{1,0:T(8,128)(2,1)S(1)} %collective-permute-done.5.refs_7_), channel_id=1, source_target_pairs={{0,224},{16,240},{32,0},{48,16},{64,32},{80,48},{96,64},{112,80},{... | collective-permute-start | bytes 589832 | tf_op jit(solution)/shard_map/ppermute | solution.py:169
  143.8 2.0 collective-permute-start.3
  145.9 3.0 %collective-permute-done.6.refs_6_ = bf16[128,768]{1,0:T(8,128)(2,1)S(1)} collective-permute-done((bf16[128,768]{1,0:T(8,128)(2,1)S(1)}, bf16[128,768]{1,0:T(8,128)(2,1)S(1)}, u32[]{:S(2)}, u32[]{:S(2)}) %collective-permute-start.6) | collective-permute-done | bytes 196640 | tf_op jit(solution)/shard_map/ppermute | solution.py:169
  148.9 6.2 %collective-permute-start.7 = (bf16[128,768]{1,0:T(8,128)(2,1)S(1)}, bf16[128,768]{1,0:T(8,128)(2,1)S(1)}, u32[]{:S(2)}, u32[]{:S(2)}) collective-permute-start(bf16[128,768]{1,0:T(8,128)(2,1)S(1)} %collective-permute-done.6.refs_6_), channel_id=1, source_target_pairs={{0,224},{16,240},{32,0},{48,16},{64,32},{80,48},{96,64},{112,80},{... | collective-permute-start | bytes 589832 | tf_op jit(solution)/shard_map/ppermute | solution.py:169
  156.8 2.6 %collective-permute-start.4 = (bf16[128,768]{1,0:T(8,128)(2,1)S(1)}, bf16[128,768]{1,0:T(8,128)(2,1)S(1)}, u32[]{:S(2)}, u32[]{:S(2)}) collective-permute-start(bf16[128,768]{1,0:T(8,128)(2,1)S(1)} %collective-permute-done.3.refs_3_), channel_id=1, source_target_pairs={{0,32},{16,48},{32,64},{48,80},{64,96},{80,112},{96,128},{112,144}... | collective-permute-start | bytes 589832 | tf_op jit(solution)/shard_map/ppermute | solution.py:169
  165.2 5.1 %collective-permute-done.4.refs_4_ = bf16[128,768]{1,0:T(8,128)(2,1)S(1)} collective-permute-done((bf16[128,768]{1,0:T(8,128)(2,1)S(1)}, bf16[128,768]{1,0:T(8,128)(2,1)S(1)}, u32[]{:S(2)}, u32[]{:S(2)}) %collective-permute-start.4) | collective-permute-done | bytes 196640 | tf_op jit(solution)/shard_map/ppermute | solution.py:169
  170.3 5.0 %attend.1 = bf16[16,2,32,96]{3,2,1,0:T(8,128)(2,1)} custom-call(s32[2]{0:T(128)S(1)} %pad_add_fusion.info_1_ref, s32[3]{0:T(128)S(1)} %pad_add_fusion.1.info_2_ref, bf16[128,768]{1,0:T(8,128)(2,1)S(1)} %constant_dynamic-update-slice_fusion.refs_0_, bf16[128,768]{1,0:T(8,128)(2,1)S(1)} %collective-permute-done.1.refs_1_, ...), custom_call_target="tpu_custom_call" | custom-call | flops 654311424 | bytes 6291456 | tf_op jit(solution)/shard_map/attend/pallas_call | solution.py:128
  175.3 5.4 %all-to-all-start.2 = ((bf16[16,2,32,96]{3,2,1,0:T(8,128)(2,1)}), bf16[16,2,32,96]{3,2,1,0:T(8,128)(2,1)}, u32[]{:S(2)}, u32[]{:S(2)}) async-start(bf16[16,2,32,96]{3,2,1,0:T(8,128)(2,1)} %attend.1), calls=%async_computation.2 | async-start | bytes 524288 | tf_op jit(solution)/shard_map/all_to_all | solution.py:25
  184.6 13.1 %all-to-all-done.2 = bf16[16,2,32,96]{3,2,1,0:T(8,128)(2,1)} async-done(((bf16[16,2,32,96]{3,2,1,0:T(8,128)(2,1)}), bf16[16,2,32,96]{3,2,1,0:T(8,128)(2,1)}, u32[]{:S(2)}, u32[]{:S(2)}) %all-to-all-start.2) | async-done | bytes 196640 | tf_op jit(solution)/shard_map/all_to_all | solution.py:25
  (73 shorter events, 24.3 us)
Async XLA Ops:
  0.0 47.2 %copy-start = (bf16[1,48,768]{2,1,0:T(8,128)(2,1)S(1)}, bf16[1,48,768]{2,1,0:T(8,128)(2,1)}, u32[]{:S(2)}) copy-start(bf16[1,48,768]{2,1,0:T(8,128)(2,1)} %param.19) | copy-start | bytes 221188
  0.0 1.5 copy-start.5
  3.5 58.3 %all-to-all-start = ((f32[16,16,128]{2,1,0:T(8,128)}), f32[16,16,128]{2,1,0:T(8,128)S(1)}, u32[]{:S(2)}, u32[]{:S(2)}) async-start(f32[16,16,128]{2,1,0:T(8,128)} %bitcast.10), calls=%async_computation | async-start | bytes 262144 | tf_op jit(solution)/shard_map/all_to_all | solution.py:25
  62.5 17.3 %all-to-all-start.3 = ((bf16[16,6,384]{2,1,0:T(8,128)(2,1)}), bf16[16,6,384]{2,1,0:T(8,128)(2,1)S(1)}, u32[]{:S(2)}, u32[]{:S(2)}) async-start(bf16[16,6,384]{2,1,0:T(8,128)(2,1)} %broadcast_in_dim.40), calls=%async_computation.3 | async-start | bytes 196608 | tf_op jit(solution)/shard_map/all_to_all | solution.py:25
  80.9 50.0 %all-to-all-start.1 = ((f32[16,32,512]{2,1,0:T(8,128)}), f32[16,32,512]{2,1,0:T(8,128)S(1)}, u32[]{:S(2)}, u32[]{:S(2)}) async-start(f32[16,32,512]{2,1,0:T(8,128)} %bitcast.12), calls=%async_computation.1 | async-start | bytes 2097152 | tf_op jit(solution)/shard_map/all_to_all | solution.py:25
  90.3 11.4 %collective-permute-start = (bf16[64,768]{1,0:T(8,128)(2,1)}, bf16[64,768]{1,0:T(8,128)(2,1)S(1)}, u32[]{:S(2)}, u32[]{:S(2)}) collective-permute-start(bf16[64,768]{1,0:T(8,128)(2,1)} %get-tuple-element.8), channel_id=1, source_target_pairs={{0,16},{16,0},{32,48},{48,32},{64,80},{80,64},{96,112},{112,96},{1... | collective-permute-start | bytes 294920 | tf_op jit(solution)/shard_map/ppermute | solution.py:183
  94.1 25.7 %collective-permute-start.10 = (bf16[96,384]{1,0:T(8,128)(2,1)S(1)}, bf16[96,384]{1,0:T(8,128)(2,1)S(1)}, u32[]{:S(2)}, u32[]{:S(2)}) collective-permute-start(bf16[96,384]{1,0:T(8,128)(2,1)S(1)} %reshape.107), channel_id=1, source_target_pairs={{0,8},{2,10},{4,12},{6,14},{8,0},{10,2},{12,4},{14,6},{1,9},{3,11}... | collective-permute-start | bytes 221192 | tf_op jit(solution)/shard_map/ppermute | solution.py:216
  101.7 23.5 %collective-permute-start.1 = (bf16[128,768]{1,0:T(8,128)(2,1)S(1)}, bf16[128,768]{1,0:T(8,128)(2,1)S(1)}, u32[]{:S(2)}, u32[]{:S(2)}) collective-permute-start(bf16[128,768]{1,0:T(8,128)(2,1)S(1)} %constant_dynamic-update-slice_fusion.refs_0_), channel_id=1, source_target_pairs={{0,32},{16,48},{32,64},{48,80},{64,96},{80,112},{96,128},{112,144}... | collective-permute-start | bytes 589832 | tf_op jit(solution)/shard_map/ppermute | solution.py:169
  119.9 10.9 %collective-permute-start.11 = (bf16[2,96,384]{2,1,0:T(8,128)(2,1)S(1)}, bf16[2,96,384]{2,1,0:T(8,128)(2,1)S(1)}, u32[]{:S(2)}, u32[]{:S(2)}) collective-permute-start(bf16[2,96,384]{2,1,0:T(8,128)(2,1)S(1)} %pad_maximum_fusion.4), channel_id=1, source_target_pairs={{0,4},{2,6},{4,0},{6,2},{8,12},{10,14},{12,8},{14,10},{1,5},{3,7},... | collective-permute-start | bytes 442376 | tf_op jit(solution)/shard_map/ppermute | solution.py:216
  122.2 16.3 %collective-permute-start.5 = (bf16[128,768]{1,0:T(8,128)(2,1)S(1)}, bf16[128,768]{1,0:T(8,128)(2,1)S(1)}, u32[]{:S(2)}, u32[]{:S(2)}) collective-permute-start(bf16[128,768]{1,0:T(8,128)(2,1)S(1)} %constant_dynamic-update-slice_fusion.refs_0_), channel_id=1, source_target_pairs={{0,224},{16,240},{32,0},{48,16},{64,32},{80,48},{96,64},{112,80},{... | collective-permute-start | bytes 589832 | tf_op jit(solution)/shard_map/ppermute | solution.py:169
  125.3 18.6 %collective-permute-start.2 = (bf16[128,768]{1,0:T(8,128)(2,1)S(1)}, bf16[128,768]{1,0:T(8,128)(2,1)S(1)}, u32[]{:S(2)}, u32[]{:S(2)}) collective-permute-start(bf16[128,768]{1,0:T(8,128)(2,1)S(1)} %collective-permute-done.1.refs_1_), channel_id=1, source_target_pairs={{0,32},{16,48},{32,64},{48,80},{64,96},{80,112},{96,128},{112,144}... | collective-permute-start | bytes 589832 | tf_op jit(solution)/shard_map/ppermute | solution.py:169
  130.8 28.5 %copy-start.1 = (bf16[2,1,96,384]{3,2,0,1:T(8,128)(2,1)}, bf16[2,1,96,384]{3,2,0,1:T(8,128)(2,1)S(1)}, u32[]{:S(2)}) copy-start(bf16[2,1,96,384]{3,2,0,1:T(8,128)(2,1)S(1)} %get-tuple-element.15) | copy-start | bytes 442372
  130.8 28.5 %copy-start.2 = (bf16[2,1,96,384]{3,2,0,1:T(8,128)(2,1)}, bf16[2,1,96,384]{3,2,0,1:T(8,128)(2,1)S(1)}, u32[]{:S(2)}) copy-start(bf16[2,1,96,384]{3,2,0,1:T(8,128)(2,1)S(1)} %get-tuple-element.16) | copy-start | bytes 442372
  130.8 39.5 %collective-permute-start.9 = (f32[512,512]{1,0:T(8,128)S(1)}, f32[512,512]{1,0:T(8,128)S(1)}, u32[]{:S(2)}, u32[]{:S(2)}) collective-permute-start(f32[512,512]{1,0:T(8,128)S(1)} %bitcast.50), channel_id=1, source_target_pairs={{0,1},{1,0},{2,3},{3,2},{4,5},{5,4},{6,7},{7,6},{8,9},{9,8},{10,11... | collective-permute-start | bytes 3145736 | tf_op jit(solution)/shard_map/ppermute | solution.py:211
  132.8 26.5 %collective-permute-start.12 = (bf16[2,2,96,384]{3,2,0,1:T(8,128)(2,1)S(1)}, bf16[2,2,96,384]{3,2,0,1:T(8,128)(2,1)}, u32[]{:S(2)}, u32[]{:S(2)}) collective-permute-start(bf16[2,2,96,384]{3,2,0,1:T(8,128)(2,1)S(1)} %pad_maximum_fusion.3), channel_id=1, source_target_pairs={{0,2},{2,0},{4,6},{6,4},{8,10},{10,8},{12,14},{14,12},{1,3},{3,1},... | collective-permute-start | bytes 884744 | tf_op jit(solution)/shard_map/ppermute | solution.py:216
  134.9 28.5 %collective-permute-start.8 = (bf16[3,768,48]{1,2,0:T(8,128)(2,1)}, bf16[3,768,48]{1,2,0:T(8,128)(2,1)}, u32[]{:S(2)}, u32[]{:S(2)}) collective-permute-start(bf16[3,768,48]{1,2,0:T(8,128)(2,1)} %bitcast.55), channel_id=1, source_target_pairs={{0,16},{16,0},{32,48},{48,32},{64,80},{80,64},{96,112},{112,96},{1... | collective-permute-start | bytes 663560 | tf_op jit(solution)/shard_map/ppermute | solution.py:193
  138.5 10.4 %collective-permute-start.6 = (bf16[128,768]{1,0:T(8,128)(2,1)S(1)}, bf16[128,768]{1,0:T(8,128)(2,1)S(1)}, u32[]{:S(2)}, u32[]{:S(2)}) collective-permute-start(bf16[128,768]{1,0:T(8,128)(2,1)S(1)} %collective-permute-done.5.refs_7_), channel_id=1, source_target_pairs={{0,224},{16,240},{32,0},{48,16},{64,32},{80,48},{96,64},{112,80},{... | collective-permute-start | bytes 589832 | tf_op jit(solution)/shard_map/ppermute | solution.py:169
  143.8 13.0 %collective-permute-start.3 = (bf16[128,768]{1,0:T(8,128)(2,1)S(1)}, bf16[128,768]{1,0:T(8,128)(2,1)S(1)}, u32[]{:S(2)}, u32[]{:S(2)}) collective-permute-start(bf16[128,768]{1,0:T(8,128)(2,1)S(1)} %collective-permute-done.2.refs_2_), channel_id=1, source_target_pairs={{0,32},{16,48},{32,64},{48,80},{64,96},{80,112},{96,128},{112,144}... | collective-permute-start | bytes 589832 | tf_op jit(solution)/shard_map/ppermute | solution.py:169
  145.9 17.4 %copy-start.4 = (bf16[1,3,768,48]{2,3,1,0:T(8,128)(2,1)S(1)}, bf16[1,3,768,48]{2,3,1,0:T(8,128)(2,1)}, u32[]{:S(2)}) copy-start(bf16[1,3,768,48]{2,3,1,0:T(8,128)(2,1)} %param.18) | copy-start | bytes 663556
  148.9 16.3 %collective-permute-start.7 = (bf16[128,768]{1,0:T(8,128)(2,1)S(1)}, bf16[128,768]{1,0:T(8,128)(2,1)S(1)}, u32[]{:S(2)}, u32[]{:S(2)}) collective-permute-start(bf16[128,768]{1,0:T(8,128)(2,1)S(1)} %collective-permute-done.6.refs_6_), channel_id=1, source_target_pairs={{0,224},{16,240},{32,0},{48,16},{64,32},{80,48},{96,64},{112,80},{... | collective-permute-start | bytes 589832 | tf_op jit(solution)/shard_map/ppermute | solution.py:169
  156.8 13.5 %collective-permute-start.4 = (bf16[128,768]{1,0:T(8,128)(2,1)S(1)}, bf16[128,768]{1,0:T(8,128)(2,1)S(1)}, u32[]{:S(2)}, u32[]{:S(2)}) collective-permute-start(bf16[128,768]{1,0:T(8,128)(2,1)S(1)} %collective-permute-done.3.refs_3_), channel_id=1, source_target_pairs={{0,32},{16,48},{32,64},{48,80},{64,96},{80,112},{96,128},{112,144}... | collective-permute-start | bytes 589832 | tf_op jit(solution)/shard_map/ppermute | solution.py:169
  161.4 19.4 %collective-permute-start.13 = (bf16[2,2,2,96,384]{4,3,0,1,2:T(8,128)(2,1)}, bf16[2,2,2,96,384]{4,3,0,1,2:T(8,128)(2,1)}, u32[]{:S(2)}, u32[]{:S(2)}) collective-permute-start(bf16[2,2,2,96,384]{4,3,0,1,2:T(8,128)(2,1)} %pad_maximum_fusion.1), channel_id=1, source_target_pairs={{0,1},{1,0},{2,3},{3,2},{4,5},{5,4},{6,7},{7,6},{8,9},{9,8},{10,11... | collective-permute-start | bytes 1769480 | tf_op jit(solution)/shard_map/ppermute | solution.py:222
  175.3 22.4 %all-to-all-start.2 = ((bf16[16,2,32,96]{3,2,1,0:T(8,128)(2,1)}), bf16[16,2,32,96]{3,2,1,0:T(8,128)(2,1)}, u32[]{:S(2)}, u32[]{:S(2)}) async-start(bf16[16,2,32,96]{3,2,1,0:T(8,128)(2,1)} %attend.1), calls=%async_computation.2 | async-start | bytes 524288 | tf_op jit(solution)/shard_map/all_to_all | solution.py:25
  184.2 14.9 %copy-start.3 = (bf16[4,32,768]{2,1,0:T(8,128)(2,1)S(1)}, bf16[4,32,768]{2,1,0:T(8,128)(2,1)}, u32[]{:S(2)}) copy-start(bf16[4,32,768]{2,1,0:T(8,128)(2,1)} %tokens_ref.1) | copy-start | bytes 589828
  (3 other events, 4.3 us)

commit v9 on v7

--- a/solution.py
+++ b/solution.py
@@ -89,6 +89,8 @@
     dot = functools.partial(lax.dot_general, preferred_element_type=jnp.float32)
     for step, block_ref in enumerate(block_refs):
         blocks_ref[lax.rem(pair - step + pairs, pairs)] = block_ref[...]
+    swapped = core == 1
+    ordered = [[], []]
     starts = [side * half_rows, (1 - side) * half_rows]
     for u in range(samples):
         x = jnp.concatenate(
@@ -111,12 +113,45 @@
             inverse = 1.0 / jnp.sum(weights, axis=0, keepdims=True)
             probs = (weights * inverse).astype(jnp.bfloat16)
             outs.append(dot(value, probs, (((1,), (0,)), ((), ()))))
-        swapped = core == 1
-        low = jnp.where(swapped, outs[1], outs[0])
-        high = jnp.where(swapped, outs[0], outs[1])
-        both = jnp.concatenate([low, high]).T.astype(jnp.bfloat16)
-        for i in range(total // token_rows):
-            out_ref[i, u] = both[i * token_rows : (i + 1) * token_rows]
+        ordered[0].append(jnp.where(swapped, outs[1], outs[0]))
+        ordered[1].append(jnp.where(swapped, outs[0], outs[1]))
+    for i in range(total // token_rows):
+        at = slice(i * token_rows, (i + 1) * token_rows)
+        out_ref[i] = jnp.concatenate(
+            [value[:, at] for head in ordered for value in head], axis=1
+        ).astype(jnp.bfloat16)
+
+
+def output_kernel(back_ref, w_ref, tokens_ref, out_ref):
+    rows, _, lanes = back_ref.shape
+    half_samples = tokens_ref.shape[0] // 2
+    half = lanes // 2
+    for side in range(2):
+        pieces = []
+        for k in range(rows // 2):
+            block = back_ref[2 * k + side].astype(jnp.float32)
+            pieces += [block[:, :half], block[:, half:]]
+        attended = jnp.concatenate(pieces).astype(jnp.bfloat16)
+        update = lax.dot_general(
+            attended, w_ref[...], (((0,), (0,)), ((), ())), preferred_element_type=jnp.float32
+        )
+        samples = pl.ds(side * half_samples, half_samples)
+        before = tokens_ref[samples].astype(jnp.float32)
+        out_ref[samples] = (before + update.reshape(before.shape)).astype(jnp.bfloat16)
+
+
+def output(back, w_out, tokens):
+    vmem = pl.BlockSpec(memory_space=pltpu.VMEM)
+    return pl.pallas_call(
+        output_kernel,
+        out_shape=jax.ShapeDtypeStruct(tokens.shape, jnp.bfloat16),
+        in_specs=[vmem, vmem, vmem],
+        out_specs=vmem,
+        cost_estimate=pl.CostEstimate(
+            flops=2 * tokens.size * w_out.shape[0], bytes_accessed=4 * 1024 * 1024, transcendentals=0
+        ),
+        name="output",
+    )(back, w_out, tokens)
 
 
 def attend(info_1, info_2, blocks, w, bias_a, bias_b, samples):
@@ -128,7 +163,7 @@
     return pl.pallas_call(
         functools.partial(attend_kernel, samples=samples, scale=1.0 / math.sqrt(HEAD_DIM)),
         out_shape=jax.ShapeDtypeStruct(
-            (total // token_rows, samples, token_rows, 2 * HEAD_DIM), jnp.bfloat16
+            (total // token_rows, HEAD_DIM, 2 * samples * token_rows), jnp.bfloat16
         ),
         in_specs=[pl.BlockSpec(memory_space=pltpu.SMEM)] * 2 + [vmem] * (len(blocks) + 3),
         out_specs=vmem,
@@ -153,7 +188,7 @@
     qkv_weight,
     out_weight,
 ):
-    sample_count, token_rows, width = tokens.shape
+    sample_count, _, width = tokens.shape
     total = asym_id.shape[0]
     rows = lax.axis_size("row")
     cols = lax.axis_size("col")
@@ -230,12 +265,7 @@
 
     attended = attend(info_1, info_2, blocks, w_pair, bias_a, bias_b, half_samples)
     back = exchange(attended, "row")
-    back = back.reshape(pairs, 2, half_samples, token_rows, 2 * HEAD_DIM)
-    back = back.transpose(1, 2, 3, 0, 4).reshape(sample_count * token_rows, width)
-    update = jnp.dot(back, w_out, preferred_element_type=jnp.float32)
-    return (
-        tokens.astype(jnp.float32) + update.reshape(sample_count, token_rows, width)
-    ).astype(jnp.bfloat16)
+    return output(back, w_out, tokens)
 
 
 def solution(mesh):

time: 195 us -> 193 us (0.990)
  Pallas kernels: 6.81 us -> 9.57 us
  waiting for transfers between devices: 40.6 us -> 37.9 us
    all_to_all x2, waiting for transfers between devices: 13.7 us -> 10.9 us  [exchange(): lax.all_to_all(blocks, axis, split_axis=0, concat_axis=0, axis_index_grou...]
    pallas_call x0 -> x1, Pallas kernels: none -> 2.71 us  [output(): pl.pallas_call(output_kernel, out_shape=jax.ShapeDtypeStruct(tokens.shape...]
  transfers between devices with their start and end apart: 16 -> 16, of which waited for: 6 -> 6; matrix products, arithmetic and copies ran while one was open for 4% -> 5% of each run, Pallas kernels for 4% -> 4%
where the time goes in v9:
time: 193 us; the launch traced here: 192 us
  starting transfers between devices  65 us (34%)
  blocking collectives  64.3 us (33%)
  waiting for transfers between devices  37.9 us (20%)
  Pallas kernels  9.57 us (5%)
  other arithmetic  6.6 us (3%)
  local copies, waits for them, and re-layouts  6.53 us (3%)
    all_to_all x1, blocking collectives, exchange(): lax.all_to_all(blocks, axis, split_axis=0, concat_axis=0, axis_index_grou...  64.3 us
    ppermute x7, starting transfers between devices, shifted(): lax.ppermute(value, axis, [(i, (i + by) % size) for i in range(size)])  28.3 us
    ppermute x3, waiting for transfers between devices, per_device(): other = lax.ppermute(w_half, 'col', [(i, i ^ bit) for i in range(cols)])  14.7 us
    all_to_all x2, starting transfers between devices, exchange(): lax.all_to_all(blocks, axis, split_axis=0, concat_axis=0, axis_index_grou...  13.2 us
    ppermute x3, starting transfers between devices, per_device(): other = lax.ppermute(w_half, 'col', [(i, i ^ bit) for i in range(cols)])  12.4 us
    ppermute x7, waiting for transfers between devices, shifted(): lax.ppermute(value, axis, [(i, (i + by) % size) for i in range(size)])  12.2 us
    all_to_all x2, waiting for transfers between devices, exchange(): lax.all_to_all(blocks, axis, split_axis=0, concat_axis=0, axis_index_grou...  10.9 us
    pallas_call x1, Pallas kernels, attend(): pl.pallas_call(functools.partial(attend_kernel, samples=samples, scale=1....  5.02 us
  transfers between devices with their start and end apart: 16, of which 6 were waited for; matrix products, arithmetic and copies ran while one was open for 5% of the time, Pallas kernels for 4%

profile of v9, /device:TPU:80, one launch (start us, length us, event | category | flops | bytes accessed | tf_op | source)
XLA Modules:
  0.0 192.1 jit_solution(15833090101931045014)
XLA Ops:
  3.7 64.3 %all_to_all.15 = f32[16,34,128]{2,1,0:T(8,128)S(1)} all-to-all(f32[16,34,128]{2,1,0:T(8,128)S(1)} %pad_maximum_fusion.3), channel_id=1, replica_groups=mesh['job'=2,'row'=16,'col'=8,'samp'=2] {'row'}, dimensions={0} | all-to-all | bytes 557056 | tf_op jit(solution)/shard_map/all_to_all | solution.py:25
  69.8 7.6 %all-to-all-start.1 = ((f32[16,32,512]{2,1,0:T(8,128)}), f32[16,32,512]{2,1,0:T(8,128)S(1)}, u32[]{:S(2)}, u32[]{:S(2)}) async-start(f32[16,32,512]{2,1,0:T(8,128)} %bitcast.12), calls=%async_computation.1 | async-start | bytes 2097152 | tf_op jit(solution)/shard_map/all_to_all | solution.py:25
  77.4 1.8 normalize.1
  79.2 3.0 %collective-permute-start = (bf16[64,768]{1,0:T(8,128)(2,1)}, bf16[64,768]{1,0:T(8,128)(2,1)S(1)}, u32[]{:S(2)}, u32[]{:S(2)}) collective-permute-start(bf16[64,768]{1,0:T(8,128)(2,1)} %get-tuple-element.8), channel_id=1, source_target_pairs={{0,16},{16,0},{32,48},{48,32},{64,80},{80,64},{96,112},{112,96},{1... | collective-permute-start | bytes 294920 | tf_op jit(solution)/shard_map/ppermute | solution.py:218
  83.2 7.6 %collective-permute-start.10 = (bf16[96,384]{1,0:T(8,128)(2,1)S(1)}, bf16[96,384]{1,0:T(8,128)(2,1)S(1)}, u32[]{:S(2)}, u32[]{:S(2)}) collective-permute-start(bf16[96,384]{1,0:T(8,128)(2,1)S(1)} %reshape.106), channel_id=1, source_target_pairs={{0,8},{2,10},{4,12},{6,14},{8,0},{10,2},{12,4},{14,6},{1,9},{3,11}... | collective-permute-start | bytes 221192 | tf_op jit(solution)/shard_map/ppermute | solution.py:253
  90.8 4.4 %collective-permute-start.1 = (bf16[128,768]{1,0:T(8,128)(2,1)S(1)}, bf16[128,768]{1,0:T(8,128)(2,1)S(1)}, u32[]{:S(2)}, u32[]{:S(2)}) collective-permute-start(bf16[128,768]{1,0:T(8,128)(2,1)S(1)} %constant_dynamic-update-slice_fusion.refs_0_), channel_id=1, source_target_pairs={{0,32},{16,48},{32,64},{48,80},{64,96},{80,112},{96,128},{112,144}... | collective-permute-start | bytes 589832 | tf_op jit(solution)/shard_map/ppermute | solution.py:204
  95.3 13.5 %collective-permute-done.10 = bf16[96,384]{1,0:T(8,128)(2,1)S(1)} collective-permute-done((bf16[96,384]{1,0:T(8,128)(2,1)S(1)}, bf16[96,384]{1,0:T(8,128)(2,1)S(1)}, u32[]{:S(2)}, u32[]{:S(2)}) %collective-permute-start.10) | collective-permute-done | bytes 73760 | tf_op jit(solution)/shard_map/ppermute | solution.py:253
  108.8 2.2 %collective-permute-start.11 = (bf16[2,96,384]{2,1,0:T(8,128)(2,1)S(1)}, bf16[2,96,384]{2,1,0:T(8,128)(2,1)S(1)}, u32[]{:S(2)}, u32[]{:S(2)}) collective-permute-start(bf16[2,96,384]{2,1,0:T(8,128)(2,1)S(1)} %pad_maximum_fusion.5), channel_id=1, source_target_pairs={{0,4},{2,6},{4,0},{6,2},{8,12},{10,14},{12,8},{14,10},{1,5},{3,7},... | collective-permute-start | bytes 442376 | tf_op jit(solution)/shard_map/ppermute | solution.py:253
  111.1 5.4 %collective-permute-start.5 = (bf16[128,768]{1,0:T(8,128)(2,1)S(1)}, bf16[128,768]{1,0:T(8,128)(2,1)S(1)}, u32[]{:S(2)}, u32[]{:S(2)}) collective-permute-start(bf16[128,768]{1,0:T(8,128)(2,1)S(1)} %constant_dynamic-update-slice_fusion.refs_0_), channel_id=1, source_target_pairs={{0,224},{16,240},{32,0},{48,16},{64,32},{80,48},{96,64},{112,80},{... | collective-permute-start | bytes 589832 | tf_op jit(solution)/shard_map/ppermute | solution.py:204
  116.5 2.0 %collective-permute-start.2 = (bf16[128,768]{1,0:T(8,128)(2,1)S(1)}, bf16[128,768]{1,0:T(8,128)(2,1)S(1)}, u32[]{:S(2)}, u32[]{:S(2)}) collective-permute-start(bf16[128,768]{1,0:T(8,128)(2,1)S(1)} %collective-permute-done.1.refs_1_), channel_id=1, source_target_pairs={{0,32},{16,48},{32,64},{48,80},{64,96},{80,112},{96,128},{112,144}... | collective-permute-start | bytes 589832 | tf_op jit(solution)/shard_map/ppermute | solution.py:204
  119.7 2.0 %collective-permute-start.9 = (f32[512,512]{1,0:T(8,128)S(1)}, f32[512,512]{1,0:T(8,128)S(1)}, u32[]{:S(2)}, u32[]{:S(2)}) collective-permute-start(f32[512,512]{1,0:T(8,128)S(1)} %bitcast.41), channel_id=1, source_target_pairs={{0,1},{1,0},{2,3},{3,2},{4,5},{5,4},{6,7},{7,6},{8,9},{9,8},{10,11... | collective-permute-start | bytes 3145736 | tf_op jit(solution)/shard_map/ppermute | solution.py:248
  121.8 2.6 %collective-permute-start.12 = (bf16[2,2,96,384]{3,2,0,1:T(8,128)(2,1)S(1)}, bf16[2,2,96,384]{3,2,0,1:T(8,128)(2,1)}, u32[]{:S(2)}, u32[]{:S(2)}) collective-permute-start(bf16[2,2,96,384]{3,2,0,1:T(8,128)(2,1)S(1)} %pad_maximum_fusion.4), channel_id=1, source_target_pairs={{0,2},{2,0},{4,6},{6,4},{8,10},{10,8},{12,14},{14,12},{1,3},{3,1},... | collective-permute-start | bytes 884744 | tf_op jit(solution)/shard_map/ppermute | solution.py:253
  124.3 4.2 %collective-permute-start.8 = (bf16[3,768,48]{1,2,0:T(8,128)(2,1)}, bf16[3,768,48]{1,2,0:T(8,128)(2,1)}, u32[]{:S(2)}, u32[]{:S(2)}) collective-permute-start(bf16[3,768,48]{1,2,0:T(8,128)(2,1)} %bitcast.47), channel_id=1, source_target_pairs={{0,16},{16,0},{32,48},{48,32},{64,80},{80,64},{96,112},{112,96},{1... | collective-permute-start | bytes 663560 | tf_op jit(solution)/shard_map/ppermute | solution.py:228
  129.3 6.1 %collective-permute-start.6 = (bf16[128,768]{1,0:T(8,128)(2,1)S(1)}, bf16[128,768]{1,0:T(8,128)(2,1)S(1)}, u32[]{:S(2)}, u32[]{:S(2)}) collective-permute-start(bf16[128,768]{1,0:T(8,128)(2,1)S(1)} %collective-permute-done.5.refs_7_), channel_id=1, source_target_pairs={{0,224},{16,240},{32,0},{48,16},{64,32},{80,48},{96,64},{112,80},{... | collective-permute-start | bytes 589832 | tf_op jit(solution)/shard_map/ppermute | solution.py:204
  135.4 2.0 %collective-permute-start.3 = (bf16[128,768]{1,0:T(8,128)(2,1)S(1)}, bf16[128,768]{1,0:T(8,128)(2,1)S(1)}, u32[]{:S(2)}, u32[]{:S(2)}) collective-permute-start(bf16[128,768]{1,0:T(8,128)(2,1)S(1)} %collective-permute-done.2.refs_2_), channel_id=1, source_target_pairs={{0,32},{16,48},{32,64},{48,80},{64,96},{80,112},{96,128},{112,144}... | collective-permute-start | bytes 589832 | tf_op jit(solution)/shard_map/ppermute | solution.py:204
  137.5 6.2 %collective-permute-done.6.refs_6_ = bf16[128,768]{1,0:T(8,128)(2,1)S(1)} collective-permute-done((bf16[128,768]{1,0:T(8,128)(2,1)S(1)}, bf16[128,768]{1,0:T(8,128)(2,1)S(1)}, u32[]{:S(2)}, u32[]{:S(2)}) %collective-permute-start.6) | collective-permute-done | bytes 196640 | tf_op jit(solution)/shard_map/ppermute | solution.py:204
  143.7 6.5 %collective-permute-start.7 = (bf16[128,768]{1,0:T(8,128)(2,1)S(1)}, bf16[128,768]{1,0:T(8,128)(2,1)S(1)}, u32[]{:S(2)}, u32[]{:S(2)}) collective-permute-start(bf16[128,768]{1,0:T(8,128)(2,1)S(1)} %collective-permute-done.6.refs_6_), channel_id=1, source_target_pairs={{0,224},{16,240},{32,0},{48,16},{64,32},{80,48},{96,64},{112,80},{... | collective-permute-start | bytes 589832 | tf_op jit(solution)/shard_map/ppermute | solution.py:204
  150.2 2.0 %collective-permute-start.4 = (bf16[128,768]{1,0:T(8,128)(2,1)S(1)}, bf16[128,768]{1,0:T(8,128)(2,1)S(1)}, u32[]{:S(2)}, u32[]{:S(2)}) collective-permute-start(bf16[128,768]{1,0:T(8,128)(2,1)S(1)} %collective-permute-done.3.refs_3_), channel_id=1, source_target_pairs={{0,32},{16,48},{32,64},{48,80},{64,96},{80,112},{96,128},{112,144}... | collective-permute-start | bytes 589832 | tf_op jit(solution)/shard_map/ppermute | solution.py:204
  154.2 1.9 %collective-permute-start.13 = (bf16[2,2,2,96,384]{4,3,0,1,2:T(8,128)(2,1)}, bf16[2,2,2,96,384]{4,3,0,1,2:T(8,128)(2,1)}, u32[]{:S(2)}, u32[]{:S(2)}) collective-permute-start(bf16[2,2,2,96,384]{4,3,0,1,2:T(8,128)(2,1)} %pad_maximum_fusion.1), channel_id=1, source_target_pairs={{0,1},{1,0},{2,3},{3,2},{4,5},{5,4},{6,7},{7,6},{8,9},{9,8},{10,11... | collective-permute-start | bytes 1769480 | tf_op jit(solution)/shard_map/ppermute | solution.py:259
  158.2 5.0 %collective-permute-done.4.refs_4_ = bf16[128,768]{1,0:T(8,128)(2,1)S(1)} collective-permute-done((bf16[128,768]{1,0:T(8,128)(2,1)S(1)}, bf16[128,768]{1,0:T(8,128)(2,1)S(1)}, u32[]{:S(2)}, u32[]{:S(2)}) %collective-permute-start.4) | collective-permute-done | bytes 196640 | tf_op jit(solution)/shard_map/ppermute | solution.py:204
  163.2 5.0 %attend.1 = bf16[16,48,128]{2,1,0:T(8,128)(2,1)} custom-call(s32[2]{0:T(128)S(1)} %pad_add_fusion.info_1_ref, s32[3]{0:T(128)S(1)} %pad_add_fusion.1.info_2_ref, bf16[128,768]{1,0:T(8,128)(2,1)S(1)} %constant_dynamic-update-slice_fusion.refs_0_, bf16[128,768]{1,0:T(8,128)(2,1)S(1)} %collective-permute-done.1.refs_1_, ...), custom_call_target="tpu_custom_call" | custom-call | flops 654311424 | bytes 6291456 | tf_op jit(solution)/shard_map/attend/pallas_call | solution.py:163
  168.3 5.6 %all-to-all-start.2 = ((bf16[16,48,128]{2,1,0:T(8,128)(2,1)}), bf16[16,48,128]{2,1,0:T(8,128)(2,1)}, u32[]{:S(2)}, u32[]{:S(2)}) async-start(bf16[16,48,128]{2,1,0:T(8,128)(2,1)} %attend.1), calls=%async_computation.2 | async-start | bytes 393216 | tf_op jit(solution)/shard_map/all_to_all | solution.py:25
  178.5 10.9 %all-to-all-done.2.back_ref = bf16[16,48,128]{2,1,0:T(8,128)(2,1)} async-done(((bf16[16,48,128]{2,1,0:T(8,128)(2,1)}), bf16[16,48,128]{2,1,0:T(8,128)(2,1)}, u32[]{:S(2)}, u32[]{:S(2)}) %all-to-all-start.2) | async-done | bytes 196640 | tf_op jit(solution)/shard_map/all_to_all | solution.py:25
  189.4 2.7 %output.1 = bf16[4,32,768]{2,1,0:T(8,128)(2,1)} custom-call(bf16[16,48,128]{2,1,0:T(8,128)(2,1)} %all-to-all-done.2.back_ref, bf16[768,768]{1,0:T(8,128)(2,1)} %reshape.108.w_ref, bf16[4,32,768]{2,1,0:T(8,128)(2,1)} %tokens_ref.3), custom_call_target="tpu_custom_call" | custom-call | flops 150994944 | bytes 4194304 | tf_op jit(solution)/shard_map/output/pallas_call | solution.py:145
  (68 shorter events, 16.5 us)
Async XLA Ops:
  0.0 2.3 %copy-start = (bf16[128,128]{1,0:T(8,128)(2,1)S(1)}, bf16[128,128]{1,0:T(8,128)(2,1)}, u32[]{:S(2)}) copy-start(bf16[128,128]{1,0:T(8,128)(2,1)} %param.13) | copy-start | bytes 98308
  0.0 2.0 %copy-start.5 = (s32[512]{0:T(512)S(1)}, s32[512]{0:T(512)}, u32[]{:S(2)}) copy-start(s32[512]{0:T(512)} %param.11) | copy-start | bytes 6148
  1.8 1.5 copy-start.4
  1.8 1.5 copy-start.6
  69.8 50.0 %all-to-all-start.1 = ((f32[16,32,512]{2,1,0:T(8,128)}), f32[16,32,512]{2,1,0:T(8,128)S(1)}, u32[]{:S(2)}, u32[]{:S(2)}) async-start(f32[16,32,512]{2,1,0:T(8,128)} %bitcast.12), calls=%async_computation.1 | async-start | bytes 2097152 | tf_op jit(solution)/shard_map/all_to_all | solution.py:25
  79.2 11.6 %collective-permute-start = (bf16[64,768]{1,0:T(8,128)(2,1)}, bf16[64,768]{1,0:T(8,128)(2,1)S(1)}, u32[]{:S(2)}, u32[]{:S(2)}) collective-permute-start(bf16[64,768]{1,0:T(8,128)(2,1)} %get-tuple-element.8), channel_id=1, source_target_pairs={{0,16},{16,0},{32,48},{48,32},{64,80},{80,64},{96,112},{112,96},{1... | collective-permute-start | bytes 294920 | tf_op jit(solution)/shard_map/ppermute | solution.py:218
  83.2 25.5 %collective-permute-start.10 = (bf16[96,384]{1,0:T(8,128)(2,1)S(1)}, bf16[96,384]{1,0:T(8,128)(2,1)S(1)}, u32[]{:S(2)}, u32[]{:S(2)}) collective-permute-start(bf16[96,384]{1,0:T(8,128)(2,1)S(1)} %reshape.106), channel_id=1, source_target_pairs={{0,8},{2,10},{4,12},{6,14},{8,0},{10,2},{12,4},{14,6},{1,9},{3,11}... | collective-permute-start | bytes 221192 | tf_op jit(solution)/shard_map/ppermute | solution.py:253
  90.8 25.6 %collective-permute-start.1 = (bf16[128,768]{1,0:T(8,128)(2,1)S(1)}, bf16[128,768]{1,0:T(8,128)(2,1)S(1)}, u32[]{:S(2)}, u32[]{:S(2)}) collective-permute-start(bf16[128,768]{1,0:T(8,128)(2,1)S(1)} %constant_dynamic-update-slice_fusion.refs_0_), channel_id=1, source_target_pairs={{0,32},{16,48},{32,64},{48,80},{64,96},{80,112},{96,128},{112,144}... | collective-permute-start | bytes 589832 | tf_op jit(solution)/shard_map/ppermute | solution.py:204
  108.8 10.9 %collective-permute-start.11 = (bf16[2,96,384]{2,1,0:T(8,128)(2,1)S(1)}, bf16[2,96,384]{2,1,0:T(8,128)(2,1)S(1)}, u32[]{:S(2)}, u32[]{:S(2)}) collective-permute-start(bf16[2,96,384]{2,1,0:T(8,128)(2,1)S(1)} %pad_maximum_fusion.5), channel_id=1, source_target_pairs={{0,4},{2,6},{4,0},{6,2},{8,12},{10,14},{12,8},{14,10},{1,5},{3,7},... | collective-permute-start | bytes 442376 | tf_op jit(solution)/shard_map/ppermute | solution.py:253
  111.1 18.2 %collective-permute-start.5 = (bf16[128,768]{1,0:T(8,128)(2,1)S(1)}, bf16[128,768]{1,0:T(8,128)(2,1)S(1)}, u32[]{:S(2)}, u32[]{:S(2)}) collective-permute-start(bf16[128,768]{1,0:T(8,128)(2,1)S(1)} %constant_dynamic-update-slice_fusion.refs_0_), channel_id=1, source_target_pairs={{0,224},{16,240},{32,0},{48,16},{64,32},{80,48},{96,64},{112,80},{... | collective-permute-start | bytes 589832 | tf_op jit(solution)/shard_map/ppermute | solution.py:204
  116.5 18.9 %collective-permute-start.2 = (bf16[128,768]{1,0:T(8,128)(2,1)S(1)}, bf16[128,768]{1,0:T(8,128)(2,1)S(1)}, u32[]{:S(2)}, u32[]{:S(2)}) collective-permute-start(bf16[128,768]{1,0:T(8,128)(2,1)S(1)} %collective-permute-done.1.refs_1_), channel_id=1, source_target_pairs={{0,32},{16,48},{32,64},{48,80},{64,96},{80,112},{96,128},{112,144}... | collective-permute-start | bytes 589832 | tf_op jit(solution)/shard_map/ppermute | solution.py:204
  119.7 32.5 %copy-start.1 = (bf16[2,1,96,384]{3,2,0,1:T(8,128)(2,1)}, bf16[2,1,96,384]{3,2,0,1:T(8,128)(2,1)S(1)}, u32[]{:S(2)}) copy-start(bf16[2,1,96,384]{3,2,0,1:T(8,128)(2,1)S(1)} %get-tuple-element.15) | copy-start | bytes 442372
  119.7 32.5 %copy-start.2 = (bf16[2,1,96,384]{3,2,0,1:T(8,128)(2,1)}, bf16[2,1,96,384]{3,2,0,1:T(8,128)(2,1)S(1)}, u32[]{:S(2)}) copy-start(bf16[2,1,96,384]{3,2,0,1:T(8,128)(2,1)S(1)} %get-tuple-element.16) | copy-start | bytes 442372
  119.7 43.5 %collective-permute-start.9 = (f32[512,512]{1,0:T(8,128)S(1)}, f32[512,512]{1,0:T(8,128)S(1)}, u32[]{:S(2)}, u32[]{:S(2)}) collective-permute-start(f32[512,512]{1,0:T(8,128)S(1)} %bitcast.41), channel_id=1, source_target_pairs={{0,1},{1,0},{2,3},{3,2},{4,5},{5,4},{6,7},{7,6},{8,9},{9,8},{10,11... | collective-permute-start | bytes 3145736 | tf_op jit(solution)/shard_map/ppermute | solution.py:248
  121.8 30.4 %collective-permute-start.12 = (bf16[2,2,96,384]{3,2,0,1:T(8,128)(2,1)S(1)}, bf16[2,2,96,384]{3,2,0,1:T(8,128)(2,1)}, u32[]{:S(2)}, u32[]{:S(2)}) collective-permute-start(bf16[2,2,96,384]{3,2,0,1:T(8,128)(2,1)S(1)} %pad_maximum_fusion.4), channel_id=1, source_target_pairs={{0,2},{2,0},{4,6},{6,4},{8,10},{10,8},{12,14},{14,12},{1,3},{3,1},... | collective-permute-start | bytes 884744 | tf_op jit(solution)/shard_map/ppermute | solution.py:253
  124.3 31.8 %collective-permute-start.8 = (bf16[3,768,48]{1,2,0:T(8,128)(2,1)}, bf16[3,768,48]{1,2,0:T(8,128)(2,1)}, u32[]{:S(2)}, u32[]{:S(2)}) collective-permute-start(bf16[3,768,48]{1,2,0:T(8,128)(2,1)} %bitcast.47), channel_id=1, source_target_pairs={{0,16},{16,0},{32,48},{48,32},{64,80},{80,64},{96,112},{112,96},{1... | collective-permute-start | bytes 663560 | tf_op jit(solution)/shard_map/ppermute | solution.py:228
  129.3 14.4 %collective-permute-start.6 = (bf16[128,768]{1,0:T(8,128)(2,1)S(1)}, bf16[128,768]{1,0:T(8,128)(2,1)S(1)}, u32[]{:S(2)}, u32[]{:S(2)}) collective-permute-start(bf16[128,768]{1,0:T(8,128)(2,1)S(1)} %collective-permute-done.5.refs_7_), channel_id=1, source_target_pairs={{0,224},{16,240},{32,0},{48,16},{64,32},{80,48},{96,64},{112,80},{... | collective-permute-start | bytes 589832 | tf_op jit(solution)/shard_map/ppermute | solution.py:204
  135.4 14.8 %collective-permute-start.3 = (bf16[128,768]{1,0:T(8,128)(2,1)S(1)}, bf16[128,768]{1,0:T(8,128)(2,1)S(1)}, u32[]{:S(2)}, u32[]{:S(2)}) collective-permute-start(bf16[128,768]{1,0:T(8,128)(2,1)S(1)} %collective-permute-done.2.refs_2_), channel_id=1, source_target_pairs={{0,32},{16,48},{32,64},{48,80},{64,96},{80,112},{96,128},{112,144}... | collective-permute-start | bytes 589832 | tf_op jit(solution)/shard_map/ppermute | solution.py:204
  137.5 18.7 %copy-start.3 = (bf16[1,3,768,48]{2,3,1,0:T(8,128)(2,1)S(1)}, bf16[1,3,768,48]{2,3,1,0:T(8,128)(2,1)}, u32[]{:S(2)}) copy-start(bf16[1,3,768,48]{2,3,1,0:T(8,128)(2,1)} %param.18) | copy-start | bytes 663556
  143.7 14.5 %collective-permute-start.7 = (bf16[128,768]{1,0:T(8,128)(2,1)S(1)}, bf16[128,768]{1,0:T(8,128)(2,1)S(1)}, u32[]{:S(2)}, u32[]{:S(2)}) collective-permute-start(bf16[128,768]{1,0:T(8,128)(2,1)S(1)} %collective-permute-done.6.refs_6_), channel_id=1, source_target_pairs={{0,224},{16,240},{32,0},{48,16},{64,32},{80,48},{96,64},{112,80},{... | collective-permute-start | bytes 589832 | tf_op jit(solution)/shard_map/ppermute | solution.py:204
  150.2 13.0 %collective-permute-start.4 = (bf16[128,768]{1,0:T(8,128)(2,1)S(1)}, bf16[128,768]{1,0:T(8,128)(2,1)S(1)}, u32[]{:S(2)}, u32[]{:S(2)}) collective-permute-start(bf16[128,768]{1,0:T(8,128)(2,1)S(1)} %collective-permute-done.3.refs_3_), channel_id=1, source_target_pairs={{0,32},{16,48},{32,64},{48,80},{64,96},{80,112},{96,128},{112,144}... | collective-permute-start | bytes 589832 | tf_op jit(solution)/shard_map/ppermute | solution.py:204
  154.2 19.6 %collective-permute-start.13 = (bf16[2,2,2,96,384]{4,3,0,1,2:T(8,128)(2,1)}, bf16[2,2,2,96,384]{4,3,0,1,2:T(8,128)(2,1)}, u32[]{:S(2)}, u32[]{:S(2)}) collective-permute-start(bf16[2,2,2,96,384]{4,3,0,1,2:T(8,128)(2,1)} %pad_maximum_fusion.1), channel_id=1, source_target_pairs={{0,1},{1,0},{2,3},{3,2},{4,5},{5,4},{6,7},{7,6},{8,9},{9,8},{10,11... | collective-permute-start | bytes 1769480 | tf_op jit(solution)/shard_map/ppermute | solution.py:259
  168.3 21.1 %all-to-all-start.2 = ((bf16[16,48,128]{2,1,0:T(8,128)(2,1)}), bf16[16,48,128]{2,1,0:T(8,128)(2,1)}, u32[]{:S(2)}, u32[]{:S(2)}) async-start(bf16[16,48,128]{2,1,0:T(8,128)(2,1)} %attend.1), calls=%async_computation.2 | async-start | bytes 393216 | tf_op jit(solution)/shard_map/all_to_all | solution.py:25

commit v10 on v9

--- a/solution.py
+++ b/solution.py
@@ -122,36 +122,41 @@
         ).astype(jnp.bfloat16)
 
 
-def output_kernel(back_ref, w_ref, tokens_ref, out_ref):
+def output_kernel(core_ref, back_ref, own_ref, other_ref, tokens_ref, out_ref):
     rows, _, lanes = back_ref.shape
     half_samples = tokens_ref.shape[0] // 2
     half = lanes // 2
+    width = own_ref.shape[1]
+    core = core_ref[0]
     for side in range(2):
         pieces = []
         for k in range(rows // 2):
             block = back_ref[2 * k + side].astype(jnp.float32)
             pieces += [block[:, :half], block[:, half:]]
         attended = jnp.concatenate(pieces).astype(jnp.bfloat16)
-        update = lax.dot_general(
-            attended, w_ref[...], (((0,), (0,)), ((), ())), preferred_element_type=jnp.float32
-        )
         samples = pl.ds(side * half_samples, half_samples)
-        before = tokens_ref[samples].astype(jnp.float32)
-        out_ref[samples] = (before + update.reshape(before.shape)).astype(jnp.bfloat16)
-
-
-def output(back, w_out, tokens):
+        for w_ref, place in ((own_ref, core), (other_ref, 1 - core)):
+            update = lax.dot_general(
+                attended, w_ref[...], (((0,), (0,)), ((), ())), preferred_element_type=jnp.float32
+            )
+            columns = pl.ds(pl.multiple_of(place * width, 128), width)
+            before = tokens_ref[samples, :, columns].astype(jnp.float32)
+            after = before + update.reshape(before.shape)
+            out_ref[samples, :, columns] = after.astype(jnp.bfloat16)
+
+
+def output(core, back, own, other, tokens):
     vmem = pl.BlockSpec(memory_space=pltpu.VMEM)
     return pl.pallas_call(
         output_kernel,
         out_shape=jax.ShapeDtypeStruct(tokens.shape, jnp.bfloat16),
-        in_specs=[vmem, vmem, vmem],
+        in_specs=[pl.BlockSpec(memory_space=pltpu.SMEM)] + [vmem] * 4,
         out_specs=vmem,
         cost_estimate=pl.CostEstimate(
-            flops=2 * tokens.size * w_out.shape[0], bytes_accessed=4 * 1024 * 1024, transcendentals=0
+            flops=2 * tokens.size * own.shape[0], bytes_accessed=4 * 1024 * 1024, transcendentals=0
         ),
         name="output",
-    )(back, w_out, tokens)
+    )(core, back, own, other, tokens)
 
 
 def attend(info_1, info_2, blocks, w, bias_a, bias_b, samples):
@@ -199,6 +204,7 @@
     col = lax.axis_index("col")
     core = lax.axis_index("samp")
     swap = [(0, 1), (1, 0)]
+
     def shifted(value, axis, by):
         size = lax.axis_size(axis)
         return lax.ppermute(value, axis, [(i, (i + by) % size) for i in range(size)])
@@ -257,15 +263,14 @@
         )
         bit, place = bit // 2, place + 1
     other = lax.ppermute(w_half, "samp", swap)
-    w_out = jnp.concatenate(
-        [jnp.where(core == 0, w_half, other), jnp.where(core == 0, other, w_half)], axis=-1
-    )
-    w_out = w_out.reshape(cols, rows, slice_rows, width).transpose(1, 0, 2, 3)
-    w_out = w_out.reshape(width, width)
+
+    def arranged(half):
+        half = half.reshape(cols, rows, slice_rows, half_width).transpose(1, 0, 2, 3)
+        return half.reshape(width, half_width)
 
     attended = attend(info_1, info_2, blocks, w_pair, bias_a, bias_b, half_samples)
     back = exchange(attended, "row")
-    return output(back, w_out, tokens)
+    return output(core.reshape(1), back, arranged(w_half), arranged(other), tokens)
 
 
 def solution(mesh):

time: 193 us -> 181 us (0.938)
  waiting for transfers between devices: 37.9 us -> 21.2 us
  local copies, waits for them, and re-layouts: 6.53 us -> 9.26 us
    ppermute x3, waiting for transfers between devices: 14.7 us -> 1.28 us  [per_device(): other = lax.ppermute(w_half, 'col', [(i, i ^ bit) for i in range(cols)])]
    ppermute x7, waiting for transfers between devices: 12.2 us -> 8.02 us  [shifted(): lax.ppermute(value, axis, [(i, (i + by) % size) for i in range(size)])]
    ppermute x1, waiting for transfers between devices: 0.01 us -> 3.11 us  [per_device(): given = lax.ppermute(give, 'row', neighbour)]
    ppermute x1, starting transfers between devices: 4.25 us -> 7.09 us  [per_device(): other_w = lax.ppermute(qkv_weight[0], 'row', neighbour)]
    all_to_all x2, waiting for transfers between devices: 10.9 us -> 8.77 us  [exchange(): lax.all_to_all(blocks, axis, split_axis=0, concat_axis=0, axis_index_grou...]
    unnamed x15 -> x17, local copies, waits for them, and re-layouts: 0.94 us -> 2.95 us
where the time goes in v10:
time: 181 us; the launch traced here: 180 us
  starting transfers between devices  66.3 us (37%)
  blocking collectives  64.3 us (36%)
  waiting for transfers between devices  21.2 us (12%)
  Pallas kernels  9.48 us (5%)
  local copies, waits for them, and re-layouts  9.26 us (5%)
  other arithmetic  6.8 us (4%)
    all_to_all x1, blocking collectives, exchange(): lax.all_to_all(blocks, axis, split_axis=0, concat_axis=0, axis_index_grou...  64.3 us
    ppermute x7, starting transfers between devices, shifted(): lax.ppermute(value, axis, [(i, (i + by) % size) for i in range(size)])  26.8 us
    all_to_all x2, starting transfers between devices, exchange(): lax.all_to_all(blocks, axis, split_axis=0, concat_axis=0, axis_index_grou...  13.6 us
    ppermute x3, starting transfers between devices, per_device(): other = lax.ppermute(w_half, 'col', [(i, i ^ bit) for i in range(cols)])  11.8 us
    all_to_all x2, waiting for transfers between devices, exchange(): lax.all_to_all(blocks, axis, split_axis=0, concat_axis=0, axis_index_grou...  8.77 us
    ppermute x7, waiting for transfers between devices, shifted(): lax.ppermute(value, axis, [(i, (i + by) % size) for i in range(size)])  8.02 us
    ppermute x1, starting transfers between devices, per_device(): other_w = lax.ppermute(qkv_weight[0], 'row', neighbour)  7.09 us
    pallas_call x1, Pallas kernels, attend(): pl.pallas_call(functools.partial(attend_kernel, samples=samples, scale=1....  5.02 us
  transfers between devices with their start and end apart: 16, of which 6 were waited for; matrix products, arithmetic and copies ran while one was open for 5% of the time, Pallas kernels for 4%

profile of v10, /device:TPU:80, one launch (start us, length us, event | category | flops | bytes accessed | tf_op | source)
XLA Modules:
  0.0 179.6 jit_solution(7899696231096458230)
XLA Ops:
  5.0 64.3 %all_to_all.15 = f32[16,34,128]{2,1,0:T(8,128)S(1)} all-to-all(f32[16,34,128]{2,1,0:T(8,128)S(1)} %pad_maximum_fusion.2), channel_id=1, replica_groups=mesh['job'=2,'row'=16,'col'=8,'samp'=2] {'row'}, dimensions={0} | all-to-all | bytes 557056 | tf_op jit(solution)/shard_map/all_to_all | solution.py:25
  71.1 7.6 %all-to-all-start.1 = ((f32[16,32,512]{2,1,0:T(8,128)}), f32[16,32,512]{2,1,0:T(8,128)S(1)}, u32[]{:S(2)}, u32[]{:S(2)}) async-start(f32[16,32,512]{2,1,0:T(8,128)} %bitcast.12), calls=%async_computation.1 | async-start | bytes 2097152 | tf_op jit(solution)/shard_map/all_to_all | solution.py:25
  78.7 1.8 %normalize.1 = (bf16[64,768]{1,0:T(8,128)(2,1)}, bf16[64,768]{1,0:T(8,128)(2,1)}) custom-call(s32[1]{0:T(128)} %bitcast.1.side_ref, bf16[4,32,768]{2,1,0:T(8,128)(2,1)} %tokens_ref.3, f32[1,768]{1,0:T(1,128)} %gain_ref.1), custom_call_target="tpu_custom_call" | custom-call | flops 983040 | bytes 393216 | tf_op jit(solution)/shard_map/normalize/pallas_call | solution.py:69
  80.5 3.0 %collective-permute-start = (bf16[64,768]{1,0:T(8,128)(2,1)}, bf16[64,768]{1,0:T(8,128)(2,1)S(1)}, u32[]{:S(2)}, u32[]{:S(2)}) collective-permute-start(bf16[64,768]{1,0:T(8,128)(2,1)} %get-tuple-element.8), channel_id=1, source_target_pairs={{0,16},{16,0},{32,48},{48,32},{64,80},{80,64},{96,112},{112,96},{1... | collective-permute-start | bytes 294920 | tf_op jit(solution)/shard_map/ppermute | solution.py:224
  84.5 3.1 %collective-permute-done = bf16[64,768]{1,0:T(8,128)(2,1)S(1)} collective-permute-done((bf16[64,768]{1,0:T(8,128)(2,1)}, bf16[64,768]{1,0:T(8,128)(2,1)S(1)}, u32[]{:S(2)}, u32[]{:S(2)}) %collective-permute-start) | collective-permute-done | bytes 98336 | tf_op jit(solution)/shard_map/ppermute | solution.py:224
  87.6 4.4 %collective-permute-start.1 = (bf16[128,768]{1,0:T(8,128)(2,1)S(1)}, bf16[128,768]{1,0:T(8,128)(2,1)S(1)}, u32[]{:S(2)}, u32[]{:S(2)}) collective-permute-start(bf16[128,768]{1,0:T(8,128)(2,1)S(1)} %constant_dynamic-update-slice_fusion.refs_0_), channel_id=1, source_target_pairs={{0,32},{16,48},{32,64},{48,80},{64,96},{80,112},{96,128},{112,144}... | collective-permute-start | bytes 589832 | tf_op jit(solution)/shard_map/ppermute | solution.py:210
  92.0 3.6 %collective-permute-start.5 = (bf16[128,768]{1,0:T(8,128)(2,1)S(1)}, bf16[128,768]{1,0:T(8,128)(2,1)S(1)}, u32[]{:S(2)}, u32[]{:S(2)}) collective-permute-start(bf16[128,768]{1,0:T(8,128)(2,1)S(1)} %constant_dynamic-update-slice_fusion.refs_0_), channel_id=1, source_target_pairs={{0,224},{16,240},{32,0},{48,16},{64,32},{80,48},{96,64},{112,80},{... | collective-permute-start | bytes 589832 | tf_op jit(solution)/shard_map/ppermute | solution.py:210
  95.6 2.8 %collective-permute-done.1.refs_1_ = bf16[128,768]{1,0:T(8,128)(2,1)S(1)} collective-permute-done((bf16[128,768]{1,0:T(8,128)(2,1)S(1)}, bf16[128,768]{1,0:T(8,128)(2,1)S(1)}, u32[]{:S(2)}, u32[]{:S(2)}) %collective-permute-start.1) | collective-permute-done | bytes 196640 | tf_op jit(solution)/shard_map/ppermute | solution.py:210
  98.4 2.7 %collective-permute-start.2 = (bf16[128,768]{1,0:T(8,128)(2,1)S(1)}, bf16[128,768]{1,0:T(8,128)(2,1)S(1)}, u32[]{:S(2)}, u32[]{:S(2)}) collective-permute-start(bf16[128,768]{1,0:T(8,128)(2,1)S(1)} %collective-permute-done.1.refs_1_), channel_id=1, source_target_pairs={{0,32},{16,48},{32,64},{48,80},{64,96},{80,112},{96,128},{112,144}... | collective-permute-start | bytes 589832 | tf_op jit(solution)/shard_map/ppermute | solution.py:210
  101.3 7.4 %collective-permute-start.10 = (bf16[96,384]{1,0:T(8,128)(2,1)S(1)}, bf16[96,384]{1,0:T(8,128)(2,1)S(1)}, u32[]{:S(2)}, u32[]{:S(2)}) collective-permute-start(bf16[96,384]{1,0:T(8,128)(2,1)S(1)} %reshape.116), channel_id=1, source_target_pairs={{0,8},{2,10},{4,12},{6,14},{8,0},{10,2},{12,4},{14,6},{1,9},{3,11}... | collective-permute-start | bytes 221192 | tf_op jit(solution)/shard_map/ppermute | solution.py:259
  108.7 7.1 %collective-permute-start.8 = (bf16[3,768,48]{1,2,0:T(8,128)(2,1)}, bf16[3,768,48]{1,2,0:T(8,128)(2,1)}, u32[]{:S(2)}, u32[]{:S(2)}) collective-permute-start(bf16[3,768,48]{1,2,0:T(8,128)(2,1)} %bitcast.3), channel_id=1, source_target_pairs={{0,16},{16,0},{32,48},{48,32},{64,80},{80,64},{96,112},{112,96},{1... | collective-permute-start | bytes 663560 | tf_op jit(solution)/shard_map/ppermute | solution.py:234
  116.4 5.7 %collective-permute-start.6 = (bf16[128,768]{1,0:T(8,128)(2,1)S(1)}, bf16[128,768]{1,0:T(8,128)(2,1)S(1)}, u32[]{:S(2)}, u32[]{:S(2)}) collective-permute-start(bf16[128,768]{1,0:T(8,128)(2,1)S(1)} %collective-permute-done.5.refs_7_), channel_id=1, source_target_pairs={{0,224},{16,240},{32,0},{48,16},{64,32},{80,48},{96,64},{112,80},{... | collective-permute-start | bytes 589832 | tf_op jit(solution)/shard_map/ppermute | solution.py:210
  122.1 2.0 %collective-permute-start.3 = (bf16[128,768]{1,0:T(8,128)(2,1)S(1)}, bf16[128,768]{1,0:T(8,128)(2,1)S(1)}, u32[]{:S(2)}, u32[]{:S(2)}) collective-permute-start(bf16[128,768]{1,0:T(8,128)(2,1)S(1)} %collective-permute-done.2.refs_2_), channel_id=1, source_target_pairs={{0,32},{16,48},{32,64},{48,80},{64,96},{80,112},{96,128},{112,144}... | collective-permute-start | bytes 589832 | tf_op jit(solution)/shard_map/ppermute | solution.py:210
  124.2 2.0 %collective-permute-start.9 = (f32[512,512]{1,0:T(8,128)S(1)}, f32[512,512]{1,0:T(8,128)S(1)}, u32[]{:S(2)}, u32[]{:S(2)}) collective-permute-start(f32[512,512]{1,0:T(8,128)S(1)} %bitcast.44), channel_id=1, source_target_pairs={{0,1},{1,0},{2,3},{3,2},{4,5},{5,4},{6,7},{7,6},{8,9},{9,8},{10,11... | collective-permute-start | bytes 3145736 | tf_op jit(solution)/shard_map/ppermute | solution.py:254
  126.8 2.5 %collective-permute-start.11 = (bf16[2,96,384]{2,1,0:T(8,128)(2,1)}, bf16[2,96,384]{2,1,0:T(8,128)(2,1)}, u32[]{:S(2)}, u32[]{:S(2)}) collective-permute-start(bf16[2,96,384]{2,1,0:T(8,128)(2,1)} %pad_maximum_fusion.4), channel_id=1, source_target_pairs={{0,4},{2,6},{4,0},{6,2},{8,12},{10,14},{12,8},{14,10},{1,5},{3,7},... | collective-permute-start | bytes 442376 | tf_op jit(solution)/shard_map/ppermute | solution.py:259
  129.6 6.5 %collective-permute-start.7 = (bf16[128,768]{1,0:T(8,128)(2,1)S(1)}, bf16[128,768]{1,0:T(8,128)(2,1)S(1)}, u32[]{:S(2)}, u32[]{:S(2)}) collective-permute-start(bf16[128,768]{1,0:T(8,128)(2,1)S(1)} %collective-permute-done.6.refs_6_), channel_id=1, source_target_pairs={{0,224},{16,240},{32,0},{48,16},{64,32},{80,48},{96,64},{112,80},{... | collective-permute-start | bytes 589832 | tf_op jit(solution)/shard_map/ppermute | solution.py:210
  136.1 2.0 %collective-permute-start.4 = (bf16[128,768]{1,0:T(8,128)(2,1)S(1)}, bf16[128,768]{1,0:T(8,128)(2,1)S(1)}, u32[]{:S(2)}, u32[]{:S(2)}) collective-permute-start(bf16[128,768]{1,0:T(8,128)(2,1)S(1)} %collective-permute-done.3.refs_3_), channel_id=1, source_target_pairs={{0,32},{16,48},{32,64},{48,80},{64,96},{80,112},{96,128},{112,144}... | collective-permute-start | bytes 589832 | tf_op jit(solution)/shard_map/ppermute | solution.py:210
  141.1 1.9 %collective-permute-start.12 = (bf16[2,2,96,384]{3,2,0,1:T(8,128)(2,1)}, bf16[2,2,96,384]{3,2,0,1:T(8,128)(2,1)}, u32[]{:S(2)}, u32[]{:S(2)}) collective-permute-start(bf16[2,2,96,384]{3,2,0,1:T(8,128)(2,1)} %pad_maximum_fusion.3), channel_id=1, source_target_pairs={{0,2},{2,0},{4,6},{6,4},{8,10},{10,8},{12,14},{14,12},{1,3},{3,1},... | collective-permute-start | bytes 884744 | tf_op jit(solution)/shard_map/ppermute | solution.py:259
  144.2 5.0 %collective-permute-done.4.refs_4_ = bf16[128,768]{1,0:T(8,128)(2,1)S(1)} collective-permute-done((bf16[128,768]{1,0:T(8,128)(2,1)S(1)}, bf16[128,768]{1,0:T(8,128)(2,1)S(1)}, u32[]{:S(2)}, u32[]{:S(2)}) %collective-permute-start.4) | collective-permute-done | bytes 196640 | tf_op jit(solution)/shard_map/ppermute | solution.py:210
  149.3 5.0 %attend.1 = bf16[16,48,128]{2,1,0:T(8,128)(2,1)} custom-call(s32[2]{0:T(128)S(1)} %pad_add_fusion.info_1_ref, s32[3]{0:T(128)S(1)} %pad_add_fusion.1.info_2_ref, bf16[128,768]{1,0:T(8,128)(2,1)S(1)} %constant_dynamic-update-slice_fusion.refs_0_, bf16[128,768]{1,0:T(8,128)(2,1)S(1)} %collective-permute-done.1.refs_1_, ...), custom_call_target="tpu_custom_call" | custom-call | flops 654311424 | bytes 6291456 | tf_op jit(solution)/shard_map/attend/pallas_call | solution.py:168
  154.3 6.0 %all-to-all-start.2 = ((bf16[16,48,128]{2,1,0:T(8,128)(2,1)}), bf16[16,48,128]{2,1,0:T(8,128)(2,1)S(1)}, u32[]{:S(2)}, u32[]{:S(2)}) async-start(bf16[16,48,128]{2,1,0:T(8,128)(2,1)} %attend.1), calls=%async_computation.2 | async-start | bytes 393216 | tf_op jit(solution)/shard_map/all_to_all | solution.py:25
  161.5 2.0 %collective-permute-start.13 = (bf16[2,2,2,96,384]{4,3,0,1,2:T(8,128)(2,1)S(1)}, bf16[2,2,2,96,384]{4,3,0,1,2:T(8,128)(2,1)S(1)}, u32[]{:S(2)}, u32[]{:S(2)}) collective-permute-start(bf16[2,2,2,96,384]{4,3,0,1,2:T(8,128)(2,1)S(1)} %pad_maximum_fusion), channel_id=1, source_target_pairs={{0,1},{1,0},{2,3},{3,2},{4,5},{5,4},{6,7},{7,6},{8,9},{9,8},{10,11... | collective-permute-start | bytes 1769480 | tf_op jit(solution)/shard_map/ppermute | solution.py:265
  167.5 8.8 %all-to-all-done.2.back_ref = bf16[16,48,128]{2,1,0:T(8,128)(2,1)S(1)} async-done(((bf16[16,48,128]{2,1,0:T(8,128)(2,1)}), bf16[16,48,128]{2,1,0:T(8,128)(2,1)S(1)}, u32[]{:S(2)}, u32[]{:S(2)}) %all-to-all-start.2) | async-done | bytes 196640 | tf_op jit(solution)/shard_map/all_to_all | solution.py:25
  176.9 2.6 %output.1 = bf16[4,32,768]{2,1,0:T(8,128)(2,1)} custom-call(s32[1]{0:T(128)} %bitcast.core_ref, bf16[16,48,128]{2,1,0:T(8,128)(2,1)} %copy-done.3, bf16[768,384]{1,0:T(8,128)(2,1)} %reshape.118.own_ref, bf16[768,384]{1,0:T(8,128)(2,1)} %reshape.120.other_ref, bf16[4,32,768]{2,1,0:T(8,128)(2,1)} %tokens_ref.3), custom_call_target="tpu_custom_call" | custom-call | flops 150994944 | bytes 4194304 | tf_op jit(solution)/shard_map/output/pallas_call | solution.py:150
  (72 shorter events, 18.7 us)
Async XLA Ops:
  0.0 2.9 %copy-start = (bf16[128,128]{1,0:T(8,128)(2,1)S(1)}, bf16[128,128]{1,0:T(8,128)(2,1)}, u32[]{:S(2)}) copy-start(bf16[128,128]{1,0:T(8,128)(2,1)} %param.13) | copy-start | bytes 98308
  2.0 0.7 copy-start.6
  4.0 0.7 copy-start.5
  4.0 0.7 copy-start.7
  71.1 53.1 %all-to-all-start.1 = ((f32[16,32,512]{2,1,0:T(8,128)}), f32[16,32,512]{2,1,0:T(8,128)S(1)}, u32[]{:S(2)}, u32[]{:S(2)}) async-start(f32[16,32,512]{2,1,0:T(8,128)} %bitcast.12), calls=%async_computation.1 | async-start | bytes 2097152 | tf_op jit(solution)/shard_map/all_to_all | solution.py:25
  80.5 7.0 %collective-permute-start = (bf16[64,768]{1,0:T(8,128)(2,1)}, bf16[64,768]{1,0:T(8,128)(2,1)S(1)}, u32[]{:S(2)}, u32[]{:S(2)}) collective-permute-start(bf16[64,768]{1,0:T(8,128)(2,1)} %get-tuple-element.8), channel_id=1, source_target_pairs={{0,16},{16,0},{32,48},{48,32},{64,80},{80,64},{96,112},{112,96},{1... | collective-permute-start | bytes 294920 | tf_op jit(solution)/shard_map/ppermute | solution.py:224
  87.6 10.8 %collective-permute-start.1 = (bf16[128,768]{1,0:T(8,128)(2,1)S(1)}, bf16[128,768]{1,0:T(8,128)(2,1)S(1)}, u32[]{:S(2)}, u32[]{:S(2)}) collective-permute-start(bf16[128,768]{1,0:T(8,128)(2,1)S(1)} %constant_dynamic-update-slice_fusion.refs_0_), channel_id=1, source_target_pairs={{0,32},{16,48},{32,64},{48,80},{64,96},{80,112},{96,128},{112,144}... | collective-permute-start | bytes 589832 | tf_op jit(solution)/shard_map/ppermute | solution.py:210
  92.0 24.4 %collective-permute-start.5 = (bf16[128,768]{1,0:T(8,128)(2,1)S(1)}, bf16[128,768]{1,0:T(8,128)(2,1)S(1)}, u32[]{:S(2)}, u32[]{:S(2)}) collective-permute-start(bf16[128,768]{1,0:T(8,128)(2,1)S(1)} %constant_dynamic-update-slice_fusion.refs_0_), channel_id=1, source_target_pairs={{0,224},{16,240},{32,0},{48,16},{64,32},{80,48},{96,64},{112,80},{... | collective-permute-start | bytes 589832 | tf_op jit(solution)/shard_map/ppermute | solution.py:210
  98.4 23.7 %collective-permute-start.2 = (bf16[128,768]{1,0:T(8,128)(2,1)S(1)}, bf16[128,768]{1,0:T(8,128)(2,1)S(1)}, u32[]{:S(2)}, u32[]{:S(2)}) collective-permute-start(bf16[128,768]{1,0:T(8,128)(2,1)S(1)} %collective-permute-done.1.refs_1_), channel_id=1, source_target_pairs={{0,32},{16,48},{32,64},{48,80},{64,96},{80,112},{96,128},{112,144}... | collective-permute-start | bytes 589832 | tf_op jit(solution)/shard_map/ppermute | solution.py:210
  101.3 22.8 %collective-permute-start.10 = (bf16[96,384]{1,0:T(8,128)(2,1)S(1)}, bf16[96,384]{1,0:T(8,128)(2,1)S(1)}, u32[]{:S(2)}, u32[]{:S(2)}) collective-permute-start(bf16[96,384]{1,0:T(8,128)(2,1)S(1)} %reshape.116), channel_id=1, source_target_pairs={{0,8},{2,10},{4,12},{6,14},{8,0},{10,2},{12,4},{14,6},{1,9},{3,11}... | collective-permute-start | bytes 221192 | tf_op jit(solution)/shard_map/ppermute | solution.py:259
  108.7 34.4 %collective-permute-start.8 = (bf16[3,768,48]{1,2,0:T(8,128)(2,1)}, bf16[3,768,48]{1,2,0:T(8,128)(2,1)}, u32[]{:S(2)}, u32[]{:S(2)}) collective-permute-start(bf16[3,768,48]{1,2,0:T(8,128)(2,1)} %bitcast.3), channel_id=1, source_target_pairs={{0,16},{16,0},{32,48},{48,32},{64,80},{80,64},{96,112},{112,96},{1... | collective-permute-start | bytes 663560 | tf_op jit(solution)/shard_map/ppermute | solution.py:234
  116.4 13.2 %collective-permute-start.6 = (bf16[128,768]{1,0:T(8,128)(2,1)S(1)}, bf16[128,768]{1,0:T(8,128)(2,1)S(1)}, u32[]{:S(2)}, u32[]{:S(2)}) collective-permute-start(bf16[128,768]{1,0:T(8,128)(2,1)S(1)} %collective-permute-done.5.refs_7_), channel_id=1, source_target_pairs={{0,224},{16,240},{32,0},{48,16},{64,32},{80,48},{96,64},{112,80},{... | collective-permute-start | bytes 589832 | tf_op jit(solution)/shard_map/ppermute | solution.py:210
  122.1 14.0 %collective-permute-start.3 = (bf16[128,768]{1,0:T(8,128)(2,1)S(1)}, bf16[128,768]{1,0:T(8,128)(2,1)S(1)}, u32[]{:S(2)}, u32[]{:S(2)}) collective-permute-start(bf16[128,768]{1,0:T(8,128)(2,1)S(1)} %collective-permute-done.2.refs_2_), channel_id=1, source_target_pairs={{0,32},{16,48},{32,64},{48,80},{64,96},{80,112},{96,128},{112,144}... | collective-permute-start | bytes 589832 | tf_op jit(solution)/shard_map/ppermute | solution.py:210
  124.1 2.7 %copy-start.4 = (bf16[1,96,384]{2,1,0:T(8,128)(2,1)}, bf16[1,96,384]{2,1,0:T(8,128)(2,1)S(1)}, u32[]{:S(2)}) copy-start(bf16[1,96,384]{2,1,0:T(8,128)(2,1)S(1)} %get-tuple-element.16) | copy-start | bytes 221188
  124.2 25.1 %collective-permute-start.9 = (f32[512,512]{1,0:T(8,128)S(1)}, f32[512,512]{1,0:T(8,128)S(1)}, u32[]{:S(2)}, u32[]{:S(2)}) collective-permute-start(f32[512,512]{1,0:T(8,128)S(1)} %bitcast.44), channel_id=1, source_target_pairs={{0,1},{1,0},{2,3},{3,2},{4,5},{5,4},{6,7},{7,6},{8,9},{9,8},{10,11... | collective-permute-start | bytes 3145736 | tf_op jit(solution)/shard_map/ppermute | solution.py:254
  126.8 12.5 %collective-permute-start.11 = (bf16[2,96,384]{2,1,0:T(8,128)(2,1)}, bf16[2,96,384]{2,1,0:T(8,128)(2,1)}, u32[]{:S(2)}, u32[]{:S(2)}) collective-permute-start(bf16[2,96,384]{2,1,0:T(8,128)(2,1)} %pad_maximum_fusion.4), channel_id=1, source_target_pairs={{0,4},{2,6},{4,0},{6,2},{8,12},{10,14},{12,8},{14,10},{1,5},{3,7},... | collective-permute-start | bytes 442376 | tf_op jit(solution)/shard_map/ppermute | solution.py:259
  129.6 14.6 %collective-permute-start.7 = (bf16[128,768]{1,0:T(8,128)(2,1)S(1)}, bf16[128,768]{1,0:T(8,128)(2,1)S(1)}, u32[]{:S(2)}, u32[]{:S(2)}) collective-permute-start(bf16[128,768]{1,0:T(8,128)(2,1)S(1)} %collective-permute-done.6.refs_6_), channel_id=1, source_target_pairs={{0,224},{16,240},{32,0},{48,16},{64,32},{80,48},{96,64},{112,80},{... | collective-permute-start | bytes 589832 | tf_op jit(solution)/shard_map/ppermute | solution.py:210
  136.1 13.1 %collective-permute-start.4 = (bf16[128,768]{1,0:T(8,128)(2,1)S(1)}, bf16[128,768]{1,0:T(8,128)(2,1)S(1)}, u32[]{:S(2)}, u32[]{:S(2)}) collective-permute-start(bf16[128,768]{1,0:T(8,128)(2,1)S(1)} %collective-permute-done.3.refs_3_), channel_id=1, source_target_pairs={{0,32},{16,48},{32,64},{48,80},{64,96},{80,112},{96,128},{112,144}... | collective-permute-start | bytes 589832 | tf_op jit(solution)/shard_map/ppermute | solution.py:210
  140.3 0.8 copy-start.1
  141.1 19.2 %collective-permute-start.12 = (bf16[2,2,96,384]{3,2,0,1:T(8,128)(2,1)}, bf16[2,2,96,384]{3,2,0,1:T(8,128)(2,1)}, u32[]{:S(2)}, u32[]{:S(2)}) collective-permute-start(bf16[2,2,96,384]{3,2,0,1:T(8,128)(2,1)} %pad_maximum_fusion.3), channel_id=1, source_target_pairs={{0,2},{2,0},{4,6},{6,4},{8,10},{10,8},{12,14},{14,12},{1,3},{3,1},... | collective-permute-start | bytes 884744 | tf_op jit(solution)/shard_map/ppermute | solution.py:259
  154.3 6.0 %copy-start.2 = (bf16[2,1,96,384]{3,2,0,1:T(8,128)(2,1)S(1)}, bf16[2,1,96,384]{3,2,0,1:T(8,128)(2,1)}, u32[]{:S(2)}) copy-start(bf16[2,1,96,384]{3,2,0,1:T(8,128)(2,1)} %copy-done.1) | copy-start | bytes 442372
  154.3 22.0 %all-to-all-start.2 = ((bf16[16,48,128]{2,1,0:T(8,128)(2,1)}), bf16[16,48,128]{2,1,0:T(8,128)(2,1)S(1)}, u32[]{:S(2)}, u32[]{:S(2)}) async-start(bf16[16,48,128]{2,1,0:T(8,128)(2,1)} %attend.1), calls=%async_computation.2 | async-start | bytes 393216 | tf_op jit(solution)/shard_map/all_to_all | solution.py:25
  161.5 4.0 %collective-permute-start.13 = (bf16[2,2,2,96,384]{4,3,0,1,2:T(8,128)(2,1)S(1)}, bf16[2,2,2,96,384]{4,3,0,1,2:T(8,128)(2,1)S(1)}, u32[]{:S(2)}, u32[]{:S(2)}) collective-permute-start(bf16[2,2,2,96,384]{4,3,0,1,2:T(8,128)(2,1)S(1)} %pad_maximum_fusion), channel_id=1, source_target_pairs={{0,1},{1,0},{2,3},{3,2},{4,5},{5,4},{6,7},{7,6},{8,9},{9,8},{10,11... | collective-permute-start | bytes 1769480 | tf_op jit(solution)/shard_map/ppermute | solution.py:265
  176.2 0.7 copy-start.3
